TPU v7x, 256 devices: a whole 4x4x8 slice. The times are simulated.
256 devices in a mesh: dp: 2 (over y_lo), seq: 32 (over z, y_hi, core), chan: 4 (over x).
Axes of the slice: x: 4, y: 4 (y_hi: 2, y_lo: 2; y = y_hi * 2 + y_lo), z: 8, core: 2. Of those that a mesh axis runs over, the one named last changes fastest.
Arguments:
- layer_input: bfloat16 [2, 4096, 2560], P('dp', ('seq', 'chan')), may hold values from -24 to 24
- inner_weight: bfloat16 [2560, 2560], P(None, 'chan'), may hold values from -0.125 to 0.125
- mixer_weight: bfloat16 [2560, 256], replicated, may hold values from -0.01171875 to 0.01171875
- step_weight: bfloat16 [2560, 40], P(None, 'chan'), may hold values from -0.125 to 0.125
- conv_inner: float32 [4, 2560], P(None, 'chan'), may hold values from -3 to 3
- conv_mixer: float32 [4, 256], replicated, may hold values from -3 to 3
- step_bias: float32 [40], P('chan'), may hold values from -2 to 1
- decay_log: float32 [40], P('chan'), as said below
- skip_gain: float32 [40], P('chan'), may hold values from 0.5 to 1.5
- output_grad: bfloat16 [2, 4096, 2560], P('dp', 'seq', 'chan'), may hold values from -6 to 6
Outputs:
- input_grad: bfloat16 [2, 4096, 2560], P('dp', ('seq', 'chan'))
- inner_weight_grad: float32 [2560, 2560], P(('dp', 'seq'), 'chan')
- mixer_weight_grad: float32 [2560, 256], P(('dp', 'seq', 'chan'))
- step_weight_grad: float32 [2560, 40], P(('dp', 'seq'), 'chan')
Inputs may be any that keep to these rules, and one draw needn't show every extreme that they name: exp(decay_log) is at least 0.2 / 4096.
All inputs are finite; a program needn't handle non-finite values.
Results may differ from a plain program's by a relative error of at most 0.014.
Values may be sent and summed in bfloat16 or wider, within the bound.
A program may use at most 128 MiB of HBM per device.

v0:
```python
import math

import jax
import jax.numpy as jnp
from jax import lax
from jax.sharding import Mesh
from jax.sharding import PartitionSpec as P

HDIM = 64
SEQ = ("seq_0", "seq_1", "seq_2")
DP_SEQ = ("dp", "seq_0", "seq_1", "seq_2")
SEQ_CHAN = ("seq_0", "seq_1", "seq_2", "chan")
DP_SEQ_CHAN = ("dp", "seq_0", "seq_1", "seq_2", "chan")


block_tokens = 256


def in_order(parts, dim):
    dims = list(parts.shape[1:])
    dims[dim] *= parts.shape[0]
    return jnp.moveaxis(parts, 0, dim).reshape(dims)


def from_everyone(value, axis):
    copies = jnp.broadcast_to(value, (lax.axis_size(axis), *value.shape))
    return lax.all_to_all(copies, axis, split_axis=0, concat_axis=0, tiled=True)


def collect(value, axis, dim):
    return in_order(from_everyone(value, axis), dim)


def from_behind(value, axis, steps):
    count = lax.axis_size(axis)
    first, last = (max(0, -steps), min(count, count - steps))
    return lax.ppermute(value, axis, [(source, source + steps) for source in range(first, last)])


def neutral_like(value, identity):
    return jax.tree.map(
        lambda part, zero: jnp.zeros_like(part) + jnp.asarray(zero, part.dtype), value, identity
    )


def entering(value, axes, combine, identity):
    before = start = neutral_like(value, identity)
    total = value
    for axis in reversed(axes):
        size, index = (lax.axis_size(axis), lax.axis_index(axis))
        pieces = jax.tree.map(
            lambda part, kind: lax.all_gather(part.astype(kind), axis),
            total,
            (jnp.bfloat16, jnp.bfloat16),
        )
        inside, total = (start, start)
        for k in range(size):
            passed = k < index
            total = combine(
                total, jax.tree.map(lambda part, own: part[k].astype(own.dtype), pieces, value)
            )
            inside = jax.tree.map(lambda new, old: jnp.where(passed, new, old), total, inside)
        before = combine(inside, before)
    return before


def entering_2(value, axes, combine, identity):
    before = start = neutral_like(value, identity)
    total = value
    for axis in reversed(axes):
        size, index = (lax.axis_size(axis), lax.axis_index(axis))
        pieces = jax.tree.map(lambda part: lax.all_gather(part, axis), total)
        inside, total = (start, start)
        for k in reversed(range(size)):
            passed = k > index
            total = combine(total, jax.tree.map(lambda part: part[k], pieces))
            inside = jax.tree.map(lambda new, old: jnp.where(passed, new, old), total, inside)
        before = combine(inside, before)
    return before


def cut_along(value, dim, size):
    before, after = (value.shape[:dim], value.shape[dim + 1 :])
    return jnp.moveaxis(value.reshape(*before, size, -1, *after), dim, 0)


def sent_and_summed(value, axis, dim):
    parts = cut_along(value, dim, lax.axis_size(axis))
    arrived = lax.all_to_all(parts, axis, split_axis=0, concat_axis=0, tiled=True)
    return arrived.astype(jnp.float32).sum(axis=0)


def over_copies(value, axis):
    return from_everyone(value, axis).astype(jnp.float32).sum(axis=0)


def side_by_side(arrays, axis, dim, along):
    widths = [a.shape[along] for a in arrays]
    both = jnp.concatenate(arrays, axis=along)
    result = sent_and_summed(both, axis, dim)
    return tuple(jnp.split(result, [sum(widths[:k]) for k in range(1, len(widths))], axis=along))


def conv_silu(inputs, history, kernel):
    length = inputs.shape[0]
    padded = jnp.concatenate([history, inputs], axis=0)
    summed = kernel[0][None, :] * padded[0:length]
    for offset in range(1, kernel.shape[0]):
        summed = summed + kernel[offset][None, :] * padded[offset : offset + length]
    return jax.nn.silu(summed)


def activations(
    inner_proj,
    mixer_proj,
    step_raw,
    inner_hist,
    mixer_hist,
    conv_inner,
    conv_mixer,
    step_bias,
    decay_log,
):
    length = inner_proj.shape[0]
    head_count = step_bias.shape[0]
    state_width = mixer_proj.shape[1] // 2
    inner_act = conv_silu(inner_proj, inner_hist, conv_inner).reshape(length, head_count, -1)
    mixer_act = conv_silu(mixer_proj, mixer_hist, conv_mixer)
    step_size = jax.nn.softplus(step_raw + step_bias[None, :])
    log_decay = -step_size * jnp.exp(decay_log)[None, :]
    return (inner_act, mixer_act[:, :state_width], mixer_act[:, state_width:], step_size, log_decay)


def spanned_scan(inner_act, input_mix, output_mix, step_size, log_decay, skip_gain, initial):
    length, head_count, head_dim = inner_act.shape
    block_len = min(block_tokens, length)
    blocks = length // block_len
    highest = lax.Precision.HIGHEST

    def to_blocks(values):
        return values.reshape((blocks, block_len) + values.shape[1:])

    def advance(carry_state, pieces):
        part_inner, part_input, part_output, part_step, part_decay = pieces
        cumulative = jnp.cumsum(part_decay, axis=0)
        scores = jnp.dot(part_output, part_input.T, precision=highest)
        causal = (jnp.arange(block_len)[:, None] >= jnp.arange(block_len)[None, :])[:, :, None]
        spread = cumulative[:, None, :] - cumulative[None, :, :]
        weights = jnp.where(causal, jnp.exp(jnp.where(causal, spread, 0.0)), 0.0)
        weights = weights * scores[:, :, None] * part_step[None, :, :]
        within = jnp.einsum("ijh,jhp->ihp", weights, part_inner, precision=highest)
        carried = jnp.exp(cumulative)[:, :, None] * jnp.einsum(
            "in,hpn->ihp", part_output, carry_state, precision=highest
        )
        result = within + carried + skip_gain[None, :, None] * part_inner
        tail_weight = jnp.exp(cumulative[-1][None, :] - cumulative) * part_step
        update_term = jnp.einsum(
            "jh,jhp,jn->hpn", tail_weight, part_inner, part_input, precision=highest
        )
        carry_state = jnp.exp(cumulative[-1])[:, None, None] * carry_state + update_term
        return (carry_state, result)

    final, results = lax.scan(
        advance,
        initial,
        (
            to_blocks(inner_act),
            to_blocks(input_mix),
            to_blocks(output_mix),
            to_blocks(step_size),
            to_blocks(log_decay),
        ),
    )
    return (results.reshape(length, head_count, head_dim), final)


def combine_carry(earlier, latter):
    return (earlier[0] + latter[0], jnp.exp(latter[0])[:, None, None] * earlier[1] + latter[1])


def contract_rows(left_rows, right_rows):
    return lax.dot_general(
        left_rows, right_rows, (((0,), (0,)), ((), ())), preferred_element_type=jnp.float32
    )


def project_back(gradient, weight):
    return lax.dot_general(
        gradient, weight, (((1,), (1,)), ((), ())), preferred_element_type=jnp.float32
    )


def split_pair(values):
    leading = values.astype(jnp.bfloat16)
    residue = (values - leading.astype(jnp.float32)).astype(jnp.bfloat16)
    return (leading, residue)


def body(
    layer_input,
    inner_weight,
    mixer_weight,
    step_weight,
    conv_inner,
    conv_mixer,
    step_bias,
    decay_log,
    skip_gain,
    output_grad,
):
    gathered = collect(layer_input[0], "chan", 0)
    seg_len = gathered.shape[0]
    chan_count = lax.axis_size("chan")
    history_len = conv_inner.shape[0] - 1
    highest = lax.Precision.HIGHEST
    inner_proj = jnp.dot(gathered, inner_weight, preferred_element_type=jnp.float32).astype(
        jnp.bfloat16
    )
    mixer_proj = jnp.dot(gathered, mixer_weight, preferred_element_type=jnp.float32).astype(
        jnp.bfloat16
    )
    step_raw = jnp.dot(gathered, step_weight, preferred_element_type=jnp.float32)
    last_rows = from_behind(gathered[seg_len - history_len :], SEQ, 1)
    inner_hist = jnp.dot(last_rows, inner_weight, preferred_element_type=jnp.float32).astype(
        jnp.bfloat16
    )
    mixer_hist = jnp.dot(last_rows, mixer_weight, preferred_element_type=jnp.float32).astype(
        jnp.bfloat16
    )
    inner_wide = lax.optimization_barrier(inner_proj).astype(jnp.float32)
    mixer_wide = lax.optimization_barrier(mixer_proj).astype(jnp.float32)
    inner_prev = lax.optimization_barrier(inner_hist).astype(jnp.float32)
    mixer_prev = lax.optimization_barrier(mixer_hist).astype(jnp.float32)

    def local_acts(inner_in, mixer_in, step_in, inner_before, mixer_before):
        return activations(
            inner_in,
            mixer_in,
            step_in,
            inner_before,
            mixer_before,
            conv_inner,
            conv_mixer,
            step_bias,
            decay_log,
        )

    acts, pull_acts = jax.vjp(local_acts, inner_wide, mixer_wide, step_raw, inner_prev, mixer_prev)
    inner_act, input_mix, output_mix, step_size, log_decay = acts
    head_count = step_bias.shape[0]
    upstream = output_grad[0].astype(jnp.float32).reshape(seg_len, head_count, HDIM)
    cumulative = jnp.cumsum(log_decay, axis=0)
    segment_decay = cumulative[-1]
    local_state = jnp.einsum(
        "th,thp,tn->hpn",
        jnp.exp(segment_decay[None, :] - cumulative) * step_size,
        inner_act,
        input_mix,
        precision=highest,
    )
    local_grad = jnp.einsum(
        "th,thp,tn->hpn", jnp.exp(cumulative), upstream, output_mix, precision=highest
    )
    neutral = (jnp.zeros_like(segment_decay), jnp.zeros_like(local_state))
    start_state = entering((segment_decay, local_state), SEQ, combine_carry, neutral)[1]
    end_grad = entering_2((segment_decay, local_grad), SEQ, combine_carry, neutral)[1]

    def scan_local(inner_in, input_in, output_in, step_in, decay_in):
        return spanned_scan(
            inner_in, input_in, output_in, step_in, decay_in, skip_gain, start_state
        )

    unused, pull_scan = jax.vjp(scan_local, inner_act, input_mix, output_mix, step_size, log_decay)
    act_grads = pull_scan((upstream, end_grad))
    inner_local, mixer_local, step_local, inner_back, mixer_back = pull_acts(act_grads)
    inner_next, mixer_next = from_behind((inner_back, mixer_back), SEQ, -1)
    keep_rows = seg_len - history_len
    inner_total = jnp.concatenate(
        [inner_local[:keep_rows], inner_local[keep_rows:] + inner_next], axis=0
    )
    grad_mixer = jnp.concatenate(
        [mixer_local[:keep_rows], mixer_local[keep_rows:] + mixer_next], axis=0
    )
    grad_inner = inner_total.astype(jnp.bfloat16)
    grad_step = step_local.astype(jnp.bfloat16)
    mixer_lead, mixer_rest = split_pair(grad_mixer)
    summed = project_back(grad_inner, inner_weight) + project_back(grad_step, step_weight)
    input_grad = sent_and_summed(
        (
            summed + project_back(mixer_lead, mixer_weight) + project_back(mixer_rest, mixer_weight)
        ).astype(jnp.bfloat16),
        "chan",
        0,
    ).astype(jnp.bfloat16)
    token_count = seg_len * lax.axis_size(SEQ) * lax.axis_size("dp")
    norm_factor = 1.0 / math.sqrt(token_count)
    inner_term = contract_rows(gathered, grad_inner) * norm_factor
    step_term = contract_rows(gathered, grad_step) * norm_factor
    mixer_total = over_copies(grad_mixer.astype(jnp.bfloat16), "chan").astype(jnp.float32)
    group_count = lax.axis_size("dp") * lax.axis_size(SEQ)
    row_share = gathered.shape[1] // (group_count * chan_count)
    grouped = gathered.reshape(seg_len, group_count, chan_count, row_share)
    picked = lax.dynamic_index_in_dim(grouped, lax.axis_index("chan"), 2, keepdims=False).reshape(
        seg_len, group_count * row_share
    )
    total_lead, total_rest = split_pair(mixer_total)
    mixer_term = (
        contract_rows(picked, total_lead) + contract_rows(picked, total_rest)
    ) * norm_factor
    inner_weight_grad, step_weight_grad, mixer_weight_grad = (
        *side_by_side(
            (inner_term.astype(jnp.bfloat16), step_term.astype(jnp.bfloat16)), DP_SEQ, 0, 1
        ),
        sent_and_summed(mixer_term.astype(jnp.bfloat16), DP_SEQ, 0),
    )
    return (input_grad[None], inner_weight_grad, mixer_weight_grad, step_weight_grad)


def solution(mesh):
    split = Mesh(
        mesh.devices.reshape(mesh.shape["dp"], 8, 2, 2, mesh.shape["chan"]),
        ("dp", "seq_0", "seq_1", "seq_2", "chan"),
    )
    placed = (
        P("dp", SEQ_CHAN, None),
        P(None, "chan"),
        P(),
        P(None, "chan"),
        P(None, "chan"),
        P(),
        P("chan"),
        P("chan"),
        P("chan"),
        P("dp", SEQ, "chan"),
    )
    return jax.shard_map(
        body,
        mesh=split,
        in_specs=placed,
        out_specs=(
            P("dp", SEQ_CHAN, None),
            P(DP_SEQ, "chan"),
            P(DP_SEQ_CHAN, None),
            P(DP_SEQ, "chan"),
        ),
        check_vma=False,
    )
```

profile of v0, /device:TPU:1, one launch (start us, length us, event | category | flops | bytes accessed | tf_op | source)
XLA Modules:
  0.0 373.8 jit_solution(11411503904716051082)
XLA Ops:
  9.2 4.8 %all-to-all-start = ((bf16[4,32,2560]{2,1,0:T(8,128)(2,1)}), bf16[4,32,2560]{2,1,0:T(8,128)(2,1)}, u32[]{:S(2)}, u32[]{:S(2)}) async-start(bf16[4,32,2560]{2,1,0:T(8,128)(2,1)} %broadcast_in_dim.167), calls=%async_computation | async-start | bytes 1310720 | tf_op jit(solution)/shard_map/all_to_all | solution.py:27
  17.8 4.5 %all-to-all-done = bf16[4,32,2560]{2,1,0:T(8,128)(2,1)} async-done(((bf16[4,32,2560]{2,1,0:T(8,128)(2,1)}), bf16[4,32,2560]{2,1,0:T(8,128)(2,1)}, u32[]{:S(2)}, u32[]{:S(2)}) %all-to-all-start) | async-done | bytes 655392 | tf_op jit(solution)/shard_map/all_to_all | solution.py:27
  23.0 8.6 %collective-permute-start = (bf16[3,2560]{1,0:T(4,128)(2,1)S(1)}, bf16[3,2560]{1,0:T(4,128)(2,1)S(1)}, u32[]{:S(2)}, u32[]{:S(2)}) collective-permute-start(bf16[3,2560]{1,0:T(4,128)(2,1)S(1)} %slice.320), channel_id=1, source_target_pairs={{0,4},{4,8},{8,12},{12,16},{16,20},{20,24},{24,28},{28,32},{32,36}... | collective-permute-start | bytes 46088 | tf_op jit(solution)/shard_map/ppermute | solution.py:37
  36.0 4.6 %all-gather.3 = f32[2,1,10]{2,1,0:T(1,128)S(1)} all-gather(f32[1,1,10]{2,1,0:T(1,128)S(1)} %get-tuple-element.429), channel_id=1, replica_groups=mesh['dp'=2,'seq_0'=8,'seq_1'=2,'seq_2'=2,'chan'=4] {'seq_1'}, dimensions={0}, use_global_device_ids=true | all-gather | bytes 120 | tf_op jit(solution)/shard_map/all_gather | solution.py:72
  45.5 3.2 all-gather
  49.7 11.1 %all_gather.56 = f32[2,10,64,128]{3,2,1,0:T(8,128)S(1)} all-gather(f32[1,10,64,128]{3,2,1,0:T(8,128)S(1)} %bitcast_add_fusion.10), channel_id=1, replica_groups=mesh['dp'=2,'seq_0'=8,'seq_1'=2,'seq_2'=2,'chan'=4] {'seq_1'}, dimensions={0}, use_global_device_ids=true | all-gather | bytes 983040 | tf_op jit(solution)/shard_map/all_gather | solution.py:72
  68.1 4.5 %all-gather.6 = bf16[2,1,10]{2,1,0:T(2,128)(2,1)} all-gather(bf16[1,1,10]{2,1,0:T(2,128)(2,1)S(1)} %get-tuple-element.424), channel_id=1, replica_groups=mesh['dp'=2,'seq_0'=8,'seq_1'=2,'seq_2'=2,'chan'=4] {'seq_1'}, dimensions={0}, use_global_device_ids=true | all-gather | bytes 60 | tf_op jit(solution)/shard_map/all_gather | solution.py:52
  76.9 4.2 %copy.101 = bf16[4,32,2560]{1,0,2:T(4,128)(2,1)} copy(bf16[4,32,2560]{2,1,0:T(8,128)(2,1)} %all-to-all-done) | data formatting | bytes 1310720 | tf_op jit(solution)/shard_map/all_to_all | solution.py:27
  81.0 4.5 %reshape_reshape.4 = bf16[128,64,4,10]{0,3,2,1:T(8,128)(2,1)} reshape(bf16[4,32,2560]{1,0,2:T(4,128)(2,1)} %copy.101) | data formatting | bytes 1310720 | tf_op jit(solution)/shard_map/reshape;reshape | solution.py:302
  90.1 16.5 %all-gather.7 = bf16[8,1,10]{2,1,0:T(2,128)(2,1)} all-gather(bf16[1,1,10]{2,1,0:T(2,128)(2,1)S(1)} %get-tuple-element.421), channel_id=1, replica_groups=mesh['dp'=2,'seq_0'=8,'seq_1'=2,'seq_2'=2,'chan'=4] {'seq_0'}, dimensions={0}, use_global_device_ids=true | all-gather | bytes 180 | tf_op jit(solution)/shard_map/all_gather | solution.py:52
  107.8 10.2 %all-gather.4 = f32[8,1,10]{2,1,0:T(1,128)S(1)} all-gather(f32[1,1,10]{2,1,0:T(1,128)S(1)} %get-tuple-element.386), channel_id=1, replica_groups=mesh['dp'=2,'seq_0'=8,'seq_1'=2,'seq_2'=2,'chan'=4] {'seq_0'}, dimensions={0}, use_global_device_ids=true | all-gather | bytes 360 | tf_op jit(solution)/shard_map/all_gather | solution.py:72
  123.3 2.9 add_add_fusion
  130.7 3.0 broadcast_multiply_fusion.3
  137.8 9.6 %all-gather.1 = bf16[20,64,128]{2,1,0:T(8,128)(2,1)S(1)} all-gather(bf16[10,64,128]{2,1,0:T(8,128)(2,1)S(1)} %convolution_convert_fusion), channel_id=3, replica_groups=mesh['dp'=2,'seq_0'=8,'seq_1'=2,'seq_2'=2,'chan'=4] {'seq_2'}, dimensions={0}, use_global_device_ids=true | all-gather | bytes 491520 | tf_op jit(solution)/shard_map/all_gather | solution.py:52
  149.0 7.5 %all_gather.63 = bf16[2,10,64,128]{3,2,1,0:T(8,128)(2,1)S(1)} all-gather(bf16[1,10,64,128]{3,2,1,0:T(8,128)(2,1)S(1)} %fusion.108), channel_id=1, replica_groups=mesh['dp'=2,'seq_0'=8,'seq_1'=2,'seq_2'=2,'chan'=4] {'seq_1'}, dimensions={0}, use_global_device_ids=true | all-gather | bytes 491520 | tf_op jit(solution)/shard_map/all_gather | solution.py:52
  163.3 3.3 collective-permute-start.1
  175.3 3.8 %fusion = bf16[2560,640]{0,1:T(8,128)(2,1)} fusion(bf16[128,2560]{1,0:T(8,128)(2,1)} %bitcast.2, bf16[3,640]{1,0:T(4,128)(2,1)S(1)} %fusion.180, bf16[125,640]{1,0:T(8,128)(2,1)S(1)} %slice.667), kind=kOutput, calls=%fused_computation.2 | convolution fusion | flops 423034880 | bytes 4096000 | tf_op jit(solution)/shard_map/dot_general | solution.py:182
  179.1 10.5 %all-gather.13.cloned.1.call-done = bf16[8,10,64,128]{3,2,1,0:T(8,128)(2,1)} async-done(((bf16[1,10,64,128]{3,2,1,0:T(8,128)(2,1)}), bf16[8,10,64,128]{3,2,1,0:T(8,128)(2,1)}) %all-gather.13.cloned.1.call-update) | async-done | bytes 1310736 | tf_op jit(solution)/shard_map/all_gather | solution.py:52
  189.9 3.2 convolution_bitcast_fusion.3
  194.3 3.5 fusion.86
  203.4 7.7 %collective-permute-start.2 = (f32[3,256]{1,0:T(4,128)S(1)}, f32[3,256]{1,0:T(4,128)S(1)}, u32[]{:S(2)}, u32[]{:S(2)}) collective-permute-start(f32[3,256]{1,0:T(4,128)S(1)} %pad_add_fusion.3), channel_id=1, source_target_pairs={{4,0},{8,4},{12,8},{16,12},{20,16},{24,20},{28,24},{32,28},{36,32}... | collective-permute-start | bytes 9224 | tf_op jit(solution)/shard_map/ppermute | solution.py:37
  213.1 3.2 convolution_add_fusion.2
  217.7 4.0 %all-to-all-start.3 = ((bf16[4,128,256]{2,1,0:T(8,128)(2,1)}), bf16[4,128,256]{2,1,0:T(8,128)(2,1)}, u32[]{:S(2)}, u32[]{:S(2)}) async-start(bf16[4,128,256]{2,1,0:T(8,128)(2,1)} %broadcast_in_dim.171), calls=%async_computation.3 | async-start | bytes 524288 | tf_op jit(solution)/shard_map/all_to_all | solution.py:27
  225.6 3.3 all-to-all-done.3
  229.0 4.2 %all-to-all-start.1 = ((bf16[4,32,2560]{2,1,0:T(8,128)(2,1)}), bf16[4,32,2560]{2,1,0:T(8,128)(2,1)}, u32[]{:S(2)}, u32[]{:S(2)}) async-start(bf16[4,32,2560]{2,1,0:T(8,128)(2,1)} %bitcast.370), calls=%async_computation.1 | async-start | bytes 1310720 | tf_op jit(solution)/shard_map/all_to_all | solution.py:89
  237.2 6.5 %all-to-all-done.1 = bf16[4,32,2560]{2,1,0:T(8,128)(2,1)} async-done(((bf16[4,32,2560]{2,1,0:T(8,128)(2,1)}), bf16[4,32,2560]{2,1,0:T(8,128)(2,1)}, u32[]{:S(2)}, u32[]{:S(2)}) %all-to-all-start.1) | async-done | bytes 655392 | tf_op jit(solution)/shard_map/all_to_all | solution.py:89
  243.7 8.4 %all-to-all-start.4 = ((bf16[64,10,256]{2,1,0:T(8,128)(2,1)}), bf16[64,10,256]{2,1,0:T(8,128)(2,1)}, u32[]{:S(2)}, u32[]{:S(2)}) async-start(bf16[64,10,256]{2,1,0:T(8,128)(2,1)} %reshape.626), calls=%async_computation.4 | async-start | bytes 1048576 | tf_op jit(solution)/shard_map/all_to_all | solution.py:89
  253.5 3.9 %pad_maximum_fusion = bf16[2560,650]{0,1:T(8,128)(2,1)} fusion(bf16[2560,10]{0,1:T(8,128)(2,1)S(1)} %fusion.3, bf16[2560,640]{0,1:T(8,128)(2,1)} %fusion), kind=kLoop, calls=%fused_computation.8 | loop fusion | flops 6656000 | bytes 6656000 | tf_op jit(solution)/shard_map/concatenate | solution.py:99
  257.3 5.9 %copy.100 = bf16[2560,650]{1,0:T(8,128)(2,1)} copy(bf16[2560,650]{0,1:T(8,128)(2,1)} %pad_maximum_fusion) | data formatting | bytes 6656000 | tf_op jit(solution)/shard_map/concatenate | solution.py:99
  263.2 5.8 %all-to-all-done.4 = bf16[64,10,256]{2,1,0:T(8,128)(2,1)} async-done(((bf16[64,10,256]{2,1,0:T(8,128)(2,1)}), bf16[64,10,256]{2,1,0:T(8,128)(2,1)}, u32[]{:S(2)}, u32[]{:S(2)}) %all-to-all-start.4) | async-done | bytes 327712 | tf_op jit(solution)/shard_map/all_to_all | solution.py:89
  269.0 6.9 %all-to-all-start.2 = ((bf16[64,40,650]{2,1,0:T(8,128)(2,1)}), bf16[64,40,650]{2,1,0:T(8,128)(2,1)}, u32[]{:S(2)}, u32[]{:S(2)}) async-start(bf16[64,40,650]{2,1,0:T(8,128)(2,1)} %bitcast.365), calls=%async_computation.2 | async-start | bytes 7864320 | tf_op jit(solution)/shard_map/all_to_all | solution.py:89
  279.5 83.4 %all-to-all-done.2 = bf16[64,40,650]{2,1,0:T(8,128)(2,1)} async-done(((bf16[64,40,650]{2,1,0:T(8,128)(2,1)}), bf16[64,40,650]{2,1,0:T(8,128)(2,1)}, u32[]{:S(2)}, u32[]{:S(2)}) %all-to-all-start.2) | async-done | bytes 3328032 | tf_op jit(solution)/shard_map/all_to_all | solution.py:89
  (274 shorter events, 91.4 us)
Async XLA Ops:
  7.2 67.2 %copy-start = (bf16[2560,640]{1,0:T(8,128)(2,1)S(1)}, bf16[2560,640]{1,0:T(8,128)(2,1)}, u32[]{:S(2)}) copy-start(bf16[2560,640]{1,0:T(8,128)(2,1)} %param.11) | copy-start | bytes 9830404
  9.2 13.1 %all-to-all-start = ((bf16[4,32,2560]{2,1,0:T(8,128)(2,1)}), bf16[4,32,2560]{2,1,0:T(8,128)(2,1)}, u32[]{:S(2)}, u32[]{:S(2)}) async-start(bf16[4,32,2560]{2,1,0:T(8,128)(2,1)} %broadcast_in_dim.167), calls=%async_computation | async-start | bytes 1310720 | tf_op jit(solution)/shard_map/all_to_all | solution.py:27
  14.0 109.2 %all-gather.11.cloned.1.call-start = ((), (), s32[]{:S(2)}) async-start(), calls=%async_computation.5 | async-start | bytes 2949120 | tf_op jit(solution)/shard_map/all_gather | solution.py:72
  14.6 18.4 %copy-start.84 = (f32[10]{0:T(128)}, f32[10]{0:T(128)S(1)}, u32[]{:S(2)}) copy-start(f32[10]{0:T(128)S(1)} %exp.409) | copy-start | bytes 124
  23.0 20.2 %collective-permute-start = (bf16[3,2560]{1,0:T(4,128)(2,1)S(1)}, bf16[3,2560]{1,0:T(4,128)(2,1)S(1)}, u32[]{:S(2)}, u32[]{:S(2)}) collective-permute-start(bf16[3,2560]{1,0:T(4,128)(2,1)S(1)} %slice.320), channel_id=1, source_target_pairs={{0,4},{4,8},{8,12},{12,16},{16,20},{20,24},{24,28},{28,32},{32,36}... | collective-permute-start | bytes 46088 | tf_op jit(solution)/shard_map/ppermute | solution.py:37
  33.4 11.5 %copy-start.43 = (f32[1,256]{1,0:T(1,128)S(1)}, f32[1,256]{1,0:T(1,128)}, u32[]{:S(2)}) copy-start(f32[1,256]{1,0:T(1,128)} %get-tuple-element.417) | copy-start | bytes 3076
  33.4 11.5 %copy-start.44 = (f32[1,256]{1,0:T(1,128)S(1)}, f32[1,256]{1,0:T(1,128)}, u32[]{:S(2)}) copy-start(f32[1,256]{1,0:T(1,128)} %get-tuple-element.418) | copy-start | bytes 3076
  33.4 11.5 %copy-start.45 = (f32[1,256]{1,0:T(1,128)S(1)}, f32[1,256]{1,0:T(1,128)}, u32[]{:S(2)}) copy-start(f32[1,256]{1,0:T(1,128)} %get-tuple-element.420) | copy-start | bytes 3076
  33.4 11.5 %copy-start.46 = (f32[1,256]{1,0:T(1,128)S(1)}, f32[1,256]{1,0:T(1,128)}, u32[]{:S(2)}) copy-start(f32[1,256]{1,0:T(1,128)} %get-tuple-element.419) | copy-start | bytes 3076
  33.4 11.6 %copy-start.18 = (bf16[1,128,640]{1,2,0:T(8,128)(2,1)S(1)}, bf16[1,128,640]{1,2,0:T(8,128)(2,1)}, u32[]{:S(2)}) copy-start(bf16[1,128,640]{1,2,0:T(8,128)(2,1)} %copy.88) | copy-start | bytes 491524
  33.6 11.2 %copy-start.41 = (f32[10]{0:T(128)}, f32[10]{0:T(128)S(1)}, u32[]{:S(2)}) copy-start(f32[10]{0:T(128)S(1)} %slice_reduce_fusion) | copy-start | bytes 124
  36.0 8.8 %copy-start.83 = (f32[1,1,10]{2,1,0:T(1,128)}, f32[1,1,10]{2,1,0:T(1,128)S(1)}, u32[]{:S(2)}) copy-start(f32[1,1,10]{2,1,0:T(1,128)S(1)} %get-tuple-element.429) | copy-start | bytes 124
  36.0 12.7 %copy-start.47 = (f32[10]{0:T(128)}, f32[10]{0:T(128)S(1)}, u32[]{:S(2)}) copy-start(f32[10]{0:T(128)S(1)} %get-tuple-element.430) | copy-start | bytes 124
  36.0 12.7 %copy-start.49 = (f32[10]{0:T(128)}, f32[10]{0:T(128)S(1)}, u32[]{:S(2)}) copy-start(f32[10]{0:T(128)S(1)} %get-tuple-element.431) | copy-start | bytes 124
  43.2 17.5 %copy-start.51 = (f32[10]{0:T(128)}, f32[10]{0:T(128)S(1)}, u32[]{:S(2)}) copy-start(f32[10]{0:T(128)S(1)} %get-tuple-element.427) | copy-start | bytes 124
  43.2 17.5 %copy-start.53 = (f32[10]{0:T(128)}, f32[10]{0:T(128)S(1)}, u32[]{:S(2)}) copy-start(f32[10]{0:T(128)S(1)} %get-tuple-element.428) | copy-start | bytes 124
  62.5 127.2 %all-gather.13.cloned.1.call-start = ((), (), s32[]{:S(2)}) async-start(), calls=%async_computation.6 | async-start | bytes 1474560 | tf_op jit(solution)/shard_map/all_gather | solution.py:52
  158.8 7.9 %copy-start.7 = (f32[128,640]{1,0:T(8,128)S(1)}, f32[128,640]{1,0:T(8,128)}, u32[]{:S(2)}) copy-start(f32[128,640]{1,0:T(8,128)} %get-tuple-element.380) | copy-start | bytes 983044
  158.8 8.7 %copy-start.8 = (f32[128,640]{0,1:T(8,128)S(1)}, f32[128,640]{0,1:T(8,128)}, u32[]{:S(2)}) copy-start(f32[128,640]{0,1:T(8,128)} %copy.94) | copy-start | bytes 983044
  158.8 8.7 %copy-start.25 = (f32[128,10,64]{0,2,1:T(8,128)S(1)}, f32[128,10,64]{0,2,1:T(8,128)}, u32[]{:S(2)}) copy-start(f32[128,10,64]{0,2,1:T(8,128)} %copy-done.24) | copy-start | bytes 983044
  158.8 8.7 %copy-start.17 = (f32[1,10,64,128]{3,2,1,0:T(8,128)S(1)}, f32[1,10,64,128]{3,2,1,0:T(8,128)}, u32[]{:S(2)}) copy-start(f32[1,10,64,128]{3,2,1,0:T(8,128)} %copy-done.16) | copy-start | bytes 983044
  158.8 8.7 %copy-start.33 = (f32[128,10]{0,1:T(8,128)S(1)}, f32[128,10]{0,1:T(8,128)}, u32[]{:S(2)}) copy-start(f32[128,10]{0,1:T(8,128)} %get-tuple-element.398) | copy-start | bytes 15364
  162.6 7.4 %copy-start.9 = (f32[128,640]{1,0:T(8,128)}, f32[128,640]{1,0:T(8,128)S(1)}, u32[]{:S(2)}) copy-start(f32[128,640]{1,0:T(8,128)S(1)} %get-tuple-element.392) | copy-start | bytes 983044
  162.6 7.3 %copy-start.10 = (f32[128,640]{1,0:T(8,128)}, f32[128,640]{1,0:T(8,128)S(1)}, u32[]{:S(2)}) copy-start(f32[128,640]{1,0:T(8,128)S(1)} %get-tuple-element.393) | copy-start | bytes 983044
  163.3 10.5 %collective-permute-start.1 = (f32[3,640]{1,0:T(4,128)}, f32[3,640]{1,0:T(4,128)}, u32[]{:S(2)}, u32[]{:S(2)}) collective-permute-start(f32[3,640]{1,0:T(4,128)} %pad_add_fusion.2), channel_id=1, source_target_pairs={{4,0},{8,4},{12,8},{16,12},{20,16},{24,20},{28,24},{32,28},{36,32}... | collective-permute-start | bytes 23048 | tf_op jit(solution)/shard_map/ppermute | solution.py:37
  201.7 11.5 %copy-start.38 = (bf16[3,640]{1,0:T(4,128)(2,1)S(1)}, bf16[3,640]{1,0:T(4,128)(2,1)}, u32[]{:S(2)}) copy-start(bf16[3,640]{1,0:T(4,128)(2,1)} %copy-done.37) | copy-start | bytes 11524
  203.4 13.0 %collective-permute-start.2 = (f32[3,256]{1,0:T(4,128)S(1)}, f32[3,256]{1,0:T(4,128)S(1)}, u32[]{:S(2)}, u32[]{:S(2)}) collective-permute-start(f32[3,256]{1,0:T(4,128)S(1)} %pad_add_fusion.3), channel_id=1, source_target_pairs={{4,0},{8,4},{12,8},{16,12},{20,16},{24,20},{28,24},{32,28},{36,32}... | collective-permute-start | bytes 9224 | tf_op jit(solution)/shard_map/ppermute | solution.py:37
  217.7 11.2 %all-to-all-start.3 = ((bf16[4,128,256]{2,1,0:T(8,128)(2,1)}), bf16[4,128,256]{2,1,0:T(8,128)(2,1)}, u32[]{:S(2)}, u32[]{:S(2)}) async-start(bf16[4,128,256]{2,1,0:T(8,128)(2,1)} %broadcast_in_dim.171), calls=%async_computation.3 | async-start | bytes 524288 | tf_op jit(solution)/shard_map/all_to_all | solution.py:27
  224.2 9.9 %copy-start.23 = (bf16[128,640]{0,1:T(8,128)(2,1)S(1)}, bf16[128,640]{0,1:T(8,128)(2,1)}, u32[]{:S(2)}) copy-start(bf16[128,640]{0,1:T(8,128)(2,1)} %reshape.625) | copy-start | bytes 491524
  229.0 14.7 %all-to-all-start.1 = ((bf16[4,32,2560]{2,1,0:T(8,128)(2,1)}), bf16[4,32,2560]{2,1,0:T(8,128)(2,1)}, u32[]{:S(2)}, u32[]{:S(2)}) async-start(bf16[4,32,2560]{2,1,0:T(8,128)(2,1)} %bitcast.370), calls=%async_computation.1 | async-start | bytes 1310720 | tf_op jit(solution)/shard_map/all_to_all | solution.py:89
  243.7 25.3 %all-to-all-start.4 = ((bf16[64,10,256]{2,1,0:T(8,128)(2,1)}), bf16[64,10,256]{2,1,0:T(8,128)(2,1)}, u32[]{:S(2)}, u32[]{:S(2)}) async-start(bf16[64,10,256]{2,1,0:T(8,128)(2,1)} %reshape.626), calls=%async_computation.4 | async-start | bytes 1048576 | tf_op jit(solution)/shard_map/all_to_all | solution.py:89
  269.0 93.9 %all-to-all-start.2 = ((bf16[64,40,650]{2,1,0:T(8,128)(2,1)}), bf16[64,40,650]{2,1,0:T(8,128)(2,1)}, u32[]{:S(2)}, u32[]{:S(2)}) async-start(bf16[64,40,650]{2,1,0:T(8,128)(2,1)} %bitcast.365), calls=%async_computation.2 | async-start | bytes 7864320 | tf_op jit(solution)/shard_map/all_to_all | solution.py:89
  (65 other events, 245.3 us)
Sparse Core Ops, SparseCore 0:
  62.6 38.9 all-gather.10
  158.9 30.6 all-gather.12
where the time goes:
time: 377 us; the launch traced here: 374 us
  waiting for transfers between devices  114 us (30%)
  blocking collectives  71.8 us (19%)
  starting transfers between devices  48 us (13%)
  local copies, waits for them, and re-layouts  45.2 us (12%)
  other arithmetic  44.3 us (12%)
  matrix products  35.2 us (9%)
  between operations  15.4 us (4%)
    all_to_all x3, waiting for transfers between devices, sent_and_summed(): lax.all_to_all(parts, axis, split_axis=0, concat_axis=0, tiled=True)  95.6 us
    all_gather x5, blocking collectives, entering(): lax.all_gather(part.astype(kind), axis)  40.9 us
    all_gather x5, blocking collectives, entering_2(): pieces = jax.tree.map(lambda part: lax.all_gather(part, axis), total)  30.9 us
    ppermute x3, starting transfers between devices, from_behind(): lax.ppermute(value, axis, [(source, source + steps) for source in range(f...  19.6 us
    all_to_all x3, starting transfers between devices, sent_and_summed(): lax.all_to_all(parts, axis, split_axis=0, concat_axis=0, tiled=True)  19.5 us
    all_gather x1, waiting for transfers between devices, entering(): lax.all_gather(part.astype(kind), axis)  10.5 us
    all_to_all x2, starting transfers between devices, from_everyone(): return lax.all_to_all(copies, axis, split_axis=0, concat_axis=0, tiled=True)  8.87 us
    unnamed x176, local copies, waits for them, and re-layouts  8.45 us
  transfers between devices with their start and end apart: 10, of which 6 were waited for; matrix products, arithmetic and copies ran while one was open for 21% of the time, Pallas kernels for 0%

commit v1 on v0

v1 whole, which is shorter than its diff:
```python
import functools
import math

import jax
import jax.numpy as jnp
from jax import lax
from jax.experimental import pallas as pl
from jax.experimental.pallas import tpu as pltpu
from jax.sharding import Mesh
from jax.sharding import PartitionSpec as P

D = 2560
HDIM = 64
HEADS = 5
INNER = HEADS * HDIM
STATE = 128
TOK = 256
PRE = 16
EXT = TOK + PRE
NZ = 8
ROWS = 80
CHUNK = 48
F32 = jnp.float32
BF16 = jnp.bfloat16
SEQ = ("seq_0", "seq_1", "seq_2")
DP_SEQ = ("dp", "seq_0", "seq_1", "seq_2")
SEQ_CHAN = ("seq_0", "seq_1", "seq_2", "chan")
DP_SEQ_CHAN = ("dp", "seq_0", "seq_1", "seq_2", "chan")
MESH = pl.DeviceIdType.MESH
VM = pl.BlockSpec(memory_space=pltpu.VMEM)
LIMIT = 60 * 1024 * 1024


def roll(v, shift):
    return pltpu.roll(v, shift % v.shape[0], 0)


def mm(a, b):
    return jnp.dot(a, b, preferred_element_type=F32)


def mm_t(a, b):
    return lax.dot_general(a, b, (((1,), (1,)), ((), ())), preferred_element_type=F32)


def t_mm(a, b):
    return lax.dot_general(a, b, (((0,), (0,)), ((), ())), preferred_element_type=F32)


def exact(a, b):
    return jnp.dot(a, b, preferred_element_type=F32, precision=lax.Precision.HIGHEST)


def iota(shape, dim):
    return lax.broadcasted_iota(jnp.int32, shape, dim)


def one_hot(cond):
    return jnp.where(cond, 1.0, 0.0).astype(F32)


def head_expand():
    return one_hot(iota((128, INNER), 1) // HDIM == iota((128, INNER), 0))


def head_sum():
    return one_hot(iota((INNER, 128), 0) // HDIM == iota((INNER, 128), 1))


def head_pick(core):
    return one_hot(
        (iota((10, 128), 0) == iota((10, 128), 1) + HEADS * core) & (iota((10, 128), 1) < HEADS)
    )


def half_of(v, core):
    return jnp.where(core == 0, v[:, :INNER], v[:, INNER:])


def conv(v, k):
    return k[3:4] * v + k[2:3] * roll(v, 1) + k[1:2] * roll(v, 2) + k[0:1] * roll(v, 3)


def conv_back(g, k):
    return k[3:4] * g + k[2:3] * roll(g, -1) + k[1:2] * roll(g, -2) + k[0:1] * roll(g, -3)


def gather_kernel(piece, og, xe, ogx, local_sem, ssem, rsem, tsem):
    z, yh, c, x = (lax.axis_index(a) for a in SEQ_CHAN)
    right, left = lax.rem(x + 1, 4), lax.rem(x + 3, 4)
    sib = 1 - c
    q = z * 2 + yh
    nq, pq = lax.rem(q + 1, 2 * NZ), lax.rem(q + 2 * NZ - 1, 2 * NZ)
    barrier = pltpu.get_barrier_semaphore()

    def tell(**where):
        pl.semaphore_signal(barrier, inc=1, device_id=where, device_id_type=MESH)

    tell(chan=right)
    tell(chan=left)
    tell(seq_2=sib)

    @pl.when(c == 1)
    def _():
        tell(seq_0=pq // 2, seq_1=lax.rem(pq, 2), chan=3)

    pl.semaphore_wait(barrier, jnp.where((c == 1) & (x == 3), 7, 3))

    def slot(core, chan, half=None):
        base = PRE + (core * 4 + chan) * 32
        if half is None:
            return xe.at[pl.ds(pl.multiple_of(base, 16), 32), :]
        return xe.at[pl.ds(pl.multiple_of(base + 16 * half, 16), 16), :]

    def copy(src, dst, k, **where):
        return pltpu.make_async_remote_copy(
            src_ref=src, dst_ref=dst, send_sem=ssem.at[k], recv_sem=rsem.at[k],
            device_id=where, device_id_type=MESH,
        )

    def half(h):
        return piece.at[pl.ds(16 * h, 16), :]

    own = pltpu.make_async_copy(piece, slot(c, x), local_sem.at[0])
    own_og = pltpu.make_async_copy(og, ogx.at[c], local_sem.at[1])
    r0 = copy(half(0), slot(c, x, 0), 0, chan=right)
    l1 = copy(half(1), slot(c, x, 1), 1, chan=left)
    r1 = copy(half(1), slot(c, x, 1), 2, chan=right)
    l0 = copy(half(0), slot(c, x, 0), 3, chan=left)
    sp = copy(piece, slot(c, x), 4, seq_2=sib)
    so = copy(og, ogx.at[c], 5, seq_2=sib)
    for d in (r0, l1):
        d.start()

    def tails(chan):
        return pltpu.make_async_remote_copy(
            src_ref=half(1), dst_ref=xe.at[pl.ds(0, 16), :], send_sem=tsem.at[chan],
            recv_sem=rsem.at[6],
            device_id={"seq_0": nq // 2, "seq_1": lax.rem(nq, 2), "chan": chan},
            device_id_type=MESH,
        )

    @pl.when((c == 1) & (x == 3))
    def _():
        for chan in range(4):
            tails(chan).start()

    for d in (r1, l0, sp, so):
        d.start()
    own.start()
    own_og.start()
    far = lax.rem(x + 2, 4)
    in_r0 = copy(half(0), slot(c, left, 0), 0, chan=right)
    in_r1 = copy(half(1), slot(c, left, 1), 2, chan=right)
    in_l1 = copy(half(1), slot(c, right, 1), 1, chan=left)
    in_l0 = copy(half(0), slot(c, right, 0), 3, chan=left)
    rr = copy(slot(c, left, 0), slot(c, left, 0), 7, chan=right)
    ll = copy(slot(c, right, 1), slot(c, right, 1), 8, chan=left)
    in_r0.wait_recv()
    rr.start()
    in_l1.wait_recv()
    ll.start()
    in_r1.wait_recv()
    s_left = copy(slot(c, left), slot(c, left), 9, seq_2=sib)
    s_left.start()
    in_l0.wait_recv()
    s_right = copy(slot(c, right), slot(c, right), 10, seq_2=sib)
    s_right.start()
    tail_on = copy(xe.at[pl.ds(0, 16), :], xe.at[pl.ds(0, 16), :], 12, seq_2=sib)

    @pl.when(c == 1)
    def _():
        tails(0).wait_recv()
        tail_on.start()

    in_rr = copy(half(0), slot(c, far, 0), 7, chan=right)
    in_ll = copy(half(1), slot(c, far, 1), 8, chan=left)
    in_rr.wait_recv()
    in_ll.wait_recv()
    s_far = copy(slot(c, far), slot(c, far), 11, seq_2=sib)
    s_far.start()
    copy(piece, slot(sib, x), 4, seq_2=sib).wait_recv()
    copy(og, ogx.at[sib], 5, seq_2=sib).wait_recv()
    copy(piece, slot(sib, left), 9, seq_2=sib).wait_recv()
    copy(piece, slot(sib, right), 10, seq_2=sib).wait_recv()
    copy(piece, slot(sib, far), 11, seq_2=sib).wait_recv()

    @pl.when(c == 0)
    def _():
        tail_on.wait_recv()

    for d in (r0, l1, r1, l0, sp, so, rr, ll, s_left, s_right, s_far):
        d.wait_send()

    @pl.when(c == 1)
    def _():
        tail_on.wait_send()

    @pl.when((c == 1) & (x == 3))
    def _():
        for chan in range(4):
            tails(chan).wait_send()

    own.wait()
    own_og.wait()


def gather(piece, og):
    return pl.pallas_call(
        gather_kernel,
        out_shape=(
            jax.ShapeDtypeStruct((EXT, D), BF16),
            jax.ShapeDtypeStruct((2, TOK // 2, 2 * INNER), BF16),
        ),
        in_specs=[VM, VM],
        out_specs=(VM, VM),
        scratch_shapes=[
            pltpu.SemaphoreType.DMA((2,)),
            pltpu.SemaphoreType.DMA((13,)),
            pltpu.SemaphoreType.DMA((13,)),
            pltpu.SemaphoreType.DMA((4,)),
        ],
        compiler_params=pltpu.CompilerParams(collective_id=0, has_side_effects=True),
        name="gather",
    )(piece, og)


def forward_kernel(
    xe, ogx, wi, wm, ws, ci, cm, bias, dlog,
    xa_o, zi_o, zm_o, dt_o, cum_o, sr_o, og_o, wih_o, send_o,
):
    z, yh, c = (lax.axis_index(a) for a in SEQ)
    flag = jnp.where(z * 2 + yh == 0, 0.0, 1.0).astype(F32)
    pick = head_pick(c)
    wih = half_of(wi[...], c)
    wih_o[...] = wih
    xv = xe[...]
    keep = jnp.where(iota((EXT, 1), 0) < PRE, flag, 1.0)

    def masked(v):
        return jnp.where(keep > 0.0, v.astype(BF16).astype(F32), 0.0)

    pi = masked(mm(xv, wih))
    pm = masked(mm(xv, wm[...]))
    sr = exact(mm(xv, ws[...])[PRE:], pick)
    zi = conv(pi, half_of(ci[...], c))[PRE:]
    zm = conv(pm, cm[...])[PRE:]
    xa = zi * jax.nn.sigmoid(zi)
    ma = zm * jax.nn.sigmoid(zm)
    srb = sr + exact(bias[...], pick)
    dt = jnp.maximum(srb, 0.0) + jnp.log1p(jnp.exp(-jnp.abs(srb)))
    rate = exact(jnp.exp(dlog[...]), pick)
    a = -dt * rate
    tri = one_hot(iota((TOK, TOK), 0) >= iota((TOK, TOK), 1))
    cum = exact(tri, a)
    tot = cum[TOK - 1 : TOK]
    og = half_of(ogx[...].reshape(TOK, 2 * INNER), c)
    ex = head_expand()
    xt = (xa * exact(dt * jnp.exp(tot - cum), ex)).astype(BF16)
    yt = (og.astype(F32) * exact(jnp.exp(cum), ex)).astype(BF16)
    f_loc = t_mm(xt, ma[:, :STATE].astype(BF16))
    g_loc = t_mm(yt, ma[:, STATE:].astype(BF16))
    diag = jnp.where(iota((8, 128), 0) == iota((8, 128), 1), tot, 0.0)
    dm = exact(diag, jnp.ones((128, 128), F32))
    hi = dm.astype(BF16).astype(F32)
    drow = jnp.where(iota((8, 128), 1) < 64, hi, dm - hi)
    for zz in range(NZ):
        for which, v in ((0, f_loc), (1, g_loc)):
            rows = [v[h * HDIM + zz * 8 : h * HDIM + zz * 8 + 8] for h in range(HEADS)]
            send_o[zz * 2 + which] = jnp.concatenate(rows + [drow], axis=0).astype(BF16)
    xa_o[...] = xa
    zi_o[...] = zi
    zm_o[...] = zm
    dt_o[...] = dt
    cum_o[...] = cum
    sr_o[...] = srb
    og_o[...] = og


def forward(*args):
    return pl.pallas_call(
        forward_kernel,
        out_shape=(
            jax.ShapeDtypeStruct((TOK, INNER), F32),
            jax.ShapeDtypeStruct((TOK, INNER), F32),
            jax.ShapeDtypeStruct((TOK, 2 * STATE), F32),
            jax.ShapeDtypeStruct((TOK, 128), F32),
            jax.ShapeDtypeStruct((TOK, 128), F32),
            jax.ShapeDtypeStruct((TOK, 128), F32),
            jax.ShapeDtypeStruct((TOK, INNER), BF16),
            jax.ShapeDtypeStruct((D, INNER), BF16),
            jax.ShapeDtypeStruct((2 * NZ, CHUNK, STATE), BF16),
        ),
        in_specs=[VM] * 9,
        out_specs=(VM,) * 9,
        compiler_params=pltpu.CompilerParams(vmem_limit_bytes=LIMIT),
        name="forward",
    )(*args)


def state_kernel(send, out, recv, back, local_sem, s1, r1, s2, r2):
    z, yh = lax.axis_index("seq_0"), lax.axis_index("seq_1")
    n = 2 * NZ
    me = z * 2 + yh
    barrier = pltpu.get_barrier_semaphore()

    def at(q):
        return {"seq_0": q // 2, "seq_1": lax.rem(q, 2)}

    for off in range(1, n):
        pl.semaphore_signal(
            barrier, inc=1, device_id=at(lax.rem(me + off, n)), device_id_type=MESH
        )
    pl.semaphore_wait(barrier, n - 1)

    def push(src, dst, ss, rs, off):
        to = lax.rem(me + off, n)
        return pltpu.make_async_remote_copy(
            src_ref=src.at[to], dst_ref=dst.at[me], send_sem=ss.at[off], recv_sem=rs.at[off],
            device_id=at(to), device_id_type=MESH,
        )

    def pull(src, dst, ss, rs, off):
        origin = lax.rem(me + n - off, n)
        return pltpu.make_async_remote_copy(
            src_ref=src.at[origin], dst_ref=dst.at[origin], send_sem=ss.at[off],
            recv_sem=rs.at[off], device_id=at(origin), device_id_type=MESH,
        )

    first = [push(send, recv, s1, r1, off) for off in range(1, n)]
    for d in first:
        d.start()
    own = pltpu.make_async_copy(send.at[me], recv.at[me], local_sem.at[0])
    own.start()
    own.wait()
    for off in range(1, n):
        pull(send, recv, s1, r1, off).wait_recv()
    run = jnp.zeros((HEADS * 8, STATE), F32)
    for j in range(n):
        k = jnp.where(yh == 0, j, n - 1 - j)
        got = recv[k].astype(F32)
        rows = got[HEADS * 8 :]
        rows = rows + pltpu.roll(rows, 64, 1)
        decay = jnp.exp(rows)
        back[k] = jnp.concatenate([run, rows], axis=0).astype(BF16)
        wide = jnp.concatenate(
            [jnp.broadcast_to(decay[h : h + 1], (8, STATE)) for h in range(HEADS)], axis=0
        )
        run = wide * run + got[: HEADS * 8]
    second = [push(back, out, s2, r2, off) for off in range(1, n)]
    for d in second:
        d.start()
    own = pltpu.make_async_copy(back.at[me], out.at[me], local_sem.at[1])
    own.start()
    own.wait()
    for off in range(1, n):
        pull(back, out, s2, r2, off).wait_recv()
    for d in first + second:
        d.wait_send()


def states(send):
    n = 2 * NZ
    return pl.pallas_call(
        state_kernel,
        out_shape=jax.ShapeDtypeStruct((n, CHUNK, STATE), BF16),
        in_specs=[VM],
        out_specs=VM,
        scratch_shapes=[
            pltpu.VMEM((n, CHUNK, STATE), BF16),
            pltpu.VMEM((n, CHUNK, STATE), BF16),
            pltpu.SemaphoreType.DMA((2,)),
            pltpu.SemaphoreType.DMA((n,)),
            pltpu.SemaphoreType.DMA((n,)),
            pltpu.SemaphoreType.DMA((n,)),
            pltpu.SemaphoreType.DMA((n,)),
        ],
        compiler_params=pltpu.CompilerParams(collective_id=1, has_side_effects=True),
        name="states",
    )(send)


def backward_kernel(
    xa_r, zi_r, zm_r, dt_r, cum_r, sr_r, og_r, st, ci, cm, dlog, skip,
    gi_o, gm_o, ds_o, gmt_o,
):
    z, yh, c = (lax.axis_index(a) for a in SEQ)
    flag = jnp.where(z * 2 + yh == 0, 0.0, 1.0).astype(F32)
    pick = head_pick(c)
    ex, hs = head_expand(), head_sum()
    xa, zi, zm = xa_r[...], zi_r[...], zm_r[...]
    dt, cum = dt_r[...], cum_r[...]
    og = og_r[...]
    dy = og.astype(F32)
    rate = exact(jnp.exp(dlog[...]), pick)
    skp = exact(skip[...], pick)
    tot = cum[TOK - 1 : TOK]
    ecum = exact(jnp.exp(cum), ex)
    etail = exact(jnp.exp(tot - cum), ex)
    dte = exact(dt, ex)

    def collect(which):
        blocks = [st[2 * zz + which].astype(F32) for zz in range(NZ)]
        rows = [blocks[zz][h * 8 : h * 8 + 8] for h in range(HEADS) for zz in range(NZ)]
        return jnp.concatenate(rows, axis=0)

    h0, ge = collect(0), collect(1)
    h0b, geb = h0.astype(BF16), ge.astype(BF16)
    sz = jax.nn.sigmoid(zm)
    ma = zm * sz
    bm, cmx = ma[:, :STATE].astype(BF16), ma[:, STATE:].astype(BF16)
    xdt = xa * dte
    xdtb = xdt.astype(BF16)
    xdtf = xdtb.astype(F32)
    scores = mm_t(cmx, bm)
    causal = iota((TOK, TOK), 0) >= iota((TOK, TOK), 1)
    cumt = cum.T
    dscore = jnp.zeros((TOK, TOK), F32)
    ys, us = [], []
    for h in range(HEADS):
        cols = slice(h * HDIM, (h + 1) * HDIM)
        decay = jnp.exp(jnp.where(causal, cum[:, h : h + 1] - cumt[h : h + 1, :], -1e30))
        m = (decay * scores).astype(BF16)
        ys.append(mm(m, xdtb[:, cols]))
        us.append(t_mm(m, og[:, cols]))
        dscore = dscore + decay * mm_t(og[:, cols], xdtb[:, cols])
    y = jnp.concatenate(ys, axis=1) + ecum * mm_t(cmx, h0b)
    ug = etail * mm_t(bm, geb)
    u = jnp.concatenate(us, axis=1) + ug
    dxa = dte * u + exact(skp, ex) * dy
    ddt = exact(xa * u, hs)
    dcum = exact(dy * y - xdtf * u, hs)
    e_sum = jnp.sum(exact(xdtf * ug, hs), axis=0, keepdims=True)
    hg = exact(
        jnp.ones((8, STATE), F32), (h0 * ge).T
    )
    carry = jnp.exp(tot) * exact(hg, hs)[0:1]
    upper = one_hot(iota((TOK, TOK), 0) <= iota((TOK, TOK), 1))
    da = exact(upper, dcum) + e_sum + carry
    dsr = (ddt - rate * da) * jax.nn.sigmoid(sr_r[...])
    dsb = dscore.astype(BF16)
    d_out = mm(dsb, bm) + mm((dy * ecum).astype(BF16), h0b)
    d_in = t_mm(dsb, cmx) + mm((xdt * etail).astype(BF16), geb)
    gm = jnp.concatenate([d_in, d_out], axis=1) * (sz * (1.0 + zm * (1.0 - sz)))
    si = jax.nn.sigmoid(zi)
    gi = dxa * (si * (1.0 + zi * (1.0 - si)))
    keep = jnp.where(iota((EXT, 1), 0) < PRE, flag, 1.0)

    def back(g, k):
        g = jnp.concatenate([jnp.zeros((PRE, g.shape[1]), F32), g], axis=0)
        return jnp.where(keep > 0.0, conv_back(g, k), 0.0).astype(BF16)

    gi_o[...] = back(gi, half_of(ci[...], c))
    gme = back(gm, cm[...])
    gm_o[...] = gme
    ds_o[...] = jnp.concatenate([jnp.zeros((PRE, 128), F32), dsr], axis=0).astype(BF16)
    eye = one_hot(iota((EXT, EXT), 0) == iota((EXT, EXT), 1)).astype(BF16)
    gmt = t_mm(gme, eye).astype(BF16)
    for j in range(8):
        gmt_o[j] = gmt[j * 32 : j * 32 + 32]


def backward(*args):
    return pl.pallas_call(
        backward_kernel,
        out_shape=(
            jax.ShapeDtypeStruct((EXT, INNER), BF16),
            jax.ShapeDtypeStruct((EXT, 2 * STATE), BF16),
            jax.ShapeDtypeStruct((EXT, 128), BF16),
            jax.ShapeDtypeStruct((8, 32, EXT), BF16),
        ),
        in_specs=[VM] * 12,
        out_specs=(VM,) * 4,
        compiler_params=pltpu.CompilerParams(vmem_limit_bytes=LIMIT),
        name="backward",
    )(*args)


def mix_kernel(src, out, local_sem, ss, rs):
    c, x = lax.axis_index("seq_2"), lax.axis_index("chan")
    me = c * 4 + x
    barrier = pltpu.get_barrier_semaphore()

    def at(j):
        return {"seq_2": j // 4, "chan": lax.rem(j, 4)}

    for off in range(1, 8):
        pl.semaphore_signal(
            barrier, inc=1, device_id=at(lax.rem(me + off, 8)), device_id_type=MESH
        )
    pl.semaphore_wait(barrier, 7)
    sends = []
    for off in range(1, 8):
        to = lax.rem(me + off, 8)
        d = pltpu.make_async_remote_copy(
            src_ref=src.at[to], dst_ref=out.at[me], send_sem=ss.at[off], recv_sem=rs.at[off],
            device_id=at(to), device_id_type=MESH,
        )
        d.start()
        sends.append(d)
    own = pltpu.make_async_copy(src.at[me], out.at[me], local_sem)
    own.start()
    own.wait()
    for off in range(1, 8):
        origin = lax.rem(me + 8 - off, 8)
        pltpu.make_async_remote_copy(
            src_ref=src.at[origin], dst_ref=out.at[origin], send_sem=ss.at[off],
            recv_sem=rs.at[off], device_id=at(origin), device_id_type=MESH,
        ).wait_recv()
    for d in sends:
        d.wait_send()


def mix(src):
    return pl.pallas_call(
        mix_kernel,
        out_shape=jax.ShapeDtypeStruct((8, 32, EXT), BF16),
        in_specs=[VM],
        out_specs=VM,
        scratch_shapes=[
            pltpu.SemaphoreType.DMA(()),
            pltpu.SemaphoreType.DMA((8,)),
            pltpu.SemaphoreType.DMA((8,)),
        ],
        compiler_params=pltpu.CompilerParams(collective_id=2, has_side_effects=True),
        name="mix",
    )(src)


def product_kernel(norm, xe, gi_r, gm_r, ds_r, mix_r, wih, wm, ws, ra_o, rb_o, p_o, pb_o):
    c = lax.axis_index("seq_2")
    total = jnp.zeros((32, EXT), F32)
    for j in range(8):
        total = total + mix_r[j].astype(F32)
    place_mix = one_hot(iota((32, 128), 1) == iota((32, 128), 0) + 64).astype(BF16)
    place_step = one_hot(
        (iota((128, 128), 1) == iota((128, 128), 0) + 96) & (iota((128, 128), 0) < HEADS)
    ).astype(BF16)
    gi = gi_r[...]
    ds = ds_r[...]
    last = t_mm(total.astype(BF16), place_mix) + mm(ds, place_step)
    last = last + jnp.concatenate([gi[:, 256:].astype(F32), jnp.zeros((EXT, 64), F32)], axis=1)
    rhs = jnp.concatenate([gi[:, :256], last.astype(BF16)], axis=1)
    for b in range(4):
        r = (t_mm(xe[:, b * 640 : (b + 1) * 640], rhs) * norm).astype(BF16)
        for g in range(8):
            dp, zz, yh = b // 2, (b % 2) * 4 + g // 2, g % 2
            block = r[g * ROWS : (g + 1) * ROWS]
            ra_o[zz, yh * 2 + dp] = block[:, :128]
            rb_o[yh * 2 + dp, zz] = block[:, 128:]
    pick = head_pick(c).astype(BF16)
    ds10 = mm_t(ds, pick).astype(BF16)
    gm = gm_r[...]
    for b in range(4):
        rows = slice(b * 640, (b + 1) * 640)
        part = mm_t(gi, wih[rows]) + mm_t(gm, wm[rows]) + mm_t(ds10, ws[rows])
        part = part.astype(BF16)
        pb_o[:, rows] = part[:PRE]
        for j in range(8):
            p_o[j, :, rows] = part[PRE + j * 32 : PRE + j * 32 + 32]


def products(norm, *args):
    return pl.pallas_call(
        functools.partial(product_kernel, norm),
        out_shape=(
            jax.ShapeDtypeStruct((NZ, 4, ROWS, 128), BF16),
            jax.ShapeDtypeStruct((4, NZ, ROWS, 256), BF16),
            jax.ShapeDtypeStruct((8, 32, D), BF16),
            jax.ShapeDtypeStruct((PRE, D), BF16),
        ),
        in_specs=[VM] * 8,
        out_specs=(VM,) * 4,
        compiler_params=pltpu.CompilerParams(vmem_limit_bytes=LIMIT),
        name="products",
    )(*args)


def reduce_kernel(
    ra, rb, p, pb, fin, tiles, pin, pbin,
    ain, bin_, sa, sb, a2, b2, full,
    lsem, sa1, ra1, sb1, rb1, sp, rp, sq, rq, sa2, ra2, sb2, rb2, sf, rf,
):
    dp = lax.axis_index("dp")
    z, yh, c, x = (lax.axis_index(a) for a in SEQ_CHAN)
    y = yh * 2 + dp
    j8 = c * 4 + x
    q = z * 2 + yh
    nq, pq = lax.rem(q + 1, 2 * NZ), lax.rem(q + 2 * NZ - 1, 2 * NZ)
    barrier = pltpu.get_barrier_semaphore()

    def at_z(k):
        return {"seq_0": k}

    def at_y(k):
        return {"seq_1": k // 2, "dp": lax.rem(k, 2)}

    def at_j(k):
        return {"seq_2": k // 4, "chan": lax.rem(k, 4)}

    def tell(where):
        pl.semaphore_signal(barrier, inc=1, device_id=where, device_id_type=MESH)

    for off in range(1, NZ):
        tell(at_z(lax.rem(z + off, NZ)))
    for off in range(1, 4):
        tell(at_y(lax.rem(y + off, 4)))
    for off in range(1, 8):
        tell(at_j(lax.rem(j8 + off, 8)))

    @pl.when((c == 1) & (x == 3))
    def _():
        for k in range(8):
            tell({"seq_0": nq // 2, "seq_1": lax.rem(nq, 2), "seq_2": k // 4, "chan": k % 4})

    pl.semaphore_wait(barrier, NZ - 1 + 3 + 7 + 1)

    def send(src, dst, me, n, at, ss, rs, off):
        to = lax.rem(me + off, n)
        return pltpu.make_async_remote_copy(
            src_ref=src.at[to], dst_ref=dst.at[me], send_sem=ss.at[off], recv_sem=rs.at[off],
            device_id=at(to), device_id_type=MESH,
        )

    def arrive(src, dst, me, n, at, ss, rs, off):
        origin = lax.rem(me + n - off, n)
        return pltpu.make_async_remote_copy(
            src_ref=src.at[origin], dst_ref=dst.at[origin], send_sem=ss.at[off],
            recv_sem=rs.at[off], device_id=at(origin), device_id_type=MESH,
        )

    za = (ra, ain, z, NZ, at_z, sa1, ra1)
    yb = (rb, bin_, y, 4, at_y, sb1, rb1)
    xp = (p, pin, j8, 8, at_j, sp, rp)
    sends = [send(*yb, off) for off in (2, 1, 3)]
    sends += [send(*za, off) for off in (4, 3, 5, 2, 6, 1, 7)]
    sends += [send(*xp, off) for off in range(1, 8)]
    edge = pltpu.make_async_remote_copy(
        src_ref=pb, dst_ref=pbin.at[j8], send_sem=sq, recv_sem=rq.at[j8],
        device_id={"seq_0": pq // 2, "seq_1": lax.rem(pq, 2), "seq_2": 1, "chan": 3},
        device_id_type=MESH,
    )
    for d in sends:
        d.start()
    edge.start()
    own_a = pltpu.make_async_copy(ra.at[z], ain.at[z], lsem.at[0])
    own_b = pltpu.make_async_copy(rb.at[y], bin_.at[y], lsem.at[1])
    own_p = pltpu.make_async_copy(p.at[j8], pin.at[j8], lsem.at[2])
    for d in (own_a, own_b, own_p):
        d.start()
    own_a.wait()
    for off in range(1, NZ):
        arrive(*za, off).wait_recv()
    for k in range(4):
        acc = ain[0, k].astype(F32)
        for i in range(1, NZ):
            acc = acc + ain[i, k].astype(F32)
        sa[k] = acc.astype(BF16)
    ya = (sa, a2, y, 4, at_y, sa2, ra2)
    zb = (sb, b2, z, NZ, at_z, sb2, rb2)
    more = [send(*ya, off) for off in (2, 1, 3)]
    for d in more:
        d.start()
    own_b.wait()
    for off in range(1, 4):
        arrive(*yb, off).wait_recv()
    for k in range(NZ):
        acc = bin_[0, k].astype(F32)
        for i in range(1, 4):
            acc = acc + bin_[i, k].astype(F32)
        sb[k] = acc.astype(BF16)
    last = [send(*zb, off) for off in (4, 3, 5, 2, 6, 1, 7)]
    for d in last:
        d.start()
    own_sa = pltpu.make_async_copy(sa.at[y], a2.at[y], lsem.at[3])
    own_sb = pltpu.make_async_copy(sb.at[z], b2.at[z], lsem.at[4])
    own_sa.start()
    own_sb.start()
    own_sa.wait()
    own_sb.wait()
    for off in range(1, 4):
        arrive(*ya, off).wait_recv()
    for off in range(1, NZ):
        arrive(*zb, off).wait_recv()
    acc_a = a2[0].astype(F32)
    for i in range(1, 4):
        acc_a = acc_a + a2[i].astype(F32)
    acc_b = b2[0].astype(F32)
    for i in range(1, NZ):
        acc_b = acc_b + b2[i].astype(F32)
    for k in range(2):
        rows = slice(k * 40, (k + 1) * 40)
        full[k, :, :128] = acc_a[rows]
        full[k, :, 128:] = acc_b[rows]
    sib = 1 - c
    swap = pltpu.make_async_remote_copy(
        src_ref=full.at[sib], dst_ref=fin.at[c], send_sem=sf.at[0], recv_sem=rf.at[0],
        device_id={"seq_2": sib}, device_id_type=MESH,
    )
    swap_in = pltpu.make_async_remote_copy(
        src_ref=full.at[sib], dst_ref=fin.at[sib], send_sem=sf.at[0], recv_sem=rf.at[0],
        device_id={"seq_2": sib}, device_id_type=MESH,
    )
    swap.start()
    outs = []
    for off in range(1, 8):
        to = lax.rem(j8 + off, 8)
        d = pltpu.make_async_remote_copy(
            src_ref=full.at[to // 4, :, pl.ds(256, 128)], dst_ref=tiles.at[j8],
            send_sem=sf.at[off], recv_sem=rf.at[off], device_id=at_j(to), device_id_type=MESH,
        )
        d.start()
        outs.append(d)
    keep = pltpu.make_async_copy(full.at[c], fin.at[c], lsem.at[5])
    keep_t = pltpu.make_async_copy(
        full.at[c, :, pl.ds(256, 128)], tiles.at[j8], lsem.at[6]
    )
    keep.start()
    keep_t.start()
    own_p.wait()
    for off in range(1, 8):
        arrive(*xp, off).wait_recv()

    @pl.when((c == 1) & (x == 3))
    def _():
        for k in range(8):
            pltpu.make_async_remote_copy(
                src_ref=pb, dst_ref=pbin.at[k], send_sem=sq, recv_sem=rq.at[k],
                device_id={"seq_2": 0}, device_id_type=MESH,
            ).wait_recv()

    keep.wait()
    keep_t.wait()
    swap_in.wait_recv()
    for off in range(1, 8):
        origin = lax.rem(j8 + 8 - off, 8)
        pltpu.make_async_remote_copy(
            src_ref=full.at[c, :, pl.ds(256, 128)], dst_ref=tiles.at[origin],
            send_sem=sf.at[off], recv_sem=rf.at[off], device_id=at_j(origin),
            device_id_type=MESH,
        ).wait_recv()
    for d in sends + more + last + outs + [edge, swap]:
        d.wait_send()


def reductions(ra, rb, p, pb):
    dma = pltpu.SemaphoreType.DMA
    return pl.pallas_call(
        reduce_kernel,
        out_shape=(
            jax.ShapeDtypeStruct((2, 40, 384), F32),
            jax.ShapeDtypeStruct((8, 40, 128), F32),
            jax.ShapeDtypeStruct((8, 32, D), BF16),
            jax.ShapeDtypeStruct((8, PRE, D), BF16),
        ),
        in_specs=[VM] * 4,
        out_specs=(VM,) * 4,
        scratch_shapes=[
            pltpu.VMEM((NZ, 4, ROWS, 128), BF16),
            pltpu.VMEM((4, NZ, ROWS, 256), BF16),
            pltpu.VMEM((4, ROWS, 128), BF16),
            pltpu.VMEM((NZ, ROWS, 256), BF16),
            pltpu.VMEM((4, ROWS, 128), BF16),
            pltpu.VMEM((NZ, ROWS, 256), BF16),
            pltpu.VMEM((2, 40, 384), F32),
            dma((7,)), dma((8,)), dma((8,)), dma((4,)), dma((4,)), dma((8,)), dma((8,)),
            dma(()), dma((8,)), dma((4,)), dma((4,)), dma((8,)), dma((8,)), dma((8,)), dma((8,)),
        ],
        compiler_params=pltpu.CompilerParams(
            collective_id=3, has_side_effects=True, vmem_limit_bytes=LIMIT
        ),
        name="reductions",
    )(ra, rb, p, pb)


def finish_kernel(fin, tiles, pin, pbin, ig_o, iw_o, mw_o, sw_o):
    z, yh, c, x = (lax.axis_index(a) for a in SEQ_CHAN)
    for k in range(2):
        iw_o[:, k * INNER : (k + 1) * INNER] = fin[k, :, :INNER]
        sw_o[:, k * HEADS : (k + 1) * HEADS] = fin[k, :, 352 : 352 + HEADS]
    rows = one_hot(iota((10, 40), 1) == iota((10, 40), 0) + 10 * x)
    for j in range(8):
        mw_o[:, j * 32 : (j + 1) * 32] = exact(rows, tiles[j])[:, 64:96]
    acc = pin[0].astype(F32)
    for j in range(1, 8):
        acc = acc + pin[j].astype(F32)
    ig_o[...] = acc.astype(BF16)

    @pl.when((c == 1) & (x == 3))
    def _():
        edge = pbin[0].astype(F32)
        for j in range(1, 8):
            edge = edge + pbin[j].astype(F32)
        ig_o[16:, :] = (acc[16:] + roll(edge, 0)).astype(BF16)


def finish(*args):
    return pl.pallas_call(
        finish_kernel,
        out_shape=(
            jax.ShapeDtypeStruct((32, D), BF16),
            jax.ShapeDtypeStruct((40, 2 * INNER), F32),
            jax.ShapeDtypeStruct((10, 2 * STATE), F32),
            jax.ShapeDtypeStruct((40, 2 * HEADS), F32),
        ),
        in_specs=[VM] * 4,
        out_specs=(VM,) * 4,
        compiler_params=pltpu.CompilerParams(vmem_limit_bytes=LIMIT),
        name="finish",
    )(*args)


def body(
    layer_input,
    inner_weight,
    mixer_weight,
    step_weight,
    conv_inner,
    conv_mixer,
    step_bias,
    decay_log,
    skip_gain,
    output_grad,
):
    norm = 1.0 / math.sqrt(8192)
    bias, dlog, skip = (v.reshape(1, -1) for v in (step_bias, decay_log, skip_gain))
    xe, ogx = gather(layer_input[0], output_grad[0])
    xa, zi, zm, dt, cum, sr, og, wih, send = forward(
        xe, ogx, inner_weight, mixer_weight, step_weight, conv_inner, conv_mixer, bias, dlog
    )
    st = states(send)
    gi, gm, ds, gmt = backward(
        xa, zi, zm, dt, cum, sr, og, st, conv_inner, conv_mixer, dlog, skip
    )
    mixed = mix(gmt)
    ra, rb, p, pb = products(norm, xe, gi, gm, ds, mixed, wih, mixer_weight, step_weight)
    fin, tiles, pin, pbin = reductions(ra, rb, p, pb)
    ig, iw, mw, sw = finish(fin, tiles, pin, pbin)
    return ig[None], iw, mw, sw


def solution(mesh):
    split = Mesh(
        mesh.devices.reshape(mesh.shape["dp"], 8, 2, 2, mesh.shape["chan"]),
        ("dp", "seq_0", "seq_1", "seq_2", "chan"),
    )
    placed = (
        P("dp", SEQ_CHAN, None),
        P(None, "chan"),
        P(),
        P(None, "chan"),
        P(None, "chan"),
        P(),
        P("chan"),
        P("chan"),
        P("chan"),
        P("dp", SEQ, "chan"),
    )
    return jax.shard_map(
        body,
        mesh=split,
        in_specs=placed,
        out_specs=(
            P("dp", SEQ_CHAN, None),
            P(DP_SEQ, "chan"),
            P(DP_SEQ_CHAN, None),
            P(DP_SEQ, "chan"),
        ),
        check_vma=False,
    )
```

time: 377 us -> 121 us (0.32)
  Pallas kernels: 0 us -> 117 us
  waiting for transfers between devices: 114 us -> 0 us
  blocking collectives: 71.8 us -> 0 us
  starting transfers between devices: 48 us -> 0 us
  other arithmetic: 44.3 us -> 0 us
  local copies, waits for them, and re-layouts: 45.2 us -> 3.43 us
  matrix products: 35.2 us -> 0 us
  between operations: 15.4 us -> 0.67 us
    pallas_call x0 -> x8, Pallas kernels: none -> 117 us  [the longest x1 39.8 us: reductions(): pl.pallas_call(reduce_kernel, out_shape=(jax.ShapeDtypeStruct((2, 40, 384...]
    all_to_all x5 -> x0, waiting for transfers between devices: 103 us -> none  [the longest x3 95.6 us: sent_and_summed(): lax.all_to_all(parts, axis, split_axis=0, concat_axis=0, tiled=True)]
    all_gather x10 -> x0, blocking collectives: 71.8 us -> none  [the longest x5 40.9 us: entering(): lax.all_gather(part.astype(kind), axis)]
    dot_general x24 -> x0, matrix products: 35.2 us -> none  [the longest x4 8.2 us: project_back(): lax.dot_general(gradient, weight, (((1,), (1,)), ((), ())), preferred_ele...]
    all_to_all x5 -> x0, starting transfers between devices: 28.4 us -> none  [the longest x3 19.5 us: sent_and_summed(): lax.all_to_all(parts, axis, split_axis=0, concat_axis=0, tiled=True)]
    ppermute x3 -> x0, starting transfers between devices: 19.6 us -> none  [from_behind(): lax.ppermute(value, axis, [(source, source + steps) for source in range(f...]
    reduce_sum x6 -> x0, other arithmetic: 11.5 us -> none  [the longest x3 6.37 us: sent_and_summed(): return arrived.astype(jnp.float32).sum(axis=0)]
    all_gather x2 -> x0, waiting for transfers between devices: 10.5 us -> none  [the longest x1 10.5 us: entering(): lax.all_gather(part.astype(kind), axis)]
  transfers between devices with their start and end apart: 10 -> 0, of which waited for: 6 -> 0; matrix products, arithmetic and copies ran while one was open for 21% -> 0% of each run, Pallas kernels for 0% -> 0%
where the time goes in v1:
time: 121 us
  Pallas kernels  117 us (97%)
  local copies, waits for them, and re-layouts  3.43 us (3%)
    pallas_call x1, Pallas kernels, reductions(): pl.pallas_call(reduce_kernel, out_shape=(jax.ShapeDtypeStruct((2, 40, 384...  39.8 us
    pallas_call x1, Pallas kernels, states(): pl.pallas_call(state_kernel, out_shape=jax.ShapeDtypeStruct((n, CHUNK, ST...  25.2 us
    pallas_call x1, Pallas kernels, gather(): pl.pallas_call(gather_kernel, out_shape=(jax.ShapeDtypeStruct((EXT, D), B...  17.5 us
    pallas_call x1, Pallas kernels, mix(): pl.pallas_call(mix_kernel, out_shape=jax.ShapeDtypeStruct((8, 32, EXT), B...  9.93 us
    pallas_call x1, Pallas kernels, forward(): pl.pallas_call(forward_kernel, out_shape=(jax.ShapeDtypeStruct((TOK, INNE...  7.5 us
    pallas_call x1, Pallas kernels, products(): pl.pallas_call(functools.partial(product_kernel, norm), out_shape=(jax.Sh...  7.09 us
    pallas_call x1, Pallas kernels, backward(): pl.pallas_call(backward_kernel, out_shape=(jax.ShapeDtypeStruct((EXT, INN...  6.99 us
    unnamed x2, local copies, waits for them, and re-layouts  3.43 us

profile of v1, /device:TPU:1, one launch (start us, length us, event | category | flops | bytes accessed | tf_op | source)
XLA Modules:
  0.0 121.0 jit_solution(14464529076146610945)
XLA Ops:
  0.6 2.0 %copy.14.ws = bf16[2560,10]{1,0:T(8,128)(2,1)} copy(bf16[2560,10]{0,1:T(8,128)(2,1)} %param.13) | data formatting | bytes 102400 | tf_op args[3]
  2.7 17.5 %gather.1 = (bf16[272,2560]{1,0:T(8,128)(2,1)}, bf16[2,128,640]{2,1,0:T(8,128)(2,1)}) custom-call(bf16[32,2560]{1,0:T(8,128)(2,1)} %bitcast.6, bf16[128,640]{1,0:T(8,128)(2,1)} %bitcast.7), custom_call_target="tpu_custom_call" | custom-call | tf_op jit(solution)/shard_map/gather/pallas_call | solution.py:209
  20.2 7.5 %forward.1 = (f32[256,320]{1,0:T(8,128)}, f32[256,320]{1,0:T(8,128)}, f32[256,256]{1,0:T(8,128)}, f32[256,128]{1,0:T(8,128)}, f32[256,128]{1,0:T(8,128)}, /*inde...) custom-call(bf16[272,2560]{1,0:T(8,128)(2,1)} %get-tuple-element.31.xe, ...), custom_call_target="tpu_custom_call" | custom-call | tf_op jit(solution)/shard_map/forward/pallas_call | solution.py:281
  27.7 25.2 %states.1.st = bf16[16,48,128]{2,1,0:T(8,128)(2,1)} custom-call(bf16[16,48,128]{2,1,0:T(8,128)(2,1)} %get-tuple-element.40.send), custom_call_target="tpu_custom_call" | custom-call | tf_op jit(solution)/shard_map/states/pallas_call | solution.py:364
  52.8 7.0 %backward.1 = (bf16[272,320]{1,0:T(8,128)(2,1)}, bf16[272,256]{1,0:T(8,128)(2,1)}, bf16[272,128]{1,0:T(8,128)(2,1)}, bf16[8,32,272]{2,1,0:T(8,128)(2,1)}) custom-call(f32[256,320]{1,0:T(8,128)} %get-tuple-element.33.xa_r, f32[256,320]{1,0:T(8,128)} %get-tuple-element.34.zi_r, f32[256,256]{1,0:T(8,128)} %get-tuple-element.35.zm_r, ...), custom_call_target="tpu_custom_call" | custom-call | tf_op jit(solution)/shard_map/backward/pallas_call | solution.py:464
  59.8 9.9 %mix.1.mix_r = bf16[8,32,272]{2,1,0:T(8,128)(2,1)} custom-call(bf16[8,32,272]{2,1,0:T(8,128)(2,1)} %get-tuple-element.44.src), custom_call_target="tpu_custom_call" | custom-call | tf_op jit(solution)/shard_map/mix/pallas_call | solution.py:515
  69.8 7.1 %products.1 = (bf16[8,4,80,128]{3,2,1,0:T(8,128)(2,1)}, bf16[4,8,80,256]{3,2,1,0:T(8,128)(2,1)}, bf16[8,32,2560]{2,1,0:T(8,128)(2,1)}, bf16[16,2560]{1,0:T(8,128)(2,1)}) custom-call(bf16[272,2560]{1,0:T(8,128)(2,1)} %get-tuple-element.31.xe, bf16[272,320]{1,0:T(8,128)(2,1)} %get-tuple-element.41.gi_r, bf16[272,256]{1,0:T(8,128)(2,1)} %get-tuple-element.42.gm_r, ...), custom_call_target="tpu_custom_call" | custom-call | tf_op jit(solution)/shard_map/products/pallas_call | solution.py:564
  76.8 39.8 %reductions.1 = (f32[2,40,384]{2,1,0:T(8,128)}, f32[8,40,128]{2,1,0:T(8,128)}, bf16[8,32,2560]{2,1,0:T(8,128)(2,1)}, bf16[8,16,2560]{2,1,0:T(8,128)(2,1)}) custom-call(bf16[8,4,80,128]{3,2,1,0:T(8,128)(2,1)} %get-tuple-element.46.ra, bf16[4,8,80,256]{3,2,1,0:T(8,128)(2,1)} %get-tuple-element.47.rb, bf16[8,32,2560]{2,1,0:T(8,128)(2,1)} %get-tuple-element.48.p, ...), custom_call_target="tpu_custom_call" | custom-call | tf_op jit(solution)/shard_map/reductions/pallas_call | solution.py:748
  116.7 2.9 %finish.1 = (bf16[32,2560]{1,0:T(8,128)(2,1)}, f32[40,640]{1,0:T(8,128)}, f32[10,256]{1,0:T(8,128)}, f32[40,10]{1,0:T(8,128)}) custom-call(f32[2,40,384]{2,1,0:T(8,128)} %get-tuple-element.50.fin, f32[8,40,128]{2,1,0:T(8,128)} %get-tuple-element.51.tiles, bf16[8,32,2560]{2,1,0:T(8,128)(2,1)} %get-tuple-element.52.pin, ...), custom_call_target="tpu_custom_call" | custom-call | tf_op jit(solution)/shard_map/finish/pallas_call | solution.py:798
  119.6 1.4 %copy.16 = f32[40,10]{0,1:T(8,128)} copy(f32[40,10]{1,0:T(8,128)} %get-tuple-element.61) | data formatting | bytes 3200

commit v2 on v1

--- a/solution.py
+++ b/solution.py
@@ -476,78 +476,143 @@
     )(*args)
 
 
-def mix_kernel(src, out, local_sem, ss, rs):
-    c, x = lax.axis_index("seq_2"), lax.axis_index("chan")
-    me = c * 4 + x
+def rows_of(ref, lo, n):
+    return ref[lo : lo + n]
+
+
+def sums_kernel(
+    norm, xe, gi_r, gm_r, ds_r, gmt, wih, wm, ws,
+    tiles, fb, pown, xin, pbin,
+    mixin, rb, yhold, yin, ra, a3, a4, a1, a2, sa, ya, sb, b3, b4, b1, b2, fa, fbs, p, psib, xhold,
+    pb, pbsib,
+    lsem, ms, mr, ys, yr, zs, zr, qs, qr, xs, xr, es, er, as_, ar, ts, tr, dsem, drem,
+):
+    dp = lax.axis_index("dp")
+    z, yh, c, x = (lax.axis_index(a) for a in SEQ_CHAN)
+    y = yh * 2 + dp
+    j8 = c * 4 + x
+    sib = 1 - c
+    q = z * 2 + yh
+    nq, pq = lax.rem(q + 1, 2 * NZ), lax.rem(q + 2 * NZ - 1, 2 * NZ)
     barrier = pltpu.get_barrier_semaphore()
 
-    def at(j):
-        return {"seq_2": j // 4, "chan": lax.rem(j, 4)}
-
+    def at_z(off):
+        return {"seq_0": lax.rem(z + off + NZ, NZ)}
+
+    def at_y(off):
+        k = lax.rem(y + off + 4, 4)
+        return {"seq_1": k // 2, "dp": lax.rem(k, 2)}
+
+    def at_x(off):
+        return {"chan": lax.rem(x + off + 4, 4)}
+
+    def at_j(k):
+        return {"seq_2": k // 4, "chan": lax.rem(k, 4)}
+
+    def tell(where):
+        pl.semaphore_signal(barrier, inc=1, device_id=where, device_id_type=MESH)
+
+    for off in (1, -1, 2, -2):
+        tell(at_z(off))
+    for off in (1, 2, 3):
+        tell(at_y(off))
     for off in range(1, 8):
-        pl.semaphore_signal(
-            barrier, inc=1, device_id=at(lax.rem(me + off, 8)), device_id_type=MESH
+        tell(at_j(lax.rem(j8 + off, 8)))
+
+    @pl.when((c == 1) & (x == 3))
+    def _():
+        for k in range(4):
+            tell({"seq_0": nq // 2, "seq_1": lax.rem(nq, 2), "chan": k})
+
+    pl.semaphore_wait(barrier, jnp.where(c == 1, 15, 14))
+
+    def remote(src, dst, ss, rs, where):
+        return pltpu.make_async_remote_copy(
+            src_ref=src, dst_ref=dst, send_sem=ss, recv_sem=rs, device_id=where,
+            device_id_type=MESH,
         )
-    pl.semaphore_wait(barrier, 7)
-    sends = []
+
+    pending = []
+
+    def go(d):
+        d.start()
+        pending.append(d)
+        return d
+
     for off in range(1, 8):
-        to = lax.rem(me + off, 8)
-        d = pltpu.make_async_remote_copy(
-            src_ref=src.at[to], dst_ref=out.at[me], send_sem=ss.at[off], recv_sem=rs.at[off],
-            device_id=at(to), device_id_type=MESH,
-        )
-        d.start()
-        sends.append(d)
-    own = pltpu.make_async_copy(src.at[me], out.at[me], local_sem)
-    own.start()
-    own.wait()
+        to = lax.rem(j8 + off, 8)
+        go(remote(gmt.at[to], mixin.at[off], ms.at[off], mr.at[off], at_j(to)))
+
+    gi = gi_r[...]
+    rhs = gi[:, :256]
+
+    def inner_rows(side):
+        for zhi in range(2):
+            base = pl.multiple_of(side * 1280 + zhi * 640, 128)
+            r = (t_mm(xe[:, pl.ds(base, 640)], rhs) * norm).astype(BF16)
+            for g in range(8):
+                for k in range(2):
+                    rb[(g % 2) * 2 + side, zhi * 4 + g // 2, k] = r[
+                        g * ROWS : (g + 1) * ROWS, k * 128 : (k + 1) * 128
+                    ]
+
+    up, down, far = lax.rem(y + 1, 4), lax.rem(y + 3, 4), lax.rem(y + 2, 4)
+    lo, hi = pl.ds(0, 4), pl.ds(4, 4)
+    inner_rows(dp)
+    go(remote(rb.at[far, lo], yhold.at[0], ys.at[0], yr.at[0], at_y(1)))
+    go(remote(rb.at[far, hi], yhold.at[1], ys.at[1], yr.at[1], at_y(-1)))
+    inner_rows(1 - dp)
+    go(remote(rb.at[up, hi], yin.at[0, hi], ys.at[2], yr.at[2], at_y(1)))
+    go(remote(rb.at[down, lo], yin.at[1, lo], ys.at[3], yr.at[3], at_y(-1)))
+
+    total = gmt[j8].astype(F32)
     for off in range(1, 8):
-        origin = lax.rem(me + 8 - off, 8)
-        pltpu.make_async_remote_copy(
-            src_ref=src.at[origin], dst_ref=out.at[origin], send_sem=ss.at[off],
-            recv_sem=rs.at[off], device_id=at(origin), device_id_type=MESH,
-        ).wait_recv()
-    for d in sends:
-        d.wait_send()
-
-
-def mix(src):
-    return pl.pallas_call(
-        mix_kernel,
-        out_shape=jax.ShapeDtypeStruct((8, 32, EXT), BF16),
-        in_specs=[VM],
-        out_specs=VM,
-        scratch_shapes=[
-            pltpu.SemaphoreType.DMA(()),
-            pltpu.SemaphoreType.DMA((8,)),
-            pltpu.SemaphoreType.DMA((8,)),
-        ],
-        compiler_params=pltpu.CompilerParams(collective_id=2, has_side_effects=True),
-        name="mix",
-    )(src)
-
-
-def product_kernel(norm, xe, gi_r, gm_r, ds_r, mix_r, wih, wm, ws, ra_o, rb_o, p_o, pb_o):
-    c = lax.axis_index("seq_2")
-    total = jnp.zeros((32, EXT), F32)
-    for j in range(8):
-        total = total + mix_r[j].astype(F32)
+        origin = lax.rem(j8 + 8 - off, 8)
+        remote(gmt.at[origin], mixin.at[off], ms.at[off], mr.at[off], at_j(origin)).wait_recv()
+        total = total + mixin[off].astype(F32)
     place_mix = one_hot(iota((32, 128), 1) == iota((32, 128), 0) + 64).astype(BF16)
     place_step = one_hot(
         (iota((128, 128), 1) == iota((128, 128), 0) + 96) & (iota((128, 128), 0) < HEADS)
     ).astype(BF16)
-    gi = gi_r[...]
     ds = ds_r[...]
     last = t_mm(total.astype(BF16), place_mix) + mm(ds, place_step)
     last = last + jnp.concatenate([gi[:, 256:].astype(F32), jnp.zeros((EXT, 64), F32)], axis=1)
-    rhs = jnp.concatenate([gi[:, :256], last.astype(BF16)], axis=1)
+    last = last.astype(BF16)
     for b in range(4):
-        r = (t_mm(xe[:, b * 640 : (b + 1) * 640], rhs) * norm).astype(BF16)
+        r = (t_mm(xe[:, b * 640 : (b + 1) * 640], last) * norm).astype(BF16)
         for g in range(8):
-            dp, zz, yh = b // 2, (b % 2) * 4 + g // 2, g % 2
-            block = r[g * ROWS : (g + 1) * ROWS]
-            ra_o[zz, yh * 2 + dp] = block[:, :128]
-            rb_o[yh * 2 + dp, zz] = block[:, 128:]
+            ra[(b % 2) * 4 + g // 2, (g % 2) * 2 + b // 2] = r[g * ROWS : (g + 1) * ROWS]
+
+    def z_first(src, n, r3, r4, r1, s, r):
+        h = n // 2
+        for k, sign in enumerate((1, -1)):
+            part = pl.ds(k * h, h)
+            dst = [lax.rem(z + sign * d + NZ, NZ) for d in range(5)]
+            go(remote(src.at[dst[4], part], r4.at[k], s.at[4 * k], r.at[4 * k], at_z(2 * sign)))
+            go(remote(src.at[dst[3]], r3.at[k], s.at[4 * k + 1], r.at[4 * k + 1], at_z(sign)))
+            go(remote(src.at[dst[1]], r1.at[k], s.at[4 * k + 2], r.at[4 * k + 2], at_z(sign)))
+
+    def z_second(src, n, r3, r4, r2, s, r):
+        h = n // 2
+        for k, sign in enumerate((1, -1)):
+            part = pl.ds(k * h, h)
+            t = lax.rem(z + 2 * sign + NZ, NZ)
+            remote(r3.at[k], r3.at[k], s.at[4 * k + 1], r.at[4 * k + 1], at_z(sign)).wait_recv()
+            remote(r4.at[k], r4.at[k], s.at[4 * k], r.at[4 * k], at_z(2 * sign)).wait_recv()
+            for i in range(n):
+                v = src[t, i].astype(F32) + r3[k, i].astype(F32)
+                if k * h <= i < (k + 1) * h:
+                    v = v + r4[k, i - k * h].astype(F32)
+                r3[k, i] = v.astype(BF16)
+            go(remote(r3.at[k], r2.at[k], s.at[4 * k + 3], r.at[4 * k + 3], at_z(2 * sign)))
+
+    def z_last(r1, r2, s, r):
+        for k, sign in enumerate((1, -1)):
+            remote(r1.at[k], r1.at[k], s.at[4 * k + 2], r.at[4 * k + 2], at_z(sign)).wait_recv()
+            remote(r2.at[k], r2.at[k], s.at[4 * k + 3], r.at[4 * k + 3], at_z(2 * sign)).wait_recv()
+
+    z_first(ra, 4, a3, a4, a1, zs, zr)
+
     pick = head_pick(c).astype(BF16)
     ds10 = mm_t(ds, pick).astype(BF16)
     gm = gm_r[...]
@@ -555,243 +620,184 @@
         rows = slice(b * 640, (b + 1) * 640)
         part = mm_t(gi, wih[rows]) + mm_t(gm, wm[rows]) + mm_t(ds10, ws[rows])
         part = part.astype(BF16)
-        pb_o[:, rows] = part[:PRE]
+        pb[:, rows] = part[:PRE]
         for j in range(8):
-            p_o[j, :, rows] = part[PRE + j * 32 : PRE + j * 32 + 32]
-
-
-def products(norm, *args):
+            for k in range(2):
+                at = PRE + j * 32 + k * 16
+                p[j // 4, j % 4, k, :, rows] = part[at : at + 16]
+    go(remote(p.at[sib], psib, dsem.at[0], drem.at[0], {"seq_2": sib}))
+    pb_out = remote(pb, pbsib, dsem.at[1], drem.at[1], {"seq_2": sib})
+
+    @pl.when(c == 0)
+    def _():
+        pb_out.start()
+
+    remote(yhold.at[0], yhold.at[0], ys.at[0], yr.at[0], at_y(1)).wait_recv()
+    for i in range(4):
+        yhold[0, i] = (rb[up, i].astype(F32) + yhold[0, i].astype(F32)).astype(BF16)
+    go(remote(yhold.at[0], yin.at[0, lo], ys.at[4], yr.at[4], at_y(1)))
+    remote(yhold.at[1], yhold.at[1], ys.at[1], yr.at[1], at_y(-1)).wait_recv()
+    for i in range(4):
+        yhold[1, i] = (rb[down, 4 + i].astype(F32) + yhold[1, i].astype(F32)).astype(BF16)
+    go(remote(yhold.at[1], yin.at[1, hi], ys.at[5], yr.at[5], at_y(-1)))
+
+    z_second(ra, 4, a3, a4, a2, zs, zr)
+
+    remote(psib, psib, dsem.at[0], drem.at[0], {"seq_2": sib}).wait_recv()
+    for k in range(4):
+        for h in range(2):
+            psib[k, h] = (p[c, k, h].astype(F32) + psib[k, h].astype(F32)).astype(BF16)
+    xu, xd, xf = lax.rem(x + 1, 4), lax.rem(x + 3, 4), lax.rem(x + 2, 4)
+    go(remote(psib.at[xf, 0], xhold.at[0], xs.at[0], xr.at[0], at_x(1)))
+    go(remote(psib.at[xf, 1], xhold.at[1], xs.at[1], xr.at[1], at_x(-1)))
+    go(remote(psib.at[xu, 1], xin.at[0, 1], xs.at[2], xr.at[2], at_x(1)))
+    go(remote(psib.at[xd, 0], xin.at[1, 0], xs.at[3], xr.at[3], at_x(-1)))
+    edge = remote(
+        pbsib, pbin.at[x], es, er.at[x],
+        {"seq_0": pq // 2, "seq_1": lax.rem(pq, 2), "chan": 3},
+    )
+
+    @pl.when(c == 1)
+    def _():
+        pb_out.wait_recv()
+        pbsib[...] = (pb[...].astype(F32) + pbsib[...].astype(F32)).astype(BF16)
+        edge.start()
+
+    for k in (2, 4):
+        part = hi if k == 2 else lo
+        remote(yin.at[0, part], yin.at[0, part], ys.at[k], yr.at[k], at_y(1)).wait_recv()
+    for k in (3, 5):
+        part = lo if k == 3 else hi
+        remote(yin.at[1, part], yin.at[1, part], ys.at[k], yr.at[k], at_y(-1)).wait_recv()
+    for i in range(NZ):
+        v = rb[y, i].astype(F32) + yin[0, i].astype(F32) + yin[1, i].astype(F32)
+        sb[i] = v.astype(BF16)
+    z_first(sb, 2, b3, b4, b1, qs, qr)
+
+    z_last(a1, a2, zs, zr)
+    for i in range(4):
+        v = ra[z, i].astype(F32)
+        for k in range(2):
+            v = v + a1[k, i].astype(F32) + a2[k, i].astype(F32)
+        sa[i] = v.astype(BF16)
+    for off in (2, 1, 3):
+        to = lax.rem(y + off, 4)
+        go(remote(sa.at[to], ya.at[off], as_.at[off], ar.at[off], at_y(off)))
+
+    remote(xhold.at[0], xhold.at[0], xs.at[0], xr.at[0], at_x(1)).wait_recv()
+    xhold[0] = (psib[xu, 0].astype(F32) + xhold[0].astype(F32)).astype(BF16)
+    go(remote(xhold.at[0], xin.at[0, 0], xs.at[4], xr.at[4], at_x(1)))
+    remote(xhold.at[1], xhold.at[1], xs.at[1], xr.at[1], at_x(-1)).wait_recv()
+    xhold[1] = (psib[xd, 1].astype(F32) + xhold[1].astype(F32)).astype(BF16)
+    go(remote(xhold.at[1], xin.at[1, 1], xs.at[5], xr.at[5], at_x(-1)))
+    pown[...] = psib[x]
+
+    z_second(sb, 2, b3, b4, b2, qs, qr)
+
+    v = sa[y].astype(F32)
+    for off in range(1, 4):
+        remote(ya.at[off], ya.at[off], as_.at[off], ar.at[off], at_y(off)).wait_recv()
+        v = v + ya[off].astype(F32)
+    fa[0] = v[:40]
+    fa[1] = v[40:]
+    for off in range(1, 8):
+        to = lax.rem(j8 + off, 8)
+        go(remote(fa.at[to // 4], tiles.at[j8], ts.at[off], tr.at[off], at_j(to)))
+    tiles[j8] = fa[c]
+
+    z_last(b1, b2, qs, qr)
+    for i in range(2):
+        v = sb[z, i].astype(F32)
+        for k in range(2):
+            v = v + b1[k, i].astype(F32) + b2[k, i].astype(F32)
+        fbs[0, :, i * 128 : (i + 1) * 128] = v[:40]
+        fbs[1, :, i * 128 : (i + 1) * 128] = v[40:]
+    go(remote(fbs.at[sib], fb.at[c], dsem.at[2], drem.at[2], {"seq_2": sib}))
+    fb[c] = fbs[c]
+
+    for k, half in ((2, 1), (4, 0)):
+        remote(xin.at[0, half], xin.at[0, half], xs.at[k], xr.at[k], at_x(1)).wait_recv()
+    for k, half in ((3, 0), (5, 1)):
+        remote(xin.at[1, half], xin.at[1, half], xs.at[k], xr.at[k], at_x(-1)).wait_recv()
+    for off in range(1, 8):
+        origin = lax.rem(j8 + 8 - off, 8)
+        remote(fa.at[c], tiles.at[origin], ts.at[off], tr.at[off], at_j(origin)).wait_recv()
+
+    @pl.when((c == 1) & (x == 3))
+    def _():
+        for k in range(4):
+            remote(pbsib, pbin.at[k], es, er.at[k], {"chan": 0}).wait_recv()
+
+    remote(fbs.at[c], fb.at[sib], dsem.at[2], drem.at[2], {"seq_2": sib}).wait_recv()
+    for d in pending:
+        d.wait_send()
+
+    @pl.when(c == 0)
+    def _():
+        pb_out.wait_send()
+
+    @pl.when(c == 1)
+    def _():
+        edge.wait_send()
+
+
+def sums(norm, *args):
+    dma = pltpu.SemaphoreType.DMA
+
+    def vm(*shape):
+        return pltpu.VMEM(shape, BF16)
+
     return pl.pallas_call(
-        functools.partial(product_kernel, norm),
+        functools.partial(sums_kernel, norm),
         out_shape=(
-            jax.ShapeDtypeStruct((NZ, 4, ROWS, 128), BF16),
-            jax.ShapeDtypeStruct((4, NZ, ROWS, 256), BF16),
-            jax.ShapeDtypeStruct((8, 32, D), BF16),
-            jax.ShapeDtypeStruct((PRE, D), BF16),
+            jax.ShapeDtypeStruct((8, 40, 128), F32),
+            jax.ShapeDtypeStruct((2, 40, 256), F32),
+            jax.ShapeDtypeStruct((2, 16, D), BF16),
+            jax.ShapeDtypeStruct((2, 2, 16, D), BF16),
+            jax.ShapeDtypeStruct((4, PRE, D), BF16),
         ),
         in_specs=[VM] * 8,
-        out_specs=(VM,) * 4,
-        compiler_params=pltpu.CompilerParams(vmem_limit_bytes=LIMIT),
-        name="products",
-    )(*args)
-
-
-def reduce_kernel(
-    ra, rb, p, pb, fin, tiles, pin, pbin,
-    ain, bin_, sa, sb, a2, b2, full,
-    lsem, sa1, ra1, sb1, rb1, sp, rp, sq, rq, sa2, ra2, sb2, rb2, sf, rf,
-):
-    dp = lax.axis_index("dp")
-    z, yh, c, x = (lax.axis_index(a) for a in SEQ_CHAN)
-    y = yh * 2 + dp
-    j8 = c * 4 + x
-    q = z * 2 + yh
-    nq, pq = lax.rem(q + 1, 2 * NZ), lax.rem(q + 2 * NZ - 1, 2 * NZ)
-    barrier = pltpu.get_barrier_semaphore()
-
-    def at_z(k):
-        return {"seq_0": k}
-
-    def at_y(k):
-        return {"seq_1": k // 2, "dp": lax.rem(k, 2)}
-
-    def at_j(k):
-        return {"seq_2": k // 4, "chan": lax.rem(k, 4)}
-
-    def tell(where):
-        pl.semaphore_signal(barrier, inc=1, device_id=where, device_id_type=MESH)
-
-    for off in range(1, NZ):
-        tell(at_z(lax.rem(z + off, NZ)))
-    for off in range(1, 4):
-        tell(at_y(lax.rem(y + off, 4)))
-    for off in range(1, 8):
-        tell(at_j(lax.rem(j8 + off, 8)))
-
-    @pl.when((c == 1) & (x == 3))
-    def _():
-        for k in range(8):
-            tell({"seq_0": nq // 2, "seq_1": lax.rem(nq, 2), "seq_2": k // 4, "chan": k % 4})
-
-    pl.semaphore_wait(barrier, NZ - 1 + 3 + 7 + 1)
-
-    def send(src, dst, me, n, at, ss, rs, off):
-        to = lax.rem(me + off, n)
-        return pltpu.make_async_remote_copy(
-            src_ref=src.at[to], dst_ref=dst.at[me], send_sem=ss.at[off], recv_sem=rs.at[off],
-            device_id=at(to), device_id_type=MESH,
-        )
-
-    def arrive(src, dst, me, n, at, ss, rs, off):
-        origin = lax.rem(me + n - off, n)
-        return pltpu.make_async_remote_copy(
-            src_ref=src.at[origin], dst_ref=dst.at[origin], send_sem=ss.at[off],
-            recv_sem=rs.at[off], device_id=at(origin), device_id_type=MESH,
-        )
-
-    za = (ra, ain, z, NZ, at_z, sa1, ra1)
-    yb = (rb, bin_, y, 4, at_y, sb1, rb1)
-    xp = (p, pin, j8, 8, at_j, sp, rp)
-    sends = [send(*yb, off) for off in (2, 1, 3)]
-    sends += [send(*za, off) for off in (4, 3, 5, 2, 6, 1, 7)]
-    sends += [send(*xp, off) for off in range(1, 8)]
-    edge = pltpu.make_async_remote_copy(
-        src_ref=pb, dst_ref=pbin.at[j8], send_sem=sq, recv_sem=rq.at[j8],
-        device_id={"seq_0": pq // 2, "seq_1": lax.rem(pq, 2), "seq_2": 1, "chan": 3},
-        device_id_type=MESH,
-    )
-    for d in sends:
-        d.start()
-    edge.start()
-    own_a = pltpu.make_async_copy(ra.at[z], ain.at[z], lsem.at[0])
-    own_b = pltpu.make_async_copy(rb.at[y], bin_.at[y], lsem.at[1])
-    own_p = pltpu.make_async_copy(p.at[j8], pin.at[j8], lsem.at[2])
-    for d in (own_a, own_b, own_p):
-        d.start()
-    own_a.wait()
-    for off in range(1, NZ):
-        arrive(*za, off).wait_recv()
-    for k in range(4):
-        acc = ain[0, k].astype(F32)
-        for i in range(1, NZ):
-            acc = acc + ain[i, k].astype(F32)
-        sa[k] = acc.astype(BF16)
-    ya = (sa, a2, y, 4, at_y, sa2, ra2)
-    zb = (sb, b2, z, NZ, at_z, sb2, rb2)
-    more = [send(*ya, off) for off in (2, 1, 3)]
-    for d in more:
-        d.start()
-    own_b.wait()
-    for off in range(1, 4):
-        arrive(*yb, off).wait_recv()
-    for k in range(NZ):
-        acc = bin_[0, k].astype(F32)
-        for i in range(1, 4):
-            acc = acc + bin_[i, k].astype(F32)
-        sb[k] = acc.astype(BF16)
-    last = [send(*zb, off) for off in (4, 3, 5, 2, 6, 1, 7)]
-    for d in last:
-        d.start()
-    own_sa = pltpu.make_async_copy(sa.at[y], a2.at[y], lsem.at[3])
-    own_sb = pltpu.make_async_copy(sb.at[z], b2.at[z], lsem.at[4])
-    own_sa.start()
-    own_sb.start()
-    own_sa.wait()
-    own_sb.wait()
-    for off in range(1, 4):
-        arrive(*ya, off).wait_recv()
-    for off in range(1, NZ):
-        arrive(*zb, off).wait_recv()
-    acc_a = a2[0].astype(F32)
-    for i in range(1, 4):
-        acc_a = acc_a + a2[i].astype(F32)
-    acc_b = b2[0].astype(F32)
-    for i in range(1, NZ):
-        acc_b = acc_b + b2[i].astype(F32)
-    for k in range(2):
-        rows = slice(k * 40, (k + 1) * 40)
-        full[k, :, :128] = acc_a[rows]
-        full[k, :, 128:] = acc_b[rows]
-    sib = 1 - c
-    swap = pltpu.make_async_remote_copy(
-        src_ref=full.at[sib], dst_ref=fin.at[c], send_sem=sf.at[0], recv_sem=rf.at[0],
-        device_id={"seq_2": sib}, device_id_type=MESH,
-    )
-    swap_in = pltpu.make_async_remote_copy(
-        src_ref=full.at[sib], dst_ref=fin.at[sib], send_sem=sf.at[0], recv_sem=rf.at[0],
-        device_id={"seq_2": sib}, device_id_type=MESH,
-    )
-    swap.start()
-    outs = []
-    for off in range(1, 8):
-        to = lax.rem(j8 + off, 8)
-        d = pltpu.make_async_remote_copy(
-            src_ref=full.at[to // 4, :, pl.ds(256, 128)], dst_ref=tiles.at[j8],
-            send_sem=sf.at[off], recv_sem=rf.at[off], device_id=at_j(to), device_id_type=MESH,
-        )
-        d.start()
-        outs.append(d)
-    keep = pltpu.make_async_copy(full.at[c], fin.at[c], lsem.at[5])
-    keep_t = pltpu.make_async_copy(
-        full.at[c, :, pl.ds(256, 128)], tiles.at[j8], lsem.at[6]
-    )
-    keep.start()
-    keep_t.start()
-    own_p.wait()
-    for off in range(1, 8):
-        arrive(*xp, off).wait_recv()
-
-    @pl.when((c == 1) & (x == 3))
-    def _():
-        for k in range(8):
-            pltpu.make_async_remote_copy(
-                src_ref=pb, dst_ref=pbin.at[k], send_sem=sq, recv_sem=rq.at[k],
-                device_id={"seq_2": 0}, device_id_type=MESH,
-            ).wait_recv()
-
-    keep.wait()
-    keep_t.wait()
-    swap_in.wait_recv()
-    for off in range(1, 8):
-        origin = lax.rem(j8 + 8 - off, 8)
-        pltpu.make_async_remote_copy(
-            src_ref=full.at[c, :, pl.ds(256, 128)], dst_ref=tiles.at[origin],
-            send_sem=sf.at[off], recv_sem=rf.at[off], device_id=at_j(origin),
-            device_id_type=MESH,
-        ).wait_recv()
-    for d in sends + more + last + outs + [edge, swap]:
-        d.wait_send()
-
-
-def reductions(ra, rb, p, pb):
-    dma = pltpu.SemaphoreType.DMA
-    return pl.pallas_call(
-        reduce_kernel,
-        out_shape=(
-            jax.ShapeDtypeStruct((2, 40, 384), F32),
-            jax.ShapeDtypeStruct((8, 40, 128), F32),
-            jax.ShapeDtypeStruct((8, 32, D), BF16),
-            jax.ShapeDtypeStruct((8, PRE, D), BF16),
-        ),
-        in_specs=[VM] * 4,
-        out_specs=(VM,) * 4,
+        out_specs=(VM,) * 5,
         scratch_shapes=[
-            pltpu.VMEM((NZ, 4, ROWS, 128), BF16),
-            pltpu.VMEM((4, NZ, ROWS, 256), BF16),
-            pltpu.VMEM((4, ROWS, 128), BF16),
-            pltpu.VMEM((NZ, ROWS, 256), BF16),
-            pltpu.VMEM((4, ROWS, 128), BF16),
-            pltpu.VMEM((NZ, ROWS, 256), BF16),
-            pltpu.VMEM((2, 40, 384), F32),
-            dma((7,)), dma((8,)), dma((8,)), dma((4,)), dma((4,)), dma((8,)), dma((8,)),
-            dma(()), dma((8,)), dma((4,)), dma((4,)), dma((8,)), dma((8,)), dma((8,)), dma((8,)),
+            vm(8, 32, EXT),
+            vm(4, NZ, 2, ROWS, 128), vm(2, 4, 2, ROWS, 128), vm(2, NZ, 2, ROWS, 128),
+            vm(NZ, 4, ROWS, 128), vm(2, 4, ROWS, 128), vm(2, 2, ROWS, 128),
+            vm(2, 4, ROWS, 128), vm(2, 4, ROWS, 128), vm(4, ROWS, 128), vm(4, ROWS, 128),
+            vm(NZ, 2, ROWS, 128), vm(2, 2, ROWS, 128), vm(2, 1, ROWS, 128),
+            vm(2, 2, ROWS, 128), vm(2, 2, ROWS, 128),
+            pltpu.VMEM((2, 40, 128), F32), pltpu.VMEM((2, 40, 256), F32),
+            vm(2, 4, 2, 16, D), vm(4, 2, 16, D), vm(2, 16, D), vm(PRE, D), vm(PRE, D),
+            dma((1,)), dma((8,)), dma((8,)), dma((6,)), dma((6,)), dma((8,)), dma((8,)),
+            dma((8,)), dma((8,)), dma((6,)), dma((6,)), dma(()), dma((4,)), dma((4,)), dma((4,)),
+            dma((8,)), dma((8,)), dma((3,)), dma((3,)),
         ],
         compiler_params=pltpu.CompilerParams(
-            collective_id=3, has_side_effects=True, vmem_limit_bytes=LIMIT
+            collective_id=2, has_side_effects=True, vmem_limit_bytes=LIMIT
         ),
-        name="reductions",
-    )(ra, rb, p, pb)
-
-
-def finish_kernel(fin, tiles, pin, pbin, ig_o, iw_o, mw_o, sw_o):
-    z, yh, c, x = (lax.axis_index(a) for a in SEQ_CHAN)
+        name="sums",
+    )(*args)
+
+
+def finish_kernel(tiles, fb, pown, xin, pbin, ig_o, iw_o, mw_o, sw_o):
+    c, x = lax.axis_index("seq_2"), lax.axis_index("chan")
     for k in range(2):
-        iw_o[:, k * INNER : (k + 1) * INNER] = fin[k, :, :INNER]
-        sw_o[:, k * HEADS : (k + 1) * HEADS] = fin[k, :, 352 : 352 + HEADS]
+        iw_o[:, k * INNER : k * INNER + 256] = fb[k]
+        own = tiles[k * 4 + x]
+        iw_o[:, k * INNER + 256 : (k + 1) * INNER] = own[:, :64]
+        sw_o[:, k * HEADS : (k + 1) * HEADS] = own[:, 96 : 96 + HEADS]
     rows = one_hot(iota((10, 40), 1) == iota((10, 40), 0) + 10 * x)
     for j in range(8):
         mw_o[:, j * 32 : (j + 1) * 32] = exact(rows, tiles[j])[:, 64:96]
-    acc = pin[0].astype(F32)
-    for j in range(1, 8):
-        acc = acc + pin[j].astype(F32)
-    ig_o[...] = acc.astype(BF16)
+    for h in range(2):
+        acc = pown[h].astype(F32) + xin[0, h].astype(F32) + xin[1, h].astype(F32)
+        ig_o[h * 16 : (h + 1) * 16, :] = acc.astype(BF16)
 
     @pl.when((c == 1) & (x == 3))
     def _():
-        edge = pbin[0].astype(F32)
-        for j in range(1, 8):
+        edge = pown[1].astype(F32) + xin[0, 1].astype(F32) + xin[1, 1].astype(F32)
+        for j in range(4):
             edge = edge + pbin[j].astype(F32)
-        ig_o[16:, :] = (acc[16:] + roll(edge, 0)).astype(BF16)
+        ig_o[16:, :] = edge.astype(BF16)
 
 
 def finish(*args):
@@ -803,7 +809,7 @@
             jax.ShapeDtypeStruct((10, 2 * STATE), F32),
             jax.ShapeDtypeStruct((40, 2 * HEADS), F32),
         ),
-        in_specs=[VM] * 4,
+        in_specs=[VM] * 5,
         out_specs=(VM,) * 4,
         compiler_params=pltpu.CompilerParams(vmem_limit_bytes=LIMIT),
         name="finish",
@@ -832,10 +838,8 @@
     gi, gm, ds, gmt = backward(
         xa, zi, zm, dt, cum, sr, og, st, conv_inner, conv_mixer, dlog, skip
     )
-    mixed = mix(gmt)
-    ra, rb, p, pb = products(norm, xe, gi, gm, ds, mixed, wih, mixer_weight, step_weight)
-    fin, tiles, pin, pbin = reductions(ra, rb, p, pb)
-    ig, iw, mw, sw = finish(fin, tiles, pin, pbin)
+    parts = sums(norm, xe, gi, gm, ds, gmt, wih, mixer_weight, step_weight)
+    ig, iw, mw, sw = finish(*parts)
     return ig[None], iw, mw, sw
 
 

time: 121 us -> 96.3 us (0.80)
  Pallas kernels: 117 us -> 92 us
    pallas_call x3 -> x1, Pallas kernels: 56.9 us -> 32.4 us  [sums(): pl.pallas_call(functools.partial(sums_kernel, norm), out_shape=(jax.Shape...]
where the time goes in v2:
time: 96.3 us; the launch traced here: 96 us
  Pallas kernels  92 us (96%)
  local copies, waits for them, and re-layouts  3.43 us (4%)
    pallas_call x1, Pallas kernels, sums(): pl.pallas_call(functools.partial(sums_kernel, norm), out_shape=(jax.Shape...  32.4 us
    pallas_call x1, Pallas kernels, states(): pl.pallas_call(state_kernel, out_shape=jax.ShapeDtypeStruct((n, CHUNK, ST...  25.2 us
    pallas_call x1, Pallas kernels, gather(): pl.pallas_call(gather_kernel, out_shape=(jax.ShapeDtypeStruct((EXT, D), B...  17.5 us
    pallas_call x1, Pallas kernels, forward(): pl.pallas_call(forward_kernel, out_shape=(jax.ShapeDtypeStruct((TOK, INNE...  7.52 us
    pallas_call x1, Pallas kernels, backward(): pl.pallas_call(backward_kernel, out_shape=(jax.ShapeDtypeStruct((EXT, INN...  7.02 us
    unnamed x2, local copies, waits for them, and re-layouts  3.43 us
    pallas_call x1, Pallas kernels, finish(): pl.pallas_call(finish_kernel, out_shape=(jax.ShapeDtypeStruct((32, D), BF...  2.37 us

profile of v2, /device:TPU:1, one launch (start us, length us, event | category | flops | bytes accessed | tf_op | source)
XLA Modules:
  0.0 96.0 jit_solution(9235930708706510236)
XLA Ops:
  0.6 2.0 %copy.14.ws = bf16[2560,10]{1,0:T(8,128)(2,1)} copy(bf16[2560,10]{0,1:T(8,128)(2,1)} %param.13) | data formatting | bytes 102400 | tf_op args[3]
  2.7 17.5 %gather.1 = (bf16[272,2560]{1,0:T(8,128)(2,1)}, bf16[2,128,640]{2,1,0:T(8,128)(2,1)}) custom-call(bf16[32,2560]{1,0:T(8,128)(2,1)} %bitcast.6, bf16[128,640]{1,0:T(8,128)(2,1)} %bitcast.7), custom_call_target="tpu_custom_call" | custom-call | tf_op jit(solution)/shard_map/gather/pallas_call | solution.py:209
  20.1 7.5 %forward.1 = (f32[256,320]{1,0:T(8,128)}, f32[256,320]{1,0:T(8,128)}, f32[256,256]{1,0:T(8,128)}, f32[256,128]{1,0:T(8,128)}, f32[256,128]{1,0:T(8,128)}, /*inde...) custom-call(bf16[272,2560]{1,0:T(8,128)(2,1)} %get-tuple-element.28.xe, ...), custom_call_target="tpu_custom_call" | custom-call | tf_op jit(solution)/shard_map/forward/pallas_call | solution.py:281
  27.6 25.2 %states.1.st = bf16[16,48,128]{2,1,0:T(8,128)(2,1)} custom-call(bf16[16,48,128]{2,1,0:T(8,128)(2,1)} %get-tuple-element.37.send), custom_call_target="tpu_custom_call" | custom-call | tf_op jit(solution)/shard_map/states/pallas_call | solution.py:364
  52.8 7.0 %backward.1 = (bf16[272,320]{1,0:T(8,128)(2,1)}, bf16[272,256]{1,0:T(8,128)(2,1)}, bf16[272,128]{1,0:T(8,128)(2,1)}, bf16[8,32,272]{2,1,0:T(8,128)(2,1)}) custom-call(f32[256,320]{1,0:T(8,128)} %get-tuple-element.30.xa_r, f32[256,320]{1,0:T(8,128)} %get-tuple-element.31.zi_r, f32[256,256]{1,0:T(8,128)} %get-tuple-element.32.zm_r, ...), custom_call_target="tpu_custom_call" | custom-call | tf_op jit(solution)/shard_map/backward/pallas_call | solution.py:464
  59.9 32.4 %sums.1 = (f32[8,40,128]{2,1,0:T(8,128)}, f32[2,40,256]{2,1,0:T(8,128)}, bf16[2,16,2560]{2,1,0:T(8,128)(2,1)}, bf16[2,2,16,2560]{3,2,1,0:T(8,128)(2,1)}, bf16[4,16,2560]{2,1,0:T(8,128)(2,1)}) custom-call(bf16[272,2560]{1,0:T(8,128)(2,1)} %get-tuple-element.28.xe, bf16[272,320]{1,0:T(8,128)(2,1)} %get-tuple-element.38.gi_r, ...), custom_call_target="tpu_custom_call" | custom-call | tf_op jit(solution)/shard_map/sums/pallas_call | solution.py:750
  92.3 2.4 %finish.1 = (bf16[32,2560]{1,0:T(8,128)(2,1)}, f32[40,640]{1,0:T(8,128)}, f32[10,256]{1,0:T(8,128)}, f32[40,10]{1,0:T(8,128)}) custom-call(f32[8,40,128]{2,1,0:T(8,128)} %get-tuple-element.43.tiles, f32[2,40,256]{2,1,0:T(8,128)} %get-tuple-element.44.fb, bf16[2,16,2560]{2,1,0:T(8,128)(2,1)} %get-tuple-element.45.pown, ...), custom_call_target="tpu_custom_call" | custom-call | tf_op jit(solution)/shard_map/finish/pallas_call | solution.py:804
  94.6 1.4 %copy.16 = f32[40,10]{0,1:T(8,128)} copy(f32[40,10]{1,0:T(8,128)} %get-tuple-element.55) | data formatting | bytes 3200

commit v3 on v2

--- a/solution.py
+++ b/solution.py
@@ -28,7 +28,7 @@
 DP_SEQ_CHAN = ("dp", "seq_0", "seq_1", "seq_2", "chan")
 MESH = pl.DeviceIdType.MESH
 VM = pl.BlockSpec(memory_space=pltpu.VMEM)
-LIMIT = 60 * 1024 * 1024
+LIMIT = 48 * 1024 * 1024
 
 
 def roll(v, shift):
@@ -85,27 +85,12 @@
     return k[3:4] * g + k[2:3] * roll(g, -1) + k[1:2] * roll(g, -2) + k[0:1] * roll(g, -3)
 
 
-def gather_kernel(piece, og, xe, ogx, local_sem, ssem, rsem, tsem):
+def gather_phase(xe, ogx, ssem, rsem, tsem):
     z, yh, c, x = (lax.axis_index(a) for a in SEQ_CHAN)
     right, left = lax.rem(x + 1, 4), lax.rem(x + 3, 4)
     sib = 1 - c
     q = z * 2 + yh
     nq, pq = lax.rem(q + 1, 2 * NZ), lax.rem(q + 2 * NZ - 1, 2 * NZ)
-    barrier = pltpu.get_barrier_semaphore()
-
-    def tell(**where):
-        pl.semaphore_signal(barrier, inc=1, device_id=where, device_id_type=MESH)
-
-    tell(chan=right)
-    tell(chan=left)
-    tell(seq_2=sib)
-
-    @pl.when(c == 1)
-    def _():
-        tell(seq_0=pq // 2, seq_1=lax.rem(pq, 2), chan=3)
-
-    pl.semaphore_wait(barrier, jnp.where((c == 1) & (x == 3), 7, 3))
-
     def slot(core, chan, half=None):
         base = PRE + (core * 4 + chan) * 32
         if half is None:
@@ -118,17 +103,18 @@
             device_id=where, device_id_type=MESH,
         )
 
+    mine = slot(c, x)
+    own_og = ogx.at[c]
+
     def half(h):
-        return piece.at[pl.ds(16 * h, 16), :]
-
-    own = pltpu.make_async_copy(piece, slot(c, x), local_sem.at[0])
-    own_og = pltpu.make_async_copy(og, ogx.at[c], local_sem.at[1])
+        return slot(c, x, h)
+
     r0 = copy(half(0), slot(c, x, 0), 0, chan=right)
     l1 = copy(half(1), slot(c, x, 1), 1, chan=left)
     r1 = copy(half(1), slot(c, x, 1), 2, chan=right)
     l0 = copy(half(0), slot(c, x, 0), 3, chan=left)
-    sp = copy(piece, slot(c, x), 4, seq_2=sib)
-    so = copy(og, ogx.at[c], 5, seq_2=sib)
+    sp = copy(mine, mine, 4, seq_2=sib)
+    so = copy(own_og, own_og, 5, seq_2=sib)
     for d in (r0, l1):
         d.start()
 
@@ -147,8 +133,6 @@
 
     for d in (r1, l0, sp, so):
         d.start()
-    own.start()
-    own_og.start()
     far = lax.rem(x + 2, 4)
     in_r0 = copy(half(0), slot(c, left, 0), 0, chan=right)
     in_r1 = copy(half(1), slot(c, left, 1), 2, chan=right)
@@ -179,11 +163,11 @@
     in_ll.wait_recv()
     s_far = copy(slot(c, far), slot(c, far), 11, seq_2=sib)
     s_far.start()
-    copy(piece, slot(sib, x), 4, seq_2=sib).wait_recv()
-    copy(og, ogx.at[sib], 5, seq_2=sib).wait_recv()
-    copy(piece, slot(sib, left), 9, seq_2=sib).wait_recv()
-    copy(piece, slot(sib, right), 10, seq_2=sib).wait_recv()
-    copy(piece, slot(sib, far), 11, seq_2=sib).wait_recv()
+    copy(mine, slot(sib, x), 4, seq_2=sib).wait_recv()
+    copy(own_og, ogx.at[sib], 5, seq_2=sib).wait_recv()
+    copy(mine, slot(sib, left), 9, seq_2=sib).wait_recv()
+    copy(mine, slot(sib, right), 10, seq_2=sib).wait_recv()
+    copy(mine, slot(sib, far), 11, seq_2=sib).wait_recv()
 
     @pl.when(c == 0)
     def _():
@@ -201,34 +185,8 @@
         for chan in range(4):
             tails(chan).wait_send()
 
-    own.wait()
-    own_og.wait()
-
-
-def gather(piece, og):
-    return pl.pallas_call(
-        gather_kernel,
-        out_shape=(
-            jax.ShapeDtypeStruct((EXT, D), BF16),
-            jax.ShapeDtypeStruct((2, TOK // 2, 2 * INNER), BF16),
-        ),
-        in_specs=[VM, VM],
-        out_specs=(VM, VM),
-        scratch_shapes=[
-            pltpu.SemaphoreType.DMA((2,)),
-            pltpu.SemaphoreType.DMA((13,)),
-            pltpu.SemaphoreType.DMA((13,)),
-            pltpu.SemaphoreType.DMA((4,)),
-        ],
-        compiler_params=pltpu.CompilerParams(collective_id=0, has_side_effects=True),
-        name="gather",
-    )(piece, og)
-
-
-def forward_kernel(
-    xe, ogx, wi, wm, ws, ci, cm, bias, dlog,
-    xa_o, zi_o, zm_o, dt_o, cum_o, sr_o, og_o, wih_o, send_o,
-):
+
+def forward_phase(xe, ogx, wi, wm, ws, ci, cm, bias, dlog, wih_o, send_o):
     z, yh, c = (lax.axis_index(a) for a in SEQ)
     flag = jnp.where(z * 2 + yh == 0, 0.0, 1.0).astype(F32)
     pick = head_pick(c)
@@ -242,7 +200,7 @@
 
     pi = masked(mm(xv, wih))
     pm = masked(mm(xv, wm[...]))
-    sr = exact(mm(xv, ws[...])[PRE:], pick)
+    sr = exact(mm_t(xv, ws[...])[PRE:], pick)
     zi = conv(pi, half_of(ci[...], c))[PRE:]
     zm = conv(pm, cm[...])[PRE:]
     xa = zi * jax.nn.sigmoid(zi)
@@ -268,50 +226,15 @@
         for which, v in ((0, f_loc), (1, g_loc)):
             rows = [v[h * HDIM + zz * 8 : h * HDIM + zz * 8 + 8] for h in range(HEADS)]
             send_o[zz * 2 + which] = jnp.concatenate(rows + [drow], axis=0).astype(BF16)
-    xa_o[...] = xa
-    zi_o[...] = zi
-    zm_o[...] = zm
-    dt_o[...] = dt
-    cum_o[...] = cum
-    sr_o[...] = srb
-    og_o[...] = og
-
-
-def forward(*args):
-    return pl.pallas_call(
-        forward_kernel,
-        out_shape=(
-            jax.ShapeDtypeStruct((TOK, INNER), F32),
-            jax.ShapeDtypeStruct((TOK, INNER), F32),
-            jax.ShapeDtypeStruct((TOK, 2 * STATE), F32),
-            jax.ShapeDtypeStruct((TOK, 128), F32),
-            jax.ShapeDtypeStruct((TOK, 128), F32),
-            jax.ShapeDtypeStruct((TOK, 128), F32),
-            jax.ShapeDtypeStruct((TOK, INNER), BF16),
-            jax.ShapeDtypeStruct((D, INNER), BF16),
-            jax.ShapeDtypeStruct((2 * NZ, CHUNK, STATE), BF16),
-        ),
-        in_specs=[VM] * 9,
-        out_specs=(VM,) * 9,
-        compiler_params=pltpu.CompilerParams(vmem_limit_bytes=LIMIT),
-        name="forward",
-    )(*args)
-
-
-def state_kernel(send, out, recv, back, local_sem, s1, r1, s2, r2):
+    return xa, zi, zm, dt, cum, srb, og
+
+
+def state_phases(send, out, recv, back, local_sem, s1, r1, s2, r2):
     z, yh = lax.axis_index("seq_0"), lax.axis_index("seq_1")
     n = 2 * NZ
     me = z * 2 + yh
-    barrier = pltpu.get_barrier_semaphore()
-
     def at(q):
         return {"seq_0": q // 2, "seq_1": lax.rem(q, 2)}
-
-    for off in range(1, n):
-        pl.semaphore_signal(
-            barrier, inc=1, device_id=at(lax.rem(me + off, n)), device_id_type=MESH
-        )
-    pl.semaphore_wait(barrier, n - 1)
 
     def push(src, dst, ss, rs, off):
         to = lax.rem(me + off, n)
@@ -328,69 +251,50 @@
         )
 
     first = [push(send, recv, s1, r1, off) for off in range(1, n)]
-    for d in first:
-        d.start()
-    own = pltpu.make_async_copy(send.at[me], recv.at[me], local_sem.at[0])
-    own.start()
-    own.wait()
-    for off in range(1, n):
-        pull(send, recv, s1, r1, off).wait_recv()
-    run = jnp.zeros((HEADS * 8, STATE), F32)
-    for j in range(n):
-        k = jnp.where(yh == 0, j, n - 1 - j)
-        got = recv[k].astype(F32)
-        rows = got[HEADS * 8 :]
-        rows = rows + pltpu.roll(rows, 64, 1)
-        decay = jnp.exp(rows)
-        back[k] = jnp.concatenate([run, rows], axis=0).astype(BF16)
-        wide = jnp.concatenate(
-            [jnp.broadcast_to(decay[h : h + 1], (8, STATE)) for h in range(HEADS)], axis=0
-        )
-        run = wide * run + got[: HEADS * 8]
     second = [push(back, out, s2, r2, off) for off in range(1, n)]
-    for d in second:
-        d.start()
-    own = pltpu.make_async_copy(back.at[me], out.at[me], local_sem.at[1])
-    own.start()
-    own.wait()
-    for off in range(1, n):
-        pull(back, out, s2, r2, off).wait_recv()
-    for d in first + second:
-        d.wait_send()
-
-
-def states(send):
-    n = 2 * NZ
-    return pl.pallas_call(
-        state_kernel,
-        out_shape=jax.ShapeDtypeStruct((n, CHUNK, STATE), BF16),
-        in_specs=[VM],
-        out_specs=VM,
-        scratch_shapes=[
-            pltpu.VMEM((n, CHUNK, STATE), BF16),
-            pltpu.VMEM((n, CHUNK, STATE), BF16),
-            pltpu.SemaphoreType.DMA((2,)),
-            pltpu.SemaphoreType.DMA((n,)),
-            pltpu.SemaphoreType.DMA((n,)),
-            pltpu.SemaphoreType.DMA((n,)),
-            pltpu.SemaphoreType.DMA((n,)),
-        ],
-        compiler_params=pltpu.CompilerParams(collective_id=1, has_side_effects=True),
-        name="states",
-    )(send)
-
-
-def backward_kernel(
-    xa_r, zi_r, zm_r, dt_r, cum_r, sr_r, og_r, st, ci, cm, dlog, skip,
-    gi_o, gm_o, ds_o, gmt_o,
-):
-    z, yh, c = (lax.axis_index(a) for a in SEQ)
-    flag = jnp.where(z * 2 + yh == 0, 0.0, 1.0).astype(F32)
+
+    def begin():
+        for d in first:
+            d.start()
+        own = pltpu.make_async_copy(send.at[me], recv.at[me], local_sem.at[0])
+        own.start()
+        own.wait()
+
+    def turn():
+        for off in range(1, n):
+            pull(send, recv, s1, r1, off).wait_recv()
+        run = jnp.zeros((HEADS * 8, STATE), F32)
+        for j in range(n):
+            k = jnp.where(yh == 0, j, n - 1 - j)
+            got = recv[k].astype(F32)
+            rows = got[HEADS * 8 :]
+            rows = rows + pltpu.roll(rows, 64, 1)
+            decay = jnp.exp(rows)
+            back[k] = jnp.concatenate([run, rows], axis=0).astype(BF16)
+            wide = jnp.concatenate(
+                [jnp.broadcast_to(decay[h : h + 1], (8, STATE)) for h in range(HEADS)], axis=0
+            )
+            run = wide * run + got[: HEADS * 8]
+        for d in second:
+            d.start()
+        own = pltpu.make_async_copy(back.at[me], out.at[me], local_sem.at[1])
+        own.start()
+        own.wait()
+
+    def end():
+        for off in range(1, n):
+            pull(back, out, s2, r2, off).wait_recv()
+        for d in first + second:
+            d.wait_send()
+
+    return begin, turn, end
+
+
+def local_phase(acts, dlog, skip):
+    c = lax.axis_index("seq_2")
     pick = head_pick(c)
-    ex, hs = head_expand(), head_sum()
-    xa, zi, zm = xa_r[...], zi_r[...], zm_r[...]
-    dt, cum = dt_r[...], cum_r[...]
-    og = og_r[...]
+    ex = head_expand()
+    xa, zi, zm, dt, cum, srb, og = acts
     dy = og.astype(F32)
     rate = exact(jnp.exp(dlog[...]), pick)
     skp = exact(skip[...], pick)
@@ -398,14 +302,6 @@
     ecum = exact(jnp.exp(cum), ex)
     etail = exact(jnp.exp(tot - cum), ex)
     dte = exact(dt, ex)
-
-    def collect(which):
-        blocks = [st[2 * zz + which].astype(F32) for zz in range(NZ)]
-        rows = [blocks[zz][h * 8 : h * 8 + 8] for h in range(HEADS) for zz in range(NZ)]
-        return jnp.concatenate(rows, axis=0)
-
-    h0, ge = collect(0), collect(1)
-    h0b, geb = h0.astype(BF16), ge.astype(BF16)
     sz = jax.nn.sigmoid(zm)
     ma = zm * sz
     bm, cmx = ma[:, :STATE].astype(BF16), ma[:, STATE:].astype(BF16)
@@ -424,10 +320,29 @@
         ys.append(mm(m, xdtb[:, cols]))
         us.append(t_mm(m, og[:, cols]))
         dscore = dscore + decay * mm_t(og[:, cols], xdtb[:, cols])
-    y = jnp.concatenate(ys, axis=1) + ecum * mm_t(cmx, h0b)
+    return (
+        jnp.concatenate(ys, axis=1), jnp.concatenate(us, axis=1), dscore.astype(BF16), bm, cmx, sz,
+        xdt, xdtf, dy, rate, exact(skp, ex), tot, ecum, etail, dte,
+    )
+
+
+def carried_phase(acts, local, st, ci, cm, gi_o, gm_o, ds_o, gmt_o):
+    z, yh, c = (lax.axis_index(a) for a in SEQ)
+    flag = jnp.where(z * 2 + yh == 0, 0.0, 1.0).astype(F32)
+    hs = head_sum()
+    xa, zi, zm, dt, cum, srb, og = acts
+    y_loc, u_loc, dsb, bm, cmx, sz, xdt, xdtf, dy, rate, skp, tot, ecum, etail, dte = local
+    def collect(which):
+        blocks = [st[2 * zz + which].astype(F32) for zz in range(NZ)]
+        rows = [blocks[zz][h * 8 : h * 8 + 8] for h in range(HEADS) for zz in range(NZ)]
+        return jnp.concatenate(rows, axis=0)
+
+    h0, ge = collect(0), collect(1)
+    h0b, geb = h0.astype(BF16), ge.astype(BF16)
+    y = y_loc + ecum * mm_t(cmx, h0b)
     ug = etail * mm_t(bm, geb)
-    u = jnp.concatenate(us, axis=1) + ug
-    dxa = dte * u + exact(skp, ex) * dy
+    u = u_loc + ug
+    dxa = dte * u + skp * dy
     ddt = exact(xa * u, hs)
     dcum = exact(dy * y - xdtf * u, hs)
     e_sum = jnp.sum(exact(xdtf * ug, hs), axis=0, keepdims=True)
@@ -437,8 +352,7 @@
     carry = jnp.exp(tot) * exact(hg, hs)[0:1]
     upper = one_hot(iota((TOK, TOK), 0) <= iota((TOK, TOK), 1))
     da = exact(upper, dcum) + e_sum + carry
-    dsr = (ddt - rate * da) * jax.nn.sigmoid(sr_r[...])
-    dsb = dscore.astype(BF16)
+    dsr = (ddt - rate * da) * jax.nn.sigmoid(srb)
     d_out = mm(dsb, bm) + mm((dy * ecum).astype(BF16), h0b)
     d_in = t_mm(dsb, cmx) + mm((xdt * etail).astype(BF16), geb)
     gm = jnp.concatenate([d_in, d_out], axis=1) * (sz * (1.0 + zm * (1.0 - sz)))
@@ -460,32 +374,12 @@
         gmt_o[j] = gmt[j * 32 : j * 32 + 32]
 
 
-def backward(*args):
-    return pl.pallas_call(
-        backward_kernel,
-        out_shape=(
-            jax.ShapeDtypeStruct((EXT, INNER), BF16),
-            jax.ShapeDtypeStruct((EXT, 2 * STATE), BF16),
-            jax.ShapeDtypeStruct((EXT, 128), BF16),
-            jax.ShapeDtypeStruct((8, 32, EXT), BF16),
-        ),
-        in_specs=[VM] * 12,
-        out_specs=(VM,) * 4,
-        compiler_params=pltpu.CompilerParams(vmem_limit_bytes=LIMIT),
-        name="backward",
-    )(*args)
-
-
-def rows_of(ref, lo, n):
-    return ref[lo : lo + n]
-
-
-def sums_kernel(
+def sums_phase(
     norm, xe, gi_r, gm_r, ds_r, gmt, wih, wm, ws,
     tiles, fb, pown, xin, pbin,
     mixin, rb, yhold, yin, ra, a3, a4, a1, a2, sa, ya, sb, b3, b4, b1, b2, fa, fbs, p, psib, xhold,
     pb, pbsib,
-    lsem, ms, mr, ys, yr, zs, zr, qs, qr, xs, xr, es, er, as_, ar, ts, tr, dsem, drem,
+    ms, mr, ys, yr, zs, zr, qs, qr, xs, xr, es, er, as_, ar, ts, tr, dsem, drem,
 ):
     dp = lax.axis_index("dp")
     z, yh, c, x = (lax.axis_index(a) for a in SEQ_CHAN)
@@ -494,8 +388,6 @@
     sib = 1 - c
     q = z * 2 + yh
     nq, pq = lax.rem(q + 1, 2 * NZ), lax.rem(q + 2 * NZ - 1, 2 * NZ)
-    barrier = pltpu.get_barrier_semaphore()
-
     def at_z(off):
         return {"seq_0": lax.rem(z + off + NZ, NZ)}
 
@@ -508,23 +400,6 @@
 
     def at_j(k):
         return {"seq_2": k // 4, "chan": lax.rem(k, 4)}
-
-    def tell(where):
-        pl.semaphore_signal(barrier, inc=1, device_id=where, device_id_type=MESH)
-
-    for off in (1, -1, 2, -2):
-        tell(at_z(off))
-    for off in (1, 2, 3):
-        tell(at_y(off))
-    for off in range(1, 8):
-        tell(at_j(lax.rem(j8 + off, 8)))
-
-    @pl.when((c == 1) & (x == 3))
-    def _():
-        for k in range(4):
-            tell({"seq_0": nq // 2, "seq_1": lax.rem(nq, 2), "chan": k})
-
-    pl.semaphore_wait(barrier, jnp.where(c == 1, 15, 14))
 
     def remote(src, dst, ss, rs, where):
         return pltpu.make_async_remote_copy(
@@ -618,7 +493,7 @@
     gm = gm_r[...]
     for b in range(4):
         rows = slice(b * 640, (b + 1) * 640)
-        part = mm_t(gi, wih[rows]) + mm_t(gm, wm[rows]) + mm_t(ds10, ws[rows])
+        part = mm_t(gi, wih[rows]) + mm_t(gm, wm[rows]) + mm(ds10, ws[:, rows])
         part = part.astype(BF16)
         pb[:, rows] = part[:PRE]
         for j in range(8):
@@ -741,14 +616,79 @@
         edge.wait_send()
 
 
-def sums(norm, *args):
+def whole_kernel(
+    norm,
+    piece, og, wi_h, wm_h, ws_h, ci_h, cm_h, bias_h, dlog_h, skip_h,
+    tiles, fb, pown, xin, pbin,
+    xe, ogx, wi, wm, ws, ci, cm, bias, dlog, skip, wih, send, recv, back, st, gi, gm, ds, gmt,
+    gs, gr, gt, hsem, lsem, s1, r1, s2, r2, *rest,
+):
+    dp = lax.axis_index("dp")
+    z, yh, c, x = (lax.axis_index(a) for a in SEQ_CHAN)
+    n = 2 * NZ
+    q = z * 2 + yh
+    nq, pq = lax.rem(q + 1, n), lax.rem(q + n - 1, n)
+    corner = (c == 1) & (x == 3)
+    barrier = pltpu.get_barrier_semaphore()
+
+    def tell(**where):
+        pl.semaphore_signal(barrier, inc=1, device_id=where, device_id_type=MESH)
+
+    for off in range(1, 8):
+        k = lax.rem(c * 4 + x + off, 8)
+        tell(seq_2=k // 4, chan=lax.rem(k, 4))
+    for off in (1, 3):
+        k = lax.rem(yh * 2 + dp + off, 4)
+        tell(seq_1=k // 2, dp=lax.rem(k, 2))
+    for off in range(1, n):
+        k = lax.rem(q + off, n)
+        tell(seq_0=k // 2, seq_1=lax.rem(k, 2))
+
+    @pl.when(c == 1)
+    def _():
+        tell(seq_0=pq // 2, seq_1=lax.rem(pq, 2), chan=3)
+
+    @pl.when(corner)
+    def _():
+        for k in range(4):
+            tell(seq_0=nq // 2, seq_1=lax.rem(nq, 2), chan=k)
+
+    base = pl.multiple_of(PRE + (c * 4 + x) * 32, 16)
+    loads = [pltpu.make_async_copy(piece, xe.at[pl.ds(base, 32), :], hsem.at[0])]
+    loads.append(pltpu.make_async_copy(og, ogx.at[c], hsem.at[1]))
+    pairs = ((wi_h, wi), (wm_h, wm), (ws_h, ws), (ci_h, ci), (cm_h, cm))
+    pairs += ((bias_h, bias), (dlog_h, dlog), (skip_h, skip))
+    for k, (src, dst) in enumerate(pairs):
+        loads.append(pltpu.make_async_copy(src, dst, hsem.at[2 + k]))
+    for d in loads:
+        d.start()
+    loads[0].wait()
+    loads[1].wait()
+    pl.semaphore_wait(
+        barrier, jnp.where(corner, 7 + 2 + n - 1 + 5, jnp.where(c == 1, 7 + 2 + n, 7 + 2 + n - 1))
+    )
+    gather_phase(xe, ogx, gs, gr, gt)
+    for d in loads[2:]:
+        d.wait()
+    acts = forward_phase(xe, ogx, wi, wm, ws, ci, cm, bias, dlog, wih, send)
+    begin, turn, end = state_phases(send, st, recv, back, lsem, s1, r1, s2, r2)
+    begin()
+    local = local_phase(acts, dlog, skip)
+    turn()
+    end()
+    carried_phase(acts, local, st, ci, cm, gi, gm, ds, gmt)
+    sums_phase(norm, xe, gi, gm, ds, gmt, wih, wm, ws, tiles, fb, pown, xin, pbin, *rest)
+
+
+def whole(norm, *args):
     dma = pltpu.SemaphoreType.DMA
+    n = 2 * NZ
 
     def vm(*shape):
         return pltpu.VMEM(shape, BF16)
 
     return pl.pallas_call(
-        functools.partial(sums_kernel, norm),
+        functools.partial(whole_kernel, norm),
         out_shape=(
             jax.ShapeDtypeStruct((8, 40, 128), F32),
             jax.ShapeDtypeStruct((2, 40, 256), F32),
@@ -756,9 +696,16 @@
             jax.ShapeDtypeStruct((2, 2, 16, D), BF16),
             jax.ShapeDtypeStruct((4, PRE, D), BF16),
         ),
-        in_specs=[VM] * 8,
+        in_specs=[pl.BlockSpec(memory_space=pltpu.HBM)] * 10,
         out_specs=(VM,) * 5,
         scratch_shapes=[
+            vm(EXT, D), vm(2, TOK // 2, 2 * INNER), vm(D, 2 * INNER), vm(D, 2 * STATE), vm(10, D),
+            pltpu.VMEM((4, 2 * INNER), F32), pltpu.VMEM((4, 2 * STATE), F32),
+            pltpu.VMEM((1, 10), F32), pltpu.VMEM((1, 10), F32), pltpu.VMEM((1, 10), F32),
+            vm(D, INNER), vm(n, CHUNK, STATE), vm(n, CHUNK, STATE), vm(n, CHUNK, STATE),
+            vm(n, CHUNK, STATE), vm(EXT, INNER), vm(EXT, 2 * STATE), vm(EXT, 128), vm(8, 32, EXT),
+            dma((13,)), dma((13,)), dma((4,)), dma((10,)), dma((2,)),
+            dma((n,)), dma((n,)), dma((n,)), dma((n,)),
             vm(8, 32, EXT),
             vm(4, NZ, 2, ROWS, 128), vm(2, 4, 2, ROWS, 128), vm(2, NZ, 2, ROWS, 128),
             vm(NZ, 4, ROWS, 128), vm(2, 4, ROWS, 128), vm(2, 2, ROWS, 128),
@@ -767,14 +714,14 @@
             vm(2, 2, ROWS, 128), vm(2, 2, ROWS, 128),
             pltpu.VMEM((2, 40, 128), F32), pltpu.VMEM((2, 40, 256), F32),
             vm(2, 4, 2, 16, D), vm(4, 2, 16, D), vm(2, 16, D), vm(PRE, D), vm(PRE, D),
-            dma((1,)), dma((8,)), dma((8,)), dma((6,)), dma((6,)), dma((8,)), dma((8,)),
+            dma((8,)), dma((8,)), dma((6,)), dma((6,)), dma((8,)), dma((8,)),
             dma((8,)), dma((8,)), dma((6,)), dma((6,)), dma(()), dma((4,)), dma((4,)), dma((4,)),
             dma((8,)), dma((8,)), dma((3,)), dma((3,)),
         ],
         compiler_params=pltpu.CompilerParams(
-            collective_id=2, has_side_effects=True, vmem_limit_bytes=LIMIT
+            collective_id=0, has_side_effects=True, vmem_limit_bytes=LIMIT
         ),
-        name="sums",
+        name="whole",
     )(*args)
 
 
@@ -829,16 +776,12 @@
     output_grad,
 ):
     norm = 1.0 / math.sqrt(8192)
+    stepw = step_weight.T
     bias, dlog, skip = (v.reshape(1, -1) for v in (step_bias, decay_log, skip_gain))
-    xe, ogx = gather(layer_input[0], output_grad[0])
-    xa, zi, zm, dt, cum, sr, og, wih, send = forward(
-        xe, ogx, inner_weight, mixer_weight, step_weight, conv_inner, conv_mixer, bias, dlog
+    parts = whole(
+        norm, layer_input[0], output_grad[0], inner_weight, mixer_weight, stepw, conv_inner,
+        conv_mixer, bias, dlog, skip,
     )
-    st = states(send)
-    gi, gm, ds, gmt = backward(
-        xa, zi, zm, dt, cum, sr, og, st, conv_inner, conv_mixer, dlog, skip
-    )
-    parts = sums(norm, xe, gi, gm, ds, gmt, wih, mixer_weight, step_weight)
     ig, iw, mw, sw = finish(*parts)
     return ig[None], iw, mw, sw
 

time: 96.3 us -> 84 us (0.87)
  Pallas kernels: 92 us -> 73 us
  local copies, waits for them, and re-layouts: 3.43 us -> 9.98 us
    pallas_call x5 -> x1, Pallas kernels: 89.6 us -> 72 us  [whole(): pl.pallas_call(functools.partial(whole_kernel, norm), out_shape=(jax.Shap...]
    unnamed x2 -> x21, local copies, waits for them, and re-layouts: 3.43 us -> 9.98 us
    pallas_call x1, Pallas kernels: 2.37 us -> 1.06 us  [finish(): pl.pallas_call(finish_kernel, out_shape=(jax.ShapeDtypeStruct((32, D), BF...]
where the time goes in v3:
time: 84 us; the launch traced here: 83.7 us
  Pallas kernels  73 us (87%)
  local copies, waits for them, and re-layouts  9.98 us (12%)
    pallas_call x1, Pallas kernels, whole(): pl.pallas_call(functools.partial(whole_kernel, norm), out_shape=(jax.Shap...  72 us
    unnamed x21, local copies, waits for them, and re-layouts  9.98 us

profile of v3, /device:TPU:1, one launch (start us, length us, event | category | flops | bytes accessed | tf_op | source)
XLA Modules:
  0.0 83.7 jit_solution(4769304901364928202)
XLA Ops:
  0.6 0.0 copy-start
  0.6 1.9 %copy-done = bf16[2560,640]{1,0:T(8,128)(2,1)S(1)} copy-done((bf16[2560,640]{1,0:T(8,128)(2,1)S(1)}, bf16[2560,640]{1,0:T(8,128)(2,1)}, u32[]{:S(2)}) %copy-start) | copy-done | bytes 3276824
  2.6 0.0 copy-start.1
  2.6 1.3 %copy-done.1 = bf16[2560,256]{1,0:T(8,128)(2,1)S(1)} copy-done((bf16[2560,256]{1,0:T(8,128)(2,1)S(1)}, bf16[2560,256]{1,0:T(8,128)(2,1)}, u32[]{:S(2)}) %copy-start.1) | copy-done | bytes 1310744
  3.9 0.0 copy-start.2
  3.9 0.9 %copy-done.2 = bf16[1,32,2560]{2,1,0:T(8,128)(2,1)S(1)} copy-done((bf16[1,32,2560]{2,1,0:T(8,128)(2,1)S(1)}, bf16[1,32,2560]{2,1,0:T(8,128)(2,1)}, u32[]{:S(2)}) %copy-start.2) | copy-done | bytes 163864
  4.8 0.0 copy-start.3
  4.8 0.9 %copy-done.3 = bf16[1,128,640]{2,1,0:T(8,128)(2,1)S(1)} copy-done((bf16[1,128,640]{2,1,0:T(8,128)(2,1)S(1)}, bf16[1,128,640]{2,1,0:T(8,128)(2,1)}, u32[]{:S(2)}) %copy-start.3) | copy-done | bytes 163864
  5.7 0.0 copy-start.4
  5.7 0.9 %copy-done.4 = bf16[2560,10]{0,1:T(8,128)(2,1)S(1)} copy-done((bf16[2560,10]{0,1:T(8,128)(2,1)S(1)}, bf16[2560,10]{0,1:T(8,128)(2,1)}, u32[]{:S(2)}) %copy-start.4) | copy-done | bytes 51224
  6.6 0.0 copy-start.5
  6.6 0.7 copy-done.5
  7.3 0.0 copy-start.6
  7.3 0.7 copy-done.6
  8.0 0.0 copy-start.7
  8.0 0.7 copy-done.7
  8.6 0.0 copy-start.8
  8.6 0.7 copy-done.8
  9.3 0.0 copy-start.9
  9.3 0.7 copy-done.9
  10.0 72.0 %whole.1 = (f32[8,40,128]{2,1,0:T(8,128)S(1)}, f32[2,40,256]{2,1,0:T(8,128)S(1)}, bf16[2,16,2560]{2,1,0:T(8,128)(2,1)S(1)}, bf16[2,2,16,2560]{3,2,1,0:T(8,128)(2,1)S(1)}, bf16[4,16,2560]{2,1,0:T(8,128)(2,1)S(1)}) custom-call(bf16[32,2560]{1,0:T(8,128)(2,1)S(1)} %bitcast.7, bf16[128,640]{1,0:T(8,128)(2,1)S(1)} %bitcast.8, bf16[2560,640]{1,0:T(8,128)(2,1)S(1)} %copy-done, ...), custom_call_target="tpu_custom_call" | custom-call | tf_op jit(solution)/shard_map/whole/pallas_call | solution.py:690
  81.9 1.1 %finish.1 = (bf16[32,2560]{1,0:T(8,128)(2,1)}, f32[40,640]{1,0:T(8,128)}, f32[10,256]{1,0:T(8,128)}, f32[40,10]{1,0:T(8,128)S(1)}) custom-call(f32[8,40,128]{2,1,0:T(8,128)S(1)} %get-tuple-element.13.tiles, f32[2,40,256]{2,1,0:T(8,128)S(1)} %get-tuple-element.14.fb, bf16[2,16,2560]{2,1,0:T(8,128)(2,1)S(1)} %get-tuple-element.15.pown, ...), custom_call_target="tpu_custom_call" | custom-call | tf_op jit(solution)/shard_map/finish/pallas_call | solution.py:751
  83.0 0.7 copy.14
Async XLA Ops:
  0.6 1.9 %copy-start = (bf16[2560,640]{1,0:T(8,128)(2,1)S(1)}, bf16[2560,640]{1,0:T(8,128)(2,1)}, u32[]{:S(2)}) copy-start(bf16[2560,640]{1,0:T(8,128)(2,1)} %wi_h.1) | copy-start | bytes 9830404
  2.6 1.3 %copy-start.1 = (bf16[2560,256]{1,0:T(8,128)(2,1)S(1)}, bf16[2560,256]{1,0:T(8,128)(2,1)}, u32[]{:S(2)}) copy-start(bf16[2560,256]{1,0:T(8,128)(2,1)} %wm_h.1) | copy-start | bytes 3932164
  3.9 0.9 %copy-start.2 = (bf16[1,32,2560]{2,1,0:T(8,128)(2,1)S(1)}, bf16[1,32,2560]{2,1,0:T(8,128)(2,1)}, u32[]{:S(2)}) copy-start(bf16[1,32,2560]{2,1,0:T(8,128)(2,1)} %param.10) | copy-start | bytes 491524
  4.8 0.9 %copy-start.3 = (bf16[1,128,640]{2,1,0:T(8,128)(2,1)S(1)}, bf16[1,128,640]{2,1,0:T(8,128)(2,1)}, u32[]{:S(2)}) copy-start(bf16[1,128,640]{2,1,0:T(8,128)(2,1)} %param.19) | copy-start | bytes 491524
  5.7 0.9 %copy-start.4 = (bf16[2560,10]{0,1:T(8,128)(2,1)S(1)}, bf16[2560,10]{0,1:T(8,128)(2,1)}, u32[]{:S(2)}) copy-start(bf16[2560,10]{0,1:T(8,128)(2,1)} %param.13) | copy-start | bytes 153604
  6.6 0.7 copy-start.5
  7.3 0.7 copy-start.6
  8.0 0.7 copy-start.7
  8.6 0.7 copy-start.8
  9.3 0.7 copy-start.9

commit v4 on v3

--- a/solution.py
+++ b/solution.py
@@ -28,7 +28,7 @@
 DP_SEQ_CHAN = ("dp", "seq_0", "seq_1", "seq_2", "chan")
 MESH = pl.DeviceIdType.MESH
 VM = pl.BlockSpec(memory_space=pltpu.VMEM)
-LIMIT = 48 * 1024 * 1024
+LIMIT = 62 * 1024 * 1024
 
 
 def roll(v, shift):
@@ -320,64 +320,67 @@
         ys.append(mm(m, xdtb[:, cols]))
         us.append(t_mm(m, og[:, cols]))
         dscore = dscore + decay * mm_t(og[:, cols], xdtb[:, cols])
+    dsb = dscore.astype(BF16)
+    d_out, d_in = mm(dsb, bm), t_mm(dsb, cmx)
+    yt, xt = (dy * ecum).astype(BF16), (xdt * etail).astype(BF16)
+    gate_m = sz * (1.0 + zm * (1.0 - sz))
+    si = jax.nn.sigmoid(zi)
+    gate_i = si * (1.0 + zi * (1.0 - si))
     return (
-        jnp.concatenate(ys, axis=1), jnp.concatenate(us, axis=1), dscore.astype(BF16), bm, cmx, sz,
-        xdt, xdtf, dy, rate, exact(skp, ex), tot, ecum, etail, dte,
+        jnp.concatenate(ys, axis=1), jnp.concatenate(us, axis=1), d_out, d_in, yt, xt, gate_m,
+        gate_i, bm, cmx, xdtf, dy, rate, exact(skp, ex), tot, ecum, etail, dte,
     )
 
 
-def carried_phase(acts, local, st, ci, cm, gi_o, gm_o, ds_o, gmt_o):
+def carried_phase(acts, local, st, ci, cm, gi_o, gm_o, ds_o, gmt_o, send_mix):
     z, yh, c = (lax.axis_index(a) for a in SEQ)
     flag = jnp.where(z * 2 + yh == 0, 0.0, 1.0).astype(F32)
     hs = head_sum()
-    xa, zi, zm, dt, cum, srb, og = acts
-    y_loc, u_loc, dsb, bm, cmx, sz, xdt, xdtf, dy, rate, skp, tot, ecum, etail, dte = local
+    xa, _, _, _, _, srb, _ = acts
+    (
+        y_loc, u_loc, d_out, d_in, yt, xt, gate_m, gate_i, bm, cmx, xdtf, dy, rate, skp, tot,
+        ecum, etail, dte,
+    ) = local
+    keep = jnp.where(iota((EXT, 1), 0) < PRE, flag, 1.0)
+
     def collect(which):
         blocks = [st[2 * zz + which].astype(F32) for zz in range(NZ)]
         rows = [blocks[zz][h * 8 : h * 8 + 8] for h in range(HEADS) for zz in range(NZ)]
         return jnp.concatenate(rows, axis=0)
 
+    def back(g, k):
+        g = jnp.concatenate([jnp.zeros((PRE, g.shape[1]), F32), g], axis=0)
+        return jnp.where(keep > 0.0, conv_back(g, k), 0.0).astype(BF16)
+
     h0, ge = collect(0), collect(1)
     h0b, geb = h0.astype(BF16), ge.astype(BF16)
-    y = y_loc + ecum * mm_t(cmx, h0b)
+    gm = jnp.concatenate([d_in + mm(xt, geb), d_out + mm(yt, h0b)], axis=1) * gate_m
+    gme = back(gm, cm[...])
+    gm_o[...] = gme
+    eye = one_hot(iota((EXT, EXT), 0) == iota((EXT, EXT), 1)).astype(BF16)
+    gmt = t_mm(gme, eye).astype(BF16)
+    for j in range(8):
+        gmt_o[j] = gmt[j * 32 : j * 32 + 32]
     ug = etail * mm_t(bm, geb)
     u = u_loc + ug
-    dxa = dte * u + skp * dy
+    gi_o[...] = back((dte * u + skp * dy) * gate_i, half_of(ci[...], c))
+    send_mix()
+    y = y_loc + ecum * mm_t(cmx, h0b)
     ddt = exact(xa * u, hs)
     dcum = exact(dy * y - xdtf * u, hs)
     e_sum = jnp.sum(exact(xdtf * ug, hs), axis=0, keepdims=True)
-    hg = exact(
-        jnp.ones((8, STATE), F32), (h0 * ge).T
-    )
+    hg = exact(jnp.ones((8, STATE), F32), (h0 * ge).T)
     carry = jnp.exp(tot) * exact(hg, hs)[0:1]
     upper = one_hot(iota((TOK, TOK), 0) <= iota((TOK, TOK), 1))
     da = exact(upper, dcum) + e_sum + carry
     dsr = (ddt - rate * da) * jax.nn.sigmoid(srb)
-    d_out = mm(dsb, bm) + mm((dy * ecum).astype(BF16), h0b)
-    d_in = t_mm(dsb, cmx) + mm((xdt * etail).astype(BF16), geb)
-    gm = jnp.concatenate([d_in, d_out], axis=1) * (sz * (1.0 + zm * (1.0 - sz)))
-    si = jax.nn.sigmoid(zi)
-    gi = dxa * (si * (1.0 + zi * (1.0 - si)))
-    keep = jnp.where(iota((EXT, 1), 0) < PRE, flag, 1.0)
-
-    def back(g, k):
-        g = jnp.concatenate([jnp.zeros((PRE, g.shape[1]), F32), g], axis=0)
-        return jnp.where(keep > 0.0, conv_back(g, k), 0.0).astype(BF16)
-
-    gi_o[...] = back(gi, half_of(ci[...], c))
-    gme = back(gm, cm[...])
-    gm_o[...] = gme
     ds_o[...] = jnp.concatenate([jnp.zeros((PRE, 128), F32), dsr], axis=0).astype(BF16)
-    eye = one_hot(iota((EXT, EXT), 0) == iota((EXT, EXT), 1)).astype(BF16)
-    gmt = t_mm(gme, eye).astype(BF16)
-    for j in range(8):
-        gmt_o[j] = gmt[j * 32 : j * 32 + 32]
 
 
 def sums_phase(
-    norm, xe, gi_r, gm_r, ds_r, gmt, wih, wm, ws,
-    tiles, fb, pown, xin, pbin,
-    mixin, rb, yhold, yin, ra, a3, a4, a1, a2, sa, ya, sb, b3, b4, b1, b2, fa, fbs, p, psib, xhold,
+    norm, carry_on, xe, gi_r, gm_r, ds_r, gmt, wih, wm, ws,
+    mt, fat, fb, pown, xin, pbin,
+    mixin, rb, yhold, yin, ra, a3, a4, a1, a2, sa, ya, sb, b3, b4, b1, b2, fa, mrows, fbs, p, psib, xhold,
     pb, pbsib,
     ms, mr, ys, yr, zs, zr, qs, qr, xs, xr, es, er, as_, ar, ts, tr, dsem, drem,
 ):
@@ -414,9 +417,12 @@
         pending.append(d)
         return d
 
-    for off in range(1, 8):
-        to = lax.rem(j8 + off, 8)
-        go(remote(gmt.at[to], mixin.at[off], ms.at[off], mr.at[off], at_j(to)))
+    def send_mix():
+        for off in range(1, 8):
+            to = lax.rem(j8 + off, 8)
+            go(remote(gmt.at[to], mixin.at[off], ms.at[off], mr.at[off], at_j(to)))
+
+    carry_on(send_mix)
 
     gi = gi_r[...]
     rhs = gi[:, :256]
@@ -440,54 +446,7 @@
     go(remote(rb.at[up, hi], yin.at[0, hi], ys.at[2], yr.at[2], at_y(1)))
     go(remote(rb.at[down, lo], yin.at[1, lo], ys.at[3], yr.at[3], at_y(-1)))
 
-    total = gmt[j8].astype(F32)
-    for off in range(1, 8):
-        origin = lax.rem(j8 + 8 - off, 8)
-        remote(gmt.at[origin], mixin.at[off], ms.at[off], mr.at[off], at_j(origin)).wait_recv()
-        total = total + mixin[off].astype(F32)
-    place_mix = one_hot(iota((32, 128), 1) == iota((32, 128), 0) + 64).astype(BF16)
-    place_step = one_hot(
-        (iota((128, 128), 1) == iota((128, 128), 0) + 96) & (iota((128, 128), 0) < HEADS)
-    ).astype(BF16)
     ds = ds_r[...]
-    last = t_mm(total.astype(BF16), place_mix) + mm(ds, place_step)
-    last = last + jnp.concatenate([gi[:, 256:].astype(F32), jnp.zeros((EXT, 64), F32)], axis=1)
-    last = last.astype(BF16)
-    for b in range(4):
-        r = (t_mm(xe[:, b * 640 : (b + 1) * 640], last) * norm).astype(BF16)
-        for g in range(8):
-            ra[(b % 2) * 4 + g // 2, (g % 2) * 2 + b // 2] = r[g * ROWS : (g + 1) * ROWS]
-
-    def z_first(src, n, r3, r4, r1, s, r):
-        h = n // 2
-        for k, sign in enumerate((1, -1)):
-            part = pl.ds(k * h, h)
-            dst = [lax.rem(z + sign * d + NZ, NZ) for d in range(5)]
-            go(remote(src.at[dst[4], part], r4.at[k], s.at[4 * k], r.at[4 * k], at_z(2 * sign)))
-            go(remote(src.at[dst[3]], r3.at[k], s.at[4 * k + 1], r.at[4 * k + 1], at_z(sign)))
-            go(remote(src.at[dst[1]], r1.at[k], s.at[4 * k + 2], r.at[4 * k + 2], at_z(sign)))
-
-    def z_second(src, n, r3, r4, r2, s, r):
-        h = n // 2
-        for k, sign in enumerate((1, -1)):
-            part = pl.ds(k * h, h)
-            t = lax.rem(z + 2 * sign + NZ, NZ)
-            remote(r3.at[k], r3.at[k], s.at[4 * k + 1], r.at[4 * k + 1], at_z(sign)).wait_recv()
-            remote(r4.at[k], r4.at[k], s.at[4 * k], r.at[4 * k], at_z(2 * sign)).wait_recv()
-            for i in range(n):
-                v = src[t, i].astype(F32) + r3[k, i].astype(F32)
-                if k * h <= i < (k + 1) * h:
-                    v = v + r4[k, i - k * h].astype(F32)
-                r3[k, i] = v.astype(BF16)
-            go(remote(r3.at[k], r2.at[k], s.at[4 * k + 3], r.at[4 * k + 3], at_z(2 * sign)))
-
-    def z_last(r1, r2, s, r):
-        for k, sign in enumerate((1, -1)):
-            remote(r1.at[k], r1.at[k], s.at[4 * k + 2], r.at[4 * k + 2], at_z(sign)).wait_recv()
-            remote(r2.at[k], r2.at[k], s.at[4 * k + 3], r.at[4 * k + 3], at_z(2 * sign)).wait_recv()
-
-    z_first(ra, 4, a3, a4, a1, zs, zr)
-
     pick = head_pick(c).astype(BF16)
     ds10 = mm_t(ds, pick).astype(BF16)
     gm = gm_r[...]
@@ -507,6 +466,53 @@
     def _():
         pb_out.start()
 
+    total = gmt[j8].astype(F32)
+    for off in range(1, 8):
+        origin = lax.rem(j8 + 8 - off, 8)
+        remote(gmt.at[origin], mixin.at[off], ms.at[off], mr.at[off], at_j(origin)).wait_recv()
+        total = total + mixin[off].astype(F32)
+    place_mix = one_hot(iota((32, 128), 1) == iota((32, 128), 0) + 64).astype(BF16)
+    place_step = one_hot(
+        (iota((128, 128), 1) == iota((128, 128), 0) + 96) & (iota((128, 128), 0) < HEADS)
+    ).astype(BF16)
+    last = t_mm(total.astype(BF16), place_mix) + mm(ds, place_step)
+    last = last + jnp.concatenate([gi[:, 256:].astype(F32), jnp.zeros((EXT, 64), F32)], axis=1)
+    last = last.astype(BF16)
+    for b in range(4):
+        r = (t_mm(xe[:, b * 640 : (b + 1) * 640], last) * norm).astype(BF16)
+        for g in range(8):
+            ra[(b % 2) * 4 + g // 2, (g % 2) * 2 + b // 2] = r[g * ROWS : (g + 1) * ROWS]
+
+    def z_first(src, n, r3, r4, r1, s, r):
+        h = n // 2
+        for k, sign in enumerate((1, -1)):
+            part = pl.ds(k * h, h)
+            dst = [lax.rem(z + sign * d + NZ, NZ) for d in range(5)]
+            go(remote(src.at[dst[4], part], r4.at[k], s.at[4 * k], r.at[4 * k], at_z(2 * sign)))
+            go(remote(src.at[dst[3]], r3.at[k], s.at[4 * k + 1], r.at[4 * k + 1], at_z(sign)))
+            go(remote(src.at[dst[1]], r1.at[k], s.at[4 * k + 2], r.at[4 * k + 2], at_z(sign)))
+
+    def z_second(src, n, r3, r4, r2, s, r):
+        h = n // 2
+        for k, sign in enumerate((1, -1)):
+            part = pl.ds(k * h, h)
+            t = lax.rem(z + 2 * sign + NZ, NZ)
+            remote(r3.at[k], r3.at[k], s.at[4 * k + 1], r.at[4 * k + 1], at_z(sign)).wait_recv()
+            remote(r4.at[k], r4.at[k], s.at[4 * k], r.at[4 * k], at_z(2 * sign)).wait_recv()
+            for i in range(n):
+                v = src[t, i].astype(F32) + r3[k, i].astype(F32)
+                if k * h <= i < (k + 1) * h:
+                    v = v + r4[k, i - k * h].astype(F32)
+                r3[k, i] = v.astype(BF16)
+            go(remote(r3.at[k], r2.at[k], s.at[4 * k + 3], r.at[4 * k + 3], at_z(2 * sign)))
+
+    def z_last(r1, r2, s, r):
+        for k, sign in enumerate((1, -1)):
+            remote(r1.at[k], r1.at[k], s.at[4 * k + 2], r.at[4 * k + 2], at_z(sign)).wait_recv()
+            remote(r2.at[k], r2.at[k], s.at[4 * k + 3], r.at[4 * k + 3], at_z(2 * sign)).wait_recv()
+
+    z_first(ra, 4, a3, a4, a1, zs, zr)
+
     remote(yhold.at[0], yhold.at[0], ys.at[0], yr.at[0], at_y(1)).wait_recv()
     for i in range(4):
         yhold[0, i] = (rb[up, i].astype(F32) + yhold[0, i].astype(F32)).astype(BF16)
@@ -575,10 +581,17 @@
         v = v + ya[off].astype(F32)
     fa[0] = v[:40]
     fa[1] = v[40:]
+    go(remote(fa.at[sib], fat.at[c], ts.at[0], tr.at[0], {"seq_2": sib}))
+    line = iota((128, 80), 0)
+    wanted = (line // 64) * 40 + (lax.rem(line // 16, 4)) * 10 + lax.rem(line, 16)
+    chosen = exact(one_hot((iota((128, 80), 1) == wanted) & (lax.rem(line, 16) < 10)), v)
+    for j in range(8):
+        mrows[j] = chosen[j * 16 : (j + 1) * 16]
     for off in range(1, 8):
         to = lax.rem(j8 + off, 8)
-        go(remote(fa.at[to // 4], tiles.at[j8], ts.at[off], tr.at[off], at_j(to)))
-    tiles[j8] = fa[c]
+        go(remote(mrows.at[to], mt.at[j8], ts.at[off], tr.at[off], at_j(to)))
+    fat[c] = fa[c]
+    mt[j8] = mrows[j8]
 
     z_last(b1, b2, qs, qr)
     for i in range(2):
@@ -596,7 +609,8 @@
         remote(xin.at[1, half], xin.at[1, half], xs.at[k], xr.at[k], at_x(-1)).wait_recv()
     for off in range(1, 8):
         origin = lax.rem(j8 + 8 - off, 8)
-        remote(fa.at[c], tiles.at[origin], ts.at[off], tr.at[off], at_j(origin)).wait_recv()
+        remote(mrows.at[0], mt.at[origin], ts.at[off], tr.at[off], at_j(origin)).wait_recv()
+    remote(fa.at[c], fat.at[sib], ts.at[0], tr.at[0], {"seq_2": sib}).wait_recv()
 
     @pl.when((c == 1) & (x == 3))
     def _():
@@ -619,7 +633,7 @@
 def whole_kernel(
     norm,
     piece, og, wi_h, wm_h, ws_h, ci_h, cm_h, bias_h, dlog_h, skip_h,
-    tiles, fb, pown, xin, pbin,
+    mt, fat, fb, pown, xin, pbin,
     xe, ogx, wi, wm, ws, ci, cm, bias, dlog, skip, wih, send, recv, back, st, gi, gm, ds, gmt,
     gs, gr, gt, hsem, lsem, s1, r1, s2, r2, *rest,
 ):
@@ -676,8 +690,13 @@
     local = local_phase(acts, dlog, skip)
     turn()
     end()
-    carried_phase(acts, local, st, ci, cm, gi, gm, ds, gmt)
-    sums_phase(norm, xe, gi, gm, ds, gmt, wih, wm, ws, tiles, fb, pown, xin, pbin, *rest)
+
+    def carry_on(send_mix):
+        carried_phase(acts, local, st, ci, cm, gi, gm, ds, gmt, send_mix)
+
+    sums_phase(
+        norm, carry_on, xe, gi, gm, ds, gmt, wih, wm, ws, mt, fat, fb, pown, xin, pbin, *rest
+    )
 
 
 def whole(norm, *args):
@@ -690,14 +709,15 @@
     return pl.pallas_call(
         functools.partial(whole_kernel, norm),
         out_shape=(
-            jax.ShapeDtypeStruct((8, 40, 128), F32),
+            jax.ShapeDtypeStruct((8, 16, 128), F32),
+            jax.ShapeDtypeStruct((2, 40, 128), F32),
             jax.ShapeDtypeStruct((2, 40, 256), F32),
             jax.ShapeDtypeStruct((2, 16, D), BF16),
             jax.ShapeDtypeStruct((2, 2, 16, D), BF16),
             jax.ShapeDtypeStruct((4, PRE, D), BF16),
         ),
         in_specs=[pl.BlockSpec(memory_space=pltpu.HBM)] * 10,
-        out_specs=(VM,) * 5,
+        out_specs=(VM,) * 6,
         scratch_shapes=[
             vm(EXT, D), vm(2, TOK // 2, 2 * INNER), vm(D, 2 * INNER), vm(D, 2 * STATE), vm(10, D),
             pltpu.VMEM((4, 2 * INNER), F32), pltpu.VMEM((4, 2 * STATE), F32),
@@ -712,7 +732,8 @@
             vm(2, 4, ROWS, 128), vm(2, 4, ROWS, 128), vm(4, ROWS, 128), vm(4, ROWS, 128),
             vm(NZ, 2, ROWS, 128), vm(2, 2, ROWS, 128), vm(2, 1, ROWS, 128),
             vm(2, 2, ROWS, 128), vm(2, 2, ROWS, 128),
-            pltpu.VMEM((2, 40, 128), F32), pltpu.VMEM((2, 40, 256), F32),
+            pltpu.VMEM((2, 40, 128), F32), pltpu.VMEM((8, 16, 128), F32),
+            pltpu.VMEM((2, 40, 256), F32),
             vm(2, 4, 2, 16, D), vm(4, 2, 16, D), vm(2, 16, D), vm(PRE, D), vm(PRE, D),
             dma((8,)), dma((8,)), dma((6,)), dma((6,)), dma((8,)), dma((8,)),
             dma((8,)), dma((8,)), dma((6,)), dma((6,)), dma(()), dma((4,)), dma((4,)), dma((4,)),
@@ -725,16 +746,19 @@
     )(*args)
 
 
-def finish_kernel(tiles, fb, pown, xin, pbin, ig_o, iw_o, mw_o, sw_o):
+def finish_kernel(mt, fat, fb, pown, xin, pbin, ig_o, iw_o, mw_o, sw_o):
     c, x = lax.axis_index("seq_2"), lax.axis_index("chan")
     for k in range(2):
         iw_o[:, k * INNER : k * INNER + 256] = fb[k]
-        own = tiles[k * 4 + x]
+        own = fat[k]
         iw_o[:, k * INNER + 256 : (k + 1) * INNER] = own[:, :64]
-        sw_o[:, k * HEADS : (k + 1) * HEADS] = own[:, 96 : 96 + HEADS]
-    rows = one_hot(iota((10, 40), 1) == iota((10, 40), 0) + 10 * x)
+        pick = one_hot(iota((HEADS, 128), 1) == iota((HEADS, 128), 0) + 96)
+        sw_o[k * HEADS : (k + 1) * HEADS, :] = lax.dot_general(
+            pick, own, (((1,), (1,)), ((), ())), preferred_element_type=F32,
+            precision=lax.Precision.HIGHEST,
+        )
     for j in range(8):
-        mw_o[:, j * 32 : (j + 1) * 32] = exact(rows, tiles[j])[:, 64:96]
+        mw_o[:, j * 32 : (j + 1) * 32] = mt[j, :10, 64:96]
     for h in range(2):
         acc = pown[h].astype(F32) + xin[0, h].astype(F32) + xin[1, h].astype(F32)
         ig_o[h * 16 : (h + 1) * 16, :] = acc.astype(BF16)
@@ -754,9 +778,9 @@
             jax.ShapeDtypeStruct((32, D), BF16),
             jax.ShapeDtypeStruct((40, 2 * INNER), F32),
             jax.ShapeDtypeStruct((10, 2 * STATE), F32),
-            jax.ShapeDtypeStruct((40, 2 * HEADS), F32),
+            jax.ShapeDtypeStruct((2 * HEADS, 40), F32),
         ),
-        in_specs=[VM] * 5,
+        in_specs=[VM] * 6,
         out_specs=(VM,) * 4,
         compiler_params=pltpu.CompilerParams(vmem_limit_bytes=LIMIT),
         name="finish",
@@ -783,7 +807,7 @@
         conv_mixer, bias, dlog, skip,
     )
     ig, iw, mw, sw = finish(*parts)
-    return ig[None], iw, mw, sw
+    return ig[None], iw, mw, sw.T
 
 
 def solution(mesh):

time: 84 us -> 75.9 us (0.904)
  local copies, waits for them, and re-layouts: 9.98 us -> 0 us
  Pallas kernels: 73 us -> 75.2 us
    unnamed x21 -> x0, local copies, waits for them, and re-layouts: 9.98 us -> none
    pallas_call x1, Pallas kernels: 1.06 us -> 2.2 us  [finish(): pl.pallas_call(finish_kernel, out_shape=(jax.ShapeDtypeStruct((32, D), BF...]
    pallas_call x1, Pallas kernels: 72 us -> 73 us  [whole(): pl.pallas_call(functools.partial(whole_kernel, norm), out_shape=(jax.Shap...]
where the time goes in v4:
time: 75.9 us; the launch traced here: 75.8 us
  Pallas kernels  75.2 us (99%)
    pallas_call x1, Pallas kernels, whole(): pl.pallas_call(functools.partial(whole_kernel, norm), out_shape=(jax.Shap...  73 us
    pallas_call x1, Pallas kernels, finish(): pl.pallas_call(finish_kernel, out_shape=(jax.ShapeDtypeStruct((32, D), BF...  2.2 us

profile of v4, /device:TPU:1, one launch (start us, length us, event | category | flops | bytes accessed | tf_op | source)
XLA Modules:
  0.0 75.8 jit_solution(5550748243133266195)
XLA Ops:
  0.6 73.0 %whole.1 = (f32[8,16,128]{2,1,0:T(8,128)}, f32[2,40,128]{2,1,0:T(8,128)}, f32[2,40,256]{2,1,0:T(8,128)}, bf16[2,16,2560]{2,1,0:T(8,128)(2,1)}, bf16[2,2,16,2560]...) custom-call(bf16[32,2560]{1,0:T(8,128)(2,1)} %bitcast.8, bf16[128,640]{1,0:T(8,128)(2,1)} %bitcast.9, ...), custom_call_target="tpu_custom_call" | custom-call | tf_op jit(solution)/shard_map/whole/pallas_call | solution.py:709
  73.6 2.2 %finish.1 = (bf16[32,2560]{1,0:T(8,128)(2,1)}, f32[40,640]{1,0:T(8,128)}, f32[10,256]{1,0:T(8,128)}, f32[10,40]{1,0:T(8,128)}) custom-call(f32[8,16,128]{2,1,0:T(8,128)} %get-tuple-element.14.mt, f32[2,40,128]{2,1,0:T(8,128)} %get-tuple-element.15.fat, f32[2,40,256]{2,1,0:T(8,128)} %get-tuple-element.16.fb, bf16[2,16,2560]{2,1,0:T(8,128)(2,1)} %get-tuple-element.17.pown, ...), custom_call_target="tpu_custom_call" | custom-call | tf_op jit(solution)/shard_map/finish/pallas_call | solution.py:775

commit v5 on v4

--- a/solution.py
+++ b/solution.py
@@ -250,8 +250,9 @@
             recv_sem=rs.at[off], device_id=at(origin), device_id_type=MESH,
         )
 
-    first = [push(send, recv, s1, r1, off) for off in range(1, n)]
-    second = [push(back, out, s2, r2, off) for off in range(1, n)]
+    order = sorted(range(1, n), key=lambda off: -min(off, n - off))
+    first = [push(send, recv, s1, r1, off) for off in order]
+    second = [push(back, out, s2, r2, off) for off in order]
 
     def begin():
         for d in first:
@@ -332,7 +333,7 @@
     )
 
 
-def carried_phase(acts, local, st, ci, cm, gi_o, gm_o, ds_o, gmt_o, send_mix):
+def carried_phase(acts, local, st, ci, cm, gi_o, gm_o, ds_o, gmt_o):
     z, yh, c = (lax.axis_index(a) for a in SEQ)
     flag = jnp.where(z * 2 + yh == 0, 0.0, 1.0).astype(F32)
     hs = head_sum()
@@ -354,32 +355,37 @@
 
     h0, ge = collect(0), collect(1)
     h0b, geb = h0.astype(BF16), ge.astype(BF16)
-    gm = jnp.concatenate([d_in + mm(xt, geb), d_out + mm(yt, h0b)], axis=1) * gate_m
-    gme = back(gm, cm[...])
-    gm_o[...] = gme
-    eye = one_hot(iota((EXT, EXT), 0) == iota((EXT, EXT), 1)).astype(BF16)
-    gmt = t_mm(gme, eye).astype(BF16)
-    for j in range(8):
-        gmt_o[j] = gmt[j * 32 : j * 32 + 32]
     ug = etail * mm_t(bm, geb)
     u = u_loc + ug
     gi_o[...] = back((dte * u + skp * dy) * gate_i, half_of(ci[...], c))
-    send_mix()
-    y = y_loc + ecum * mm_t(cmx, h0b)
-    ddt = exact(xa * u, hs)
-    dcum = exact(dy * y - xdtf * u, hs)
-    e_sum = jnp.sum(exact(xdtf * ug, hs), axis=0, keepdims=True)
-    hg = exact(jnp.ones((8, STATE), F32), (h0 * ge).T)
-    carry = jnp.exp(tot) * exact(hg, hs)[0:1]
-    upper = one_hot(iota((TOK, TOK), 0) <= iota((TOK, TOK), 1))
-    da = exact(upper, dcum) + e_sum + carry
-    dsr = (ddt - rate * da) * jax.nn.sigmoid(srb)
-    ds_o[...] = jnp.concatenate([jnp.zeros((PRE, 128), F32), dsr], axis=0).astype(BF16)
+
+    def mixing():
+        gm = jnp.concatenate([d_in + mm(xt, geb), d_out + mm(yt, h0b)], axis=1) * gate_m
+        gme = back(gm, cm[...])
+        gm_o[...] = gme
+        eye = one_hot(iota((EXT, EXT), 0) == iota((EXT, EXT), 1)).astype(BF16)
+        gmt = t_mm(gme, eye).astype(BF16)
+        for j in range(8):
+            gmt_o[j] = gmt[j * 32 : j * 32 + 32]
+
+    def stepping():
+        y = y_loc + ecum * mm_t(cmx, h0b)
+        ddt = exact(xa * u, hs)
+        dcum = exact(dy * y - xdtf * u, hs)
+        e_sum = jnp.sum(exact(xdtf * ug, hs), axis=0, keepdims=True)
+        hg = exact(jnp.ones((8, STATE), F32), (h0 * ge).T)
+        carry = jnp.exp(tot) * exact(hg, hs)[0:1]
+        upper = one_hot(iota((TOK, TOK), 0) <= iota((TOK, TOK), 1))
+        da = exact(upper, dcum) + e_sum + carry
+        dsr = (ddt - rate * da) * jax.nn.sigmoid(srb)
+        ds_o[...] = jnp.concatenate([jnp.zeros((PRE, 128), F32), dsr], axis=0).astype(BF16)
+
+    return mixing, stepping
 
 
 def sums_phase(
-    norm, carry_on, xe, gi_r, gm_r, ds_r, gmt, wih, wm, ws,
-    mt, fat, fb, pown, xin, pbin,
+    norm, later, xe, gi_r, gm_r, ds_r, gmt, wih, wm, ws,
+    mt, fat, fb, ig, xin, pbin,
     mixin, rb, yhold, yin, ra, a3, a4, a1, a2, sa, ya, sb, b3, b4, b1, b2, fa, mrows, fbs, p, psib, xhold,
     pb, pbsib,
     ms, mr, ys, yr, zs, zr, qs, qr, xs, xr, es, er, as_, ar, ts, tr, dsem, drem,
@@ -422,29 +428,33 @@
             to = lax.rem(j8 + off, 8)
             go(remote(gmt.at[to], mixin.at[off], ms.at[off], mr.at[off], at_j(to)))
 
-    carry_on(send_mix)
+    mixing, stepping = later
 
     gi = gi_r[...]
     rhs = gi[:, :256]
 
-    def inner_rows(side):
-        for zhi in range(2):
-            base = pl.multiple_of(side * 1280 + zhi * 640, 128)
-            r = (t_mm(xe[:, pl.ds(base, 640)], rhs) * norm).astype(BF16)
-            for g in range(8):
-                for k in range(2):
-                    rb[(g % 2) * 2 + side, zhi * 4 + g // 2, k] = r[
-                        g * ROWS : (g + 1) * ROWS, k * 128 : (k + 1) * 128
-                    ]
+    def inner_rows(side, zhi):
+        base = pl.multiple_of(side * 1280 + zhi * 640, 128)
+        r = (t_mm(xe[:, pl.ds(base, 640)], rhs) * norm).astype(BF16)
+        for g in range(8):
+            for k in range(2):
+                rb[(g % 2) * 2 + side, zhi * 4 + g // 2, k] = r[
+                    g * ROWS : (g + 1) * ROWS, k * 128 : (k + 1) * 128
+                ]
 
     up, down, far = lax.rem(y + 1, 4), lax.rem(y + 3, 4), lax.rem(y + 2, 4)
     lo, hi = pl.ds(0, 4), pl.ds(4, 4)
-    inner_rows(dp)
+    inner_rows(dp, 0)
     go(remote(rb.at[far, lo], yhold.at[0], ys.at[0], yr.at[0], at_y(1)))
+    inner_rows(dp, 1)
     go(remote(rb.at[far, hi], yhold.at[1], ys.at[1], yr.at[1], at_y(-1)))
-    inner_rows(1 - dp)
+    inner_rows(1 - dp, 1)
     go(remote(rb.at[up, hi], yin.at[0, hi], ys.at[2], yr.at[2], at_y(1)))
+    inner_rows(1 - dp, 0)
     go(remote(rb.at[down, lo], yin.at[1, lo], ys.at[3], yr.at[3], at_y(-1)))
+    mixing()
+    send_mix()
+    stepping()
 
     ds = ds_r[...]
     pick = head_pick(c).astype(BF16)
@@ -571,7 +581,6 @@
     remote(xhold.at[1], xhold.at[1], xs.at[1], xr.at[1], at_x(-1)).wait_recv()
     xhold[1] = (psib[xd, 1].astype(F32) + xhold[1].astype(F32)).astype(BF16)
     go(remote(xhold.at[1], xin.at[1, 1], xs.at[5], xr.at[5], at_x(-1)))
-    pown[...] = psib[x]
 
     z_second(sb, 2, b3, b4, b2, qs, qr)
 
@@ -593,6 +602,22 @@
     fat[c] = fa[c]
     mt[j8] = mrows[j8]
 
+    for k, half in ((2, 1), (4, 0)):
+        remote(xin.at[0, half], xin.at[0, half], xs.at[k], xr.at[k], at_x(1)).wait_recv()
+    for k, half in ((3, 0), (5, 1)):
+        remote(xin.at[1, half], xin.at[1, half], xs.at[k], xr.at[k], at_x(-1)).wait_recv()
+    for h in range(2):
+        v = psib[x, h].astype(F32) + xin[0, h].astype(F32) + xin[1, h].astype(F32)
+        ig[h * 16 : (h + 1) * 16, :] = v.astype(BF16)
+
+    @pl.when((c == 1) & (x == 3))
+    def _():
+        v = psib[x, 1].astype(F32) + xin[0, 1].astype(F32) + xin[1, 1].astype(F32)
+        for k in range(4):
+            remote(pbsib, pbin.at[k], es, er.at[k], {"chan": 0}).wait_recv()
+            v = v + pbin[k].astype(F32)
+        ig[16:, :] = v.astype(BF16)
+
     z_last(b1, b2, qs, qr)
     for i in range(2):
         v = sb[z, i].astype(F32)
@@ -603,20 +628,11 @@
     go(remote(fbs.at[sib], fb.at[c], dsem.at[2], drem.at[2], {"seq_2": sib}))
     fb[c] = fbs[c]
 
-    for k, half in ((2, 1), (4, 0)):
-        remote(xin.at[0, half], xin.at[0, half], xs.at[k], xr.at[k], at_x(1)).wait_recv()
-    for k, half in ((3, 0), (5, 1)):
-        remote(xin.at[1, half], xin.at[1, half], xs.at[k], xr.at[k], at_x(-1)).wait_recv()
     for off in range(1, 8):
         origin = lax.rem(j8 + 8 - off, 8)
         remote(mrows.at[0], mt.at[origin], ts.at[off], tr.at[off], at_j(origin)).wait_recv()
     remote(fa.at[c], fat.at[sib], ts.at[0], tr.at[0], {"seq_2": sib}).wait_recv()
 
-    @pl.when((c == 1) & (x == 3))
-    def _():
-        for k in range(4):
-            remote(pbsib, pbin.at[k], es, er.at[k], {"chan": 0}).wait_recv()
-
     remote(fbs.at[c], fb.at[sib], dsem.at[2], drem.at[2], {"seq_2": sib}).wait_recv()
     for d in pending:
         d.wait_send()
@@ -633,7 +649,7 @@
 def whole_kernel(
     norm,
     piece, og, wi_h, wm_h, ws_h, ci_h, cm_h, bias_h, dlog_h, skip_h,
-    mt, fat, fb, pown, xin, pbin,
+    mt, fat, fb, ig,
     xe, ogx, wi, wm, ws, ci, cm, bias, dlog, skip, wih, send, recv, back, st, gi, gm, ds, gmt,
     gs, gr, gt, hsem, lsem, s1, r1, s2, r2, *rest,
 ):
@@ -690,12 +706,9 @@
     local = local_phase(acts, dlog, skip)
     turn()
     end()
-
-    def carry_on(send_mix):
-        carried_phase(acts, local, st, ci, cm, gi, gm, ds, gmt, send_mix)
-
+    later = carried_phase(acts, local, st, ci, cm, gi, gm, ds, gmt)
     sums_phase(
-        norm, carry_on, xe, gi, gm, ds, gmt, wih, wm, ws, mt, fat, fb, pown, xin, pbin, *rest
+        norm, later, xe, gi, gm, ds, gmt, wih, wm, ws, mt, fat, fb, ig, *rest
     )
 
 
@@ -712,12 +725,10 @@
             jax.ShapeDtypeStruct((8, 16, 128), F32),
             jax.ShapeDtypeStruct((2, 40, 128), F32),
             jax.ShapeDtypeStruct((2, 40, 256), F32),
-            jax.ShapeDtypeStruct((2, 16, D), BF16),
-            jax.ShapeDtypeStruct((2, 2, 16, D), BF16),
-            jax.ShapeDtypeStruct((4, PRE, D), BF16),
+            jax.ShapeDtypeStruct((32, D), BF16),
         ),
         in_specs=[pl.BlockSpec(memory_space=pltpu.HBM)] * 10,
-        out_specs=(VM,) * 6,
+        out_specs=(VM,) * 4,
         scratch_shapes=[
             vm(EXT, D), vm(2, TOK // 2, 2 * INNER), vm(D, 2 * INNER), vm(D, 2 * STATE), vm(10, D),
             pltpu.VMEM((4, 2 * INNER), F32), pltpu.VMEM((4, 2 * STATE), F32),
@@ -726,7 +737,7 @@
             vm(n, CHUNK, STATE), vm(EXT, INNER), vm(EXT, 2 * STATE), vm(EXT, 128), vm(8, 32, EXT),
             dma((13,)), dma((13,)), dma((4,)), dma((10,)), dma((2,)),
             dma((n,)), dma((n,)), dma((n,)), dma((n,)),
-            vm(8, 32, EXT),
+            vm(2, 2, 16, D), vm(4, PRE, D), vm(8, 32, EXT),
             vm(4, NZ, 2, ROWS, 128), vm(2, 4, 2, ROWS, 128), vm(2, NZ, 2, ROWS, 128),
             vm(NZ, 4, ROWS, 128), vm(2, 4, ROWS, 128), vm(2, 2, ROWS, 128),
             vm(2, 4, ROWS, 128), vm(2, 4, ROWS, 128), vm(4, ROWS, 128), vm(4, ROWS, 128),
@@ -746,29 +757,19 @@
     )(*args)
 
 
-def finish_kernel(mt, fat, fb, pown, xin, pbin, ig_o, iw_o, mw_o, sw_o):
-    c, x = lax.axis_index("seq_2"), lax.axis_index("chan")
+def finish_kernel(mt, fat, fb, ig, ig_o, iw_o, mw_o, sw_o):
+    pick = one_hot(iota((HEADS, 128), 1) == iota((HEADS, 128), 0) + 96)
     for k in range(2):
         iw_o[:, k * INNER : k * INNER + 256] = fb[k]
         own = fat[k]
         iw_o[:, k * INNER + 256 : (k + 1) * INNER] = own[:, :64]
-        pick = one_hot(iota((HEADS, 128), 1) == iota((HEADS, 128), 0) + 96)
         sw_o[k * HEADS : (k + 1) * HEADS, :] = lax.dot_general(
             pick, own, (((1,), (1,)), ((), ())), preferred_element_type=F32,
             precision=lax.Precision.HIGHEST,
         )
     for j in range(8):
         mw_o[:, j * 32 : (j + 1) * 32] = mt[j, :10, 64:96]
-    for h in range(2):
-        acc = pown[h].astype(F32) + xin[0, h].astype(F32) + xin[1, h].astype(F32)
-        ig_o[h * 16 : (h + 1) * 16, :] = acc.astype(BF16)
-
-    @pl.when((c == 1) & (x == 3))
-    def _():
-        edge = pown[1].astype(F32) + xin[0, 1].astype(F32) + xin[1, 1].astype(F32)
-        for j in range(4):
-            edge = edge + pbin[j].astype(F32)
-        ig_o[16:, :] = edge.astype(BF16)
+    ig_o[...] = ig[...]
 
 
 def finish(*args):
@@ -780,7 +781,7 @@
             jax.ShapeDtypeStruct((10, 2 * STATE), F32),
             jax.ShapeDtypeStruct((2 * HEADS, 40), F32),
         ),
-        in_specs=[VM] * 6,
+        in_specs=[VM] * 4,
         out_specs=(VM,) * 4,
         compiler_params=pltpu.CompilerParams(vmem_limit_bytes=LIMIT),
         name="finish",

time: 75.9 us -> 75.8 us (level)
  no operation moved by 1% of the time
where the time goes in v5:
time: 75.8 us; the launch traced here: 75.7 us
  Pallas kernels  75.1 us (99%)
    pallas_call x1, Pallas kernels, whole(): pl.pallas_call(functools.partial(whole_kernel, norm), out_shape=(jax.Shap...  73.3 us
    pallas_call x1, Pallas kernels, finish(): pl.pallas_call(finish_kernel, out_shape=(jax.ShapeDtypeStruct((32, D), BF...  1.82 us

profile of v5, /device:TPU:1, one launch (start us, length us, event | category | flops | bytes accessed | tf_op | source)
XLA Modules:
  0.0 75.7 jit_solution(17097010395285092437)
XLA Ops:
  0.6 73.3 %whole.1 = (f32[8,16,128]{2,1,0:T(8,128)}, f32[2,40,128]{2,1,0:T(8,128)}, f32[2,40,256]{2,1,0:T(8,128)}, bf16[32,2560]{1,0:T(8,128)(2,1)}) custom-call(bf16[32,2560]{1,0:T(8,128)(2,1)} %bitcast.8, bf16[128,640]{1,0:T(8,128)(2,1)} %bitcast.9, bf16[2560,640]{1,0:T(8,128)(2,1)} %wi_h.1, bf16[2560,256]{1,0:T(8,128)(2,1)} %wm_h.1, bf16[10,2560]{1,0:T(8,128)(2,1)} %bitcast.10, ...), custom_call_target="tpu_custom_call" | custom-call | tf_op jit(solution)/shard_map/whole/pallas_call | solution.py:722
  73.9 1.8 %finish.1 = (bf16[32,2560]{1,0:T(8,128)(2,1)}, f32[40,640]{1,0:T(8,128)}, f32[10,256]{1,0:T(8,128)}, f32[10,40]{1,0:T(8,128)}) custom-call(f32[8,16,128]{2,1,0:T(8,128)} %get-tuple-element.12.mt, f32[2,40,128]{2,1,0:T(8,128)} %get-tuple-element.13.fat, f32[2,40,256]{2,1,0:T(8,128)} %get-tuple-element.14.fb, bf16[32,2560]{1,0:T(8,128)(2,1)} %get-tuple-element.15.ig), custom_call_target="tpu_custom_call" | custom-call | tf_op jit(solution)/shard_map/finish/pallas_call | solution.py:776

commit v6 on v5

--- a/solution.py
+++ b/solution.py
@@ -271,7 +271,7 @@
             rows = got[HEADS * 8 :]
             rows = rows + pltpu.roll(rows, 64, 1)
             decay = jnp.exp(rows)
-            back[k] = jnp.concatenate([run, rows], axis=0).astype(BF16)
+            back[k] = run.astype(BF16)
             wide = jnp.concatenate(
                 [jnp.broadcast_to(decay[h : h + 1], (8, STATE)) for h in range(HEADS)], axis=0
             )
@@ -361,12 +361,19 @@
 
     def mixing():
         gm = jnp.concatenate([d_in + mm(xt, geb), d_out + mm(yt, h0b)], axis=1) * gate_m
-        gme = back(gm, cm[...])
-        gm_o[...] = gme
-        eye = one_hot(iota((EXT, EXT), 0) == iota((EXT, EXT), 1)).astype(BF16)
-        gmt = t_mm(gme, eye).astype(BF16)
+        gm_o[...] = back(gm, cm[...])
+        eye = one_hot(iota((TOK, TOK), 0) == iota((TOK, TOK), 1)).astype(BF16)
+        gmt = t_mm(gm.astype(BF16), eye).astype(BF16)
         for j in range(8):
             gmt_o[j] = gmt[j * 32 : j * 32 + 32]
+
+    def mixed(total):
+        j8 = c * 4 + lax.axis_index("chan")
+        place = one_hot(iota((32, 128), 1) == iota((32, 128), 0) + 64).astype(BF16)
+        cols = one_hot(iota((2 * STATE, 128), 0) == j8 * 32 + iota((2 * STATE, 128), 1) - 64)
+        lanes = iota((2 * STATE, 128), 1)
+        cols = jnp.where((lanes >= 64) & (lanes < 96), cols, 0.0)
+        return back(t_mm(total.astype(BF16), place), exact(cm[...], cols))
 
     def stepping():
         y = y_loc + ecum * mm_t(cmx, h0b)
@@ -380,11 +387,11 @@
         dsr = (ddt - rate * da) * jax.nn.sigmoid(srb)
         ds_o[...] = jnp.concatenate([jnp.zeros((PRE, 128), F32), dsr], axis=0).astype(BF16)
 
-    return mixing, stepping
+    return mixing, mixed, stepping
 
 
 def sums_phase(
-    norm, later, xe, gi_r, gm_r, ds_r, gmt, wih, wm, ws,
+    norm, later, xet, gi_r, gm_r, ds_r, gmt, wih, wm, ws,
     mt, fat, fb, ig, xin, pbin,
     mixin, rb, yhold, yin, ra, a3, a4, a1, a2, sa, ya, sb, b3, b4, b1, b2, fa, mrows, fbs, p, psib, xhold,
     pb, pbsib,
@@ -428,33 +435,81 @@
             to = lax.rem(j8 + off, 8)
             go(remote(gmt.at[to], mixin.at[off], ms.at[off], mr.at[off], at_j(to)))
 
-    mixing, stepping = later
+    mixing, mixed, stepping = later
 
     gi = gi_r[...]
     rhs = gi[:, :256]
 
     def inner_rows(side, zhi):
         base = pl.multiple_of(side * 1280 + zhi * 640, 128)
-        r = (t_mm(xe[:, pl.ds(base, 640)], rhs) * norm).astype(BF16)
+        r = (mm(xet[pl.ds(base, 640), :], rhs) * norm).astype(BF16)
         for g in range(8):
             for k in range(2):
-                rb[(g % 2) * 2 + side, zhi * 4 + g // 2, k] = r[
+                rb[k, (g % 2) * 2 + side, zhi * 4 + g // 2] = r[
                     g * ROWS : (g + 1) * ROWS, k * 128 : (k + 1) * 128
                 ]
 
     up, down, far = lax.rem(y + 1, 4), lax.rem(y + 3, 4), lax.rem(y + 2, 4)
     lo, hi = pl.ds(0, 4), pl.ds(4, 4)
+
+    def hold(k, sign):
+        i = 0 if sign == 1 else 1
+        part = lo if sign == 1 else hi
+        return remote(
+            rb.at[k, far, part], yhold.at[k, i], ys.at[6 * k + i], yr.at[6 * k + i], at_y(sign)
+        )
+
+    def plain(k, sign):
+        i = 0 if sign == 1 else 1
+        to, part = (up, hi) if sign == 1 else (down, lo)
+        return remote(
+            rb.at[k, to, part], yin.at[k, i, part], ys.at[6 * k + 2 + i], yr.at[6 * k + 2 + i],
+            at_y(sign),
+        )
+
+    def second(k, sign):
+        i = 0 if sign == 1 else 1
+        part = lo if sign == 1 else hi
+        return remote(
+            yhold.at[k, i], yin.at[k, i, part], ys.at[6 * k + 4 + i], yr.at[6 * k + 4 + i],
+            at_y(sign),
+        )
+
+    def ring_on(k):
+        for sign, to, first in ((1, up, 0), (-1, down, 4)):
+            i = 0 if sign == 1 else 1
+            hold(k, sign).wait_recv()
+            for e in range(4):
+                v = rb[k, to, first + e].astype(F32) + yhold[k, i, e].astype(F32)
+                yhold[k, i, e] = v.astype(BF16)
+            go(second(k, sign))
+
+    def ring_end(k):
+        for sign in (1, -1):
+            plain(k, sign).wait_recv()
+            second(k, sign).wait_recv()
+        for e in range(NZ):
+            v = rb[k, y, e].astype(F32) + yin[k, 0, e].astype(F32) + yin[k, 1, e].astype(F32)
+            v = v.astype(BF16)
+            sb[k, e, 0] = v[:40]
+            sb[k, e, 1] = v[40:]
+
     inner_rows(dp, 0)
-    go(remote(rb.at[far, lo], yhold.at[0], ys.at[0], yr.at[0], at_y(1)))
+    go(hold(0, 1))
     inner_rows(dp, 1)
-    go(remote(rb.at[far, hi], yhold.at[1], ys.at[1], yr.at[1], at_y(-1)))
-    inner_rows(1 - dp, 1)
-    go(remote(rb.at[up, hi], yin.at[0, hi], ys.at[2], yr.at[2], at_y(1)))
-    inner_rows(1 - dp, 0)
-    go(remote(rb.at[down, lo], yin.at[1, lo], ys.at[3], yr.at[3], at_y(-1)))
+    go(hold(0, -1))
     mixing()
     send_mix()
+    inner_rows(1 - dp, 1)
+    go(plain(0, 1))
+    inner_rows(1 - dp, 0)
+    go(plain(0, -1))
+    go(hold(1, 1))
+    go(hold(1, -1))
     stepping()
+    ring_on(0)
+    go(plain(1, 1))
+    go(plain(1, -1))
 
     ds = ds_r[...]
     pick = head_pick(c).astype(BF16)
@@ -481,58 +536,48 @@
         origin = lax.rem(j8 + 8 - off, 8)
         remote(gmt.at[origin], mixin.at[off], ms.at[off], mr.at[off], at_j(origin)).wait_recv()
         total = total + mixin[off].astype(F32)
-    place_mix = one_hot(iota((32, 128), 1) == iota((32, 128), 0) + 64).astype(BF16)
     place_step = one_hot(
         (iota((128, 128), 1) == iota((128, 128), 0) + 96) & (iota((128, 128), 0) < HEADS)
     ).astype(BF16)
-    last = t_mm(total.astype(BF16), place_mix) + mm(ds, place_step)
+    last = mixed(total).astype(F32) + mm(ds, place_step)
     last = last + jnp.concatenate([gi[:, 256:].astype(F32), jnp.zeros((EXT, 64), F32)], axis=1)
     last = last.astype(BF16)
     for b in range(4):
-        r = (t_mm(xe[:, b * 640 : (b + 1) * 640], last) * norm).astype(BF16)
+        r = (mm(xet[b * 640 : (b + 1) * 640, :], last) * norm).astype(BF16)
         for g in range(8):
             ra[(b % 2) * 4 + g // 2, (g % 2) * 2 + b // 2] = r[g * ROWS : (g + 1) * ROWS]
 
-    def z_first(src, n, r3, r4, r1, s, r):
+    def z_first(src, n, r3, r4, r1, s, r, o=0):
         h = n // 2
         for k, sign in enumerate((1, -1)):
             part = pl.ds(k * h, h)
             dst = [lax.rem(z + sign * d + NZ, NZ) for d in range(5)]
-            go(remote(src.at[dst[4], part], r4.at[k], s.at[4 * k], r.at[4 * k], at_z(2 * sign)))
-            go(remote(src.at[dst[3]], r3.at[k], s.at[4 * k + 1], r.at[4 * k + 1], at_z(sign)))
-            go(remote(src.at[dst[1]], r1.at[k], s.at[4 * k + 2], r.at[4 * k + 2], at_z(sign)))
-
-    def z_second(src, n, r3, r4, r2, s, r):
+            go(remote(src.at[dst[4], part], r4.at[k], s.at[o + 4 * k], r.at[o + 4 * k], at_z(2 * sign)))
+            go(remote(src.at[dst[3]], r3.at[k], s.at[o + 4 * k + 1], r.at[o + 4 * k + 1], at_z(sign)))
+            go(remote(src.at[dst[1]], r1.at[k], s.at[o + 4 * k + 2], r.at[o + 4 * k + 2], at_z(sign)))
+
+    def z_second(src, n, r3, r4, r2, s, r, o=0):
         h = n // 2
         for k, sign in enumerate((1, -1)):
             part = pl.ds(k * h, h)
             t = lax.rem(z + 2 * sign + NZ, NZ)
-            remote(r3.at[k], r3.at[k], s.at[4 * k + 1], r.at[4 * k + 1], at_z(sign)).wait_recv()
-            remote(r4.at[k], r4.at[k], s.at[4 * k], r.at[4 * k], at_z(2 * sign)).wait_recv()
+            remote(r3.at[k], r3.at[k], s.at[o + 4 * k + 1], r.at[o + 4 * k + 1], at_z(sign)).wait_recv()
+            remote(r4.at[k], r4.at[k], s.at[o + 4 * k], r.at[o + 4 * k], at_z(2 * sign)).wait_recv()
             for i in range(n):
                 v = src[t, i].astype(F32) + r3[k, i].astype(F32)
                 if k * h <= i < (k + 1) * h:
                     v = v + r4[k, i - k * h].astype(F32)
                 r3[k, i] = v.astype(BF16)
-            go(remote(r3.at[k], r2.at[k], s.at[4 * k + 3], r.at[4 * k + 3], at_z(2 * sign)))
-
-    def z_last(r1, r2, s, r):
+            go(remote(r3.at[k], r2.at[k], s.at[o + 4 * k + 3], r.at[o + 4 * k + 3], at_z(2 * sign)))
+
+    def z_last(r1, r2, s, r, o=0):
         for k, sign in enumerate((1, -1)):
-            remote(r1.at[k], r1.at[k], s.at[4 * k + 2], r.at[4 * k + 2], at_z(sign)).wait_recv()
-            remote(r2.at[k], r2.at[k], s.at[4 * k + 3], r.at[4 * k + 3], at_z(2 * sign)).wait_recv()
+            remote(r1.at[k], r1.at[k], s.at[o + 4 * k + 2], r.at[o + 4 * k + 2], at_z(sign)).wait_recv()
+            remote(r2.at[k], r2.at[k], s.at[o + 4 * k + 3], r.at[o + 4 * k + 3], at_z(2 * sign)).wait_recv()
 
     z_first(ra, 4, a3, a4, a1, zs, zr)
 
-    remote(yhold.at[0], yhold.at[0], ys.at[0], yr.at[0], at_y(1)).wait_recv()
-    for i in range(4):
-        yhold[0, i] = (rb[up, i].astype(F32) + yhold[0, i].astype(F32)).astype(BF16)
-    go(remote(yhold.at[0], yin.at[0, lo], ys.at[4], yr.at[4], at_y(1)))
-    remote(yhold.at[1], yhold.at[1], ys.at[1], yr.at[1], at_y(-1)).wait_recv()
-    for i in range(4):
-        yhold[1, i] = (rb[down, 4 + i].astype(F32) + yhold[1, i].astype(F32)).astype(BF16)
-    go(remote(yhold.at[1], yin.at[1, hi], ys.at[5], yr.at[5], at_y(-1)))
-
-    z_second(ra, 4, a3, a4, a2, zs, zr)
+    ring_on(1)
 
     remote(psib, psib, dsem.at[0], drem.at[0], {"seq_2": sib}).wait_recv()
     for k in range(4):
@@ -554,16 +599,12 @@
         pbsib[...] = (pb[...].astype(F32) + pbsib[...].astype(F32)).astype(BF16)
         edge.start()
 
-    for k in (2, 4):
-        part = hi if k == 2 else lo
-        remote(yin.at[0, part], yin.at[0, part], ys.at[k], yr.at[k], at_y(1)).wait_recv()
-    for k in (3, 5):
-        part = lo if k == 3 else hi
-        remote(yin.at[1, part], yin.at[1, part], ys.at[k], yr.at[k], at_y(-1)).wait_recv()
-    for i in range(NZ):
-        v = rb[y, i].astype(F32) + yin[0, i].astype(F32) + yin[1, i].astype(F32)
-        sb[i] = v.astype(BF16)
-    z_first(sb, 2, b3, b4, b1, qs, qr)
+    ring_end(0)
+    z_first(sb.at[0], 2, b3.at[0], b4.at[0], b1.at[0], qs, qr)
+    z_second(ra, 4, a3, a4, a2, zs, zr)
+    ring_end(1)
+    z_first(sb.at[1], 2, b3.at[1], b4.at[1], b1.at[1], qs, qr, 8)
+    z_second(sb.at[0], 2, b3.at[0], b4.at[0], b2.at[0], qs, qr)
 
     z_last(a1, a2, zs, zr)
     for i in range(4):
@@ -582,7 +623,7 @@
     xhold[1] = (psib[xd, 1].astype(F32) + xhold[1].astype(F32)).astype(BF16)
     go(remote(xhold.at[1], xin.at[1, 1], xs.at[5], xr.at[5], at_x(-1)))
 
-    z_second(sb, 2, b3, b4, b2, qs, qr)
+    z_second(sb.at[1], 2, b3.at[1], b4.at[1], b2.at[1], qs, qr, 8)
 
     v = sa[y].astype(F32)
     for off in range(1, 4):
@@ -618,13 +659,13 @@
             v = v + pbin[k].astype(F32)
         ig[16:, :] = v.astype(BF16)
 
-    z_last(b1, b2, qs, qr)
-    for i in range(2):
-        v = sb[z, i].astype(F32)
-        for k in range(2):
-            v = v + b1[k, i].astype(F32) + b2[k, i].astype(F32)
-        fbs[0, :, i * 128 : (i + 1) * 128] = v[:40]
-        fbs[1, :, i * 128 : (i + 1) * 128] = v[40:]
+    for t in range(2):
+        z_last(b1.at[t], b2.at[t], qs, qr, 8 * t)
+        for i in range(2):
+            v = sb[t, z, i].astype(F32)
+            for k in range(2):
+                v = v + b1[t, k, i].astype(F32) + b2[t, k, i].astype(F32)
+            fbs[i, :, t * 128 : (t + 1) * 128] = v
     go(remote(fbs.at[sib], fb.at[c], dsem.at[2], drem.at[2], {"seq_2": sib}))
     fb[c] = fbs[c]
 
@@ -650,7 +691,7 @@
     norm,
     piece, og, wi_h, wm_h, ws_h, ci_h, cm_h, bias_h, dlog_h, skip_h,
     mt, fat, fb, ig,
-    xe, ogx, wi, wm, ws, ci, cm, bias, dlog, skip, wih, send, recv, back, st, gi, gm, ds, gmt,
+    xe, ogx, wi, wm, ws, ci, cm, bias, dlog, skip, wih, send, recv, back, st, gi, gm, ds, gmt, xet,
     gs, gr, gt, hsem, lsem, s1, r1, s2, r2, *rest,
 ):
     dp = lax.axis_index("dp")
@@ -705,10 +746,13 @@
     begin()
     local = local_phase(acts, dlog, skip)
     turn()
+    for b in range(4):
+        cols = slice(b * 640, (b + 1) * 640)
+        xet[cols, :] = xe[:, cols].T
     end()
     later = carried_phase(acts, local, st, ci, cm, gi, gm, ds, gmt)
     sums_phase(
-        norm, later, xe, gi, gm, ds, gmt, wih, wm, ws, mt, fat, fb, ig, *rest
+        norm, later, xet, gi, gm, ds, gmt, wih, wm, ws, mt, fat, fb, ig, *rest
     )
 
 
@@ -733,21 +777,22 @@
             vm(EXT, D), vm(2, TOK // 2, 2 * INNER), vm(D, 2 * INNER), vm(D, 2 * STATE), vm(10, D),
             pltpu.VMEM((4, 2 * INNER), F32), pltpu.VMEM((4, 2 * STATE), F32),
             pltpu.VMEM((1, 10), F32), pltpu.VMEM((1, 10), F32), pltpu.VMEM((1, 10), F32),
-            vm(D, INNER), vm(n, CHUNK, STATE), vm(n, CHUNK, STATE), vm(n, CHUNK, STATE),
-            vm(n, CHUNK, STATE), vm(EXT, INNER), vm(EXT, 2 * STATE), vm(EXT, 128), vm(8, 32, EXT),
+            vm(D, INNER), vm(n, CHUNK, STATE), vm(n, CHUNK, STATE), vm(n, 8 * HEADS, STATE),
+            vm(n, 8 * HEADS, STATE), vm(EXT, INNER), vm(EXT, 2 * STATE), vm(EXT, 128), vm(8, 32, TOK),
+            vm(D, EXT),
             dma((13,)), dma((13,)), dma((4,)), dma((10,)), dma((2,)),
             dma((n,)), dma((n,)), dma((n,)), dma((n,)),
-            vm(2, 2, 16, D), vm(4, PRE, D), vm(8, 32, EXT),
-            vm(4, NZ, 2, ROWS, 128), vm(2, 4, 2, ROWS, 128), vm(2, NZ, 2, ROWS, 128),
+            vm(2, 2, 16, D), vm(4, PRE, D), vm(8, 32, TOK),
+            vm(2, 4, NZ, ROWS, 128), vm(2, 2, 4, ROWS, 128), vm(2, 2, NZ, ROWS, 128),
             vm(NZ, 4, ROWS, 128), vm(2, 4, ROWS, 128), vm(2, 2, ROWS, 128),
             vm(2, 4, ROWS, 128), vm(2, 4, ROWS, 128), vm(4, ROWS, 128), vm(4, ROWS, 128),
-            vm(NZ, 2, ROWS, 128), vm(2, 2, ROWS, 128), vm(2, 1, ROWS, 128),
-            vm(2, 2, ROWS, 128), vm(2, 2, ROWS, 128),
+            vm(2, NZ, 2, 40, 128), vm(2, 2, 2, 40, 128), vm(2, 2, 1, 40, 128),
+            vm(2, 2, 2, 40, 128), vm(2, 2, 2, 40, 128),
             pltpu.VMEM((2, 40, 128), F32), pltpu.VMEM((8, 16, 128), F32),
             pltpu.VMEM((2, 40, 256), F32),
             vm(2, 4, 2, 16, D), vm(4, 2, 16, D), vm(2, 16, D), vm(PRE, D), vm(PRE, D),
-            dma((8,)), dma((8,)), dma((6,)), dma((6,)), dma((8,)), dma((8,)),
-            dma((8,)), dma((8,)), dma((6,)), dma((6,)), dma(()), dma((4,)), dma((4,)), dma((4,)),
+            dma((8,)), dma((8,)), dma((12,)), dma((12,)), dma((8,)), dma((8,)),
+            dma((16,)), dma((16,)), dma((6,)), dma((6,)), dma(()), dma((4,)), dma((4,)), dma((4,)),
             dma((8,)), dma((8,)), dma((3,)), dma((3,)),
         ],
         compiler_params=pltpu.CompilerParams(

time: 75.8 us -> 75.8 us (level)
  no operation moved by 1% of the time
where the time goes in v6:
time: 75.8 us; the launch traced here: 75.7 us
  Pallas kernels  75 us (99%)
    pallas_call x1, Pallas kernels, whole(): pl.pallas_call(functools.partial(whole_kernel, norm), out_shape=(jax.Shap...  73.2 us
    pallas_call x1, Pallas kernels, finish(): pl.pallas_call(finish_kernel, out_shape=(jax.ShapeDtypeStruct((32, D), BF...  1.82 us

profile of v6, /device:TPU:1, one launch (start us, length us, event | category | flops | bytes accessed | tf_op | source)
XLA Modules:
  0.0 75.7 jit_solution(1608549281546471658)
XLA Ops:
  0.6 73.2 %whole.1 = (f32[8,16,128]{2,1,0:T(8,128)}, f32[2,40,128]{2,1,0:T(8,128)}, f32[2,40,256]{2,1,0:T(8,128)}, bf16[32,2560]{1,0:T(8,128)(2,1)}) custom-call(bf16[32,2560]{1,0:T(8,128)(2,1)} %bitcast.8, bf16[128,640]{1,0:T(8,128)(2,1)} %bitcast.9, bf16[2560,640]{1,0:T(8,128)(2,1)} %wi_h.1, bf16[2560,256]{1,0:T(8,128)(2,1)} %wm_h.1, bf16[10,2560]{1,0:T(8,128)(2,1)} %bitcast.10, ...), custom_call_target="tpu_custom_call" | custom-call | tf_op jit(solution)/shard_map/whole/pallas_call | solution.py:766
  73.9 1.8 %finish.1 = (bf16[32,2560]{1,0:T(8,128)(2,1)}, f32[40,640]{1,0:T(8,128)}, f32[10,256]{1,0:T(8,128)}, f32[10,40]{1,0:T(8,128)}) custom-call(f32[8,16,128]{2,1,0:T(8,128)} %get-tuple-element.12.mt, f32[2,40,128]{2,1,0:T(8,128)} %get-tuple-element.13.fat, f32[2,40,256]{2,1,0:T(8,128)} %get-tuple-element.14.fb, bf16[32,2560]{1,0:T(8,128)(2,1)} %get-tuple-element.15.ig), custom_call_target="tpu_custom_call" | custom-call | tf_op jit(solution)/shard_map/finish/pallas_call | solution.py:821

commit v7 on v6

--- a/solution.py
+++ b/solution.py
@@ -355,9 +355,13 @@
 
     h0, ge = collect(0), collect(1)
     h0b, geb = h0.astype(BF16), ge.astype(BF16)
-    ug = etail * mm_t(bm, geb)
-    u = u_loc + ug
-    gi_o[...] = back((dte * u + skp * dy) * gate_i, half_of(ci[...], c))
+    kept = []
+
+    def inner():
+        ug = etail * mm_t(bm, geb)
+        u = u_loc + ug
+        gi_o[...] = back((dte * u + skp * dy) * gate_i, half_of(ci[...], c))
+        kept.extend((u, ug))
 
     def mixing():
         gm = jnp.concatenate([d_in + mm(xt, geb), d_out + mm(yt, h0b)], axis=1) * gate_m
@@ -376,6 +380,7 @@
         return back(t_mm(total.astype(BF16), place), exact(cm[...], cols))
 
     def stepping():
+        u, ug = kept
         y = y_loc + ecum * mm_t(cmx, h0b)
         ddt = exact(xa * u, hs)
         dcum = exact(dy * y - xdtf * u, hs)
@@ -387,7 +392,7 @@
         dsr = (ddt - rate * da) * jax.nn.sigmoid(srb)
         ds_o[...] = jnp.concatenate([jnp.zeros((PRE, 128), F32), dsr], axis=0).astype(BF16)
 
-    return mixing, mixed, stepping
+    return inner, mixing, mixed, stepping
 
 
 def sums_phase(
@@ -435,7 +440,10 @@
             to = lax.rem(j8 + off, 8)
             go(remote(gmt.at[to], mixin.at[off], ms.at[off], mr.at[off], at_j(to)))
 
-    mixing, mixed, stepping = later
+    inner, mixing, mixed, stepping = later
+    mixing()
+    send_mix()
+    inner()
 
     gi = gi_r[...]
     rhs = gi[:, :256]
@@ -498,8 +506,6 @@
     go(hold(0, 1))
     inner_rows(dp, 1)
     go(hold(0, -1))
-    mixing()
-    send_mix()
     inner_rows(1 - dp, 1)
     go(plain(0, 1))
     inner_rows(1 - dp, 0)
@@ -507,29 +513,7 @@
     go(hold(1, 1))
     go(hold(1, -1))
     stepping()
-    ring_on(0)
-    go(plain(1, 1))
-    go(plain(1, -1))
-
     ds = ds_r[...]
-    pick = head_pick(c).astype(BF16)
-    ds10 = mm_t(ds, pick).astype(BF16)
-    gm = gm_r[...]
-    for b in range(4):
-        rows = slice(b * 640, (b + 1) * 640)
-        part = mm_t(gi, wih[rows]) + mm_t(gm, wm[rows]) + mm(ds10, ws[:, rows])
-        part = part.astype(BF16)
-        pb[:, rows] = part[:PRE]
-        for j in range(8):
-            for k in range(2):
-                at = PRE + j * 32 + k * 16
-                p[j // 4, j % 4, k, :, rows] = part[at : at + 16]
-    go(remote(p.at[sib], psib, dsem.at[0], drem.at[0], {"seq_2": sib}))
-    pb_out = remote(pb, pbsib, dsem.at[1], drem.at[1], {"seq_2": sib})
-
-    @pl.when(c == 0)
-    def _():
-        pb_out.start()
 
     total = gmt[j8].astype(F32)
     for off in range(1, 8):
@@ -577,6 +561,29 @@
 
     z_first(ra, 4, a3, a4, a1, zs, zr)
 
+    ring_on(0)
+    go(plain(1, 1))
+    go(plain(1, -1))
+
+    pick = head_pick(c).astype(BF16)
+    ds10 = mm_t(ds, pick).astype(BF16)
+    gm = gm_r[...]
+    for b in range(4):
+        rows = slice(b * 640, (b + 1) * 640)
+        part = mm_t(gi, wih[rows]) + mm_t(gm, wm[rows]) + mm(ds10, ws[:, rows])
+        part = part.astype(BF16)
+        pb[:, rows] = part[:PRE]
+        for j in range(8):
+            for k in range(2):
+                at = PRE + j * 32 + k * 16
+                p[j // 4, j % 4, k, :, rows] = part[at : at + 16]
+    go(remote(p.at[sib], psib, dsem.at[0], drem.at[0], {"seq_2": sib}))
+    pb_out = remote(pb, pbsib, dsem.at[1], drem.at[1], {"seq_2": sib})
+
+    @pl.when(c == 0)
+    def _():
+        pb_out.start()
+
     ring_on(1)
 
     remote(psib, psib, dsem.at[0], drem.at[0], {"seq_2": sib}).wait_recv()
@@ -599,9 +606,9 @@
         pbsib[...] = (pb[...].astype(F32) + pbsib[...].astype(F32)).astype(BF16)
         edge.start()
 
+    z_second(ra, 4, a3, a4, a2, zs, zr)
     ring_end(0)
     z_first(sb.at[0], 2, b3.at[0], b4.at[0], b1.at[0], qs, qr)
-    z_second(ra, 4, a3, a4, a2, zs, zr)
     ring_end(1)
     z_first(sb.at[1], 2, b3.at[1], b4.at[1], b1.at[1], qs, qr, 8)
     z_second(sb.at[0], 2, b3.at[0], b4.at[0], b2.at[0], qs, qr)

time: 75.8 us -> 72.5 us (0.956)
  Pallas kernels: 75 us -> 71.8 us
    pallas_call x1, Pallas kernels: 73.2 us -> 69.9 us  [whole(): pl.pallas_call(functools.partial(whole_kernel, norm), out_shape=(jax.Shap...]
where the time goes in v7:
time: 72.5 us; the launch traced here: 72.4 us
  Pallas kernels  71.8 us (99%)
    pallas_call x1, Pallas kernels, whole(): pl.pallas_call(functools.partial(whole_kernel, norm), out_shape=(jax.Shap...  69.9 us
    pallas_call x1, Pallas kernels, finish(): pl.pallas_call(finish_kernel, out_shape=(jax.ShapeDtypeStruct((32, D), BF...  1.82 us

profile of v7, /device:TPU:1, one launch (start us, length us, event | category | flops | bytes accessed | tf_op | source)
XLA Modules:
  0.0 72.4 jit_solution(10736455735857703235)
XLA Ops:
  0.6 69.9 %whole.1 = (f32[8,16,128]{2,1,0:T(8,128)}, f32[2,40,128]{2,1,0:T(8,128)}, f32[2,40,256]{2,1,0:T(8,128)}, bf16[32,2560]{1,0:T(8,128)(2,1)}) custom-call(bf16[32,2560]{1,0:T(8,128)(2,1)} %bitcast.8, bf16[128,640]{1,0:T(8,128)(2,1)} %bitcast.9, bf16[2560,640]{1,0:T(8,128)(2,1)} %wi_h.1, bf16[2560,256]{1,0:T(8,128)(2,1)} %wm_h.1, bf16[10,2560]{1,0:T(8,128)(2,1)} %bitcast.10, ...), custom_call_target="tpu_custom_call" | custom-call | tf_op jit(solution)/shard_map/whole/pallas_call | solution.py:773
  70.6 1.8 %finish.1 = (bf16[32,2560]{1,0:T(8,128)(2,1)}, f32[40,640]{1,0:T(8,128)}, f32[10,256]{1,0:T(8,128)}, f32[10,40]{1,0:T(8,128)}) custom-call(f32[8,16,128]{2,1,0:T(8,128)} %get-tuple-element.12.mt, f32[2,40,128]{2,1,0:T(8,128)} %get-tuple-element.13.fat, f32[2,40,256]{2,1,0:T(8,128)} %get-tuple-element.14.fb, bf16[32,2560]{1,0:T(8,128)(2,1)} %get-tuple-element.15.ig), custom_call_target="tpu_custom_call" | custom-call | tf_op jit(solution)/shard_map/finish/pallas_call | solution.py:828

commit v8 on v7

--- a/solution.py
+++ b/solution.py
@@ -586,6 +586,8 @@
 
     ring_on(1)
 
+    z_second(ra, 4, a3, a4, a2, zs, zr)
+
     remote(psib, psib, dsem.at[0], drem.at[0], {"seq_2": sib}).wait_recv()
     for k in range(4):
         for h in range(2):
@@ -606,7 +608,6 @@
         pbsib[...] = (pb[...].astype(F32) + pbsib[...].astype(F32)).astype(BF16)
         edge.start()
 
-    z_second(ra, 4, a3, a4, a2, zs, zr)
     ring_end(0)
     z_first(sb.at[0], 2, b3.at[0], b4.at[0], b1.at[0], qs, qr)
     ring_end(1)

time: 72.5 us -> 72.5 us (level)
  no operation moved by 1% of the time
where the time goes in v8:
time: 72.5 us; the launch traced here: 72.4 us
  Pallas kernels  71.7 us (99%)
    pallas_call x1, Pallas kernels, whole(): pl.pallas_call(functools.partial(whole_kernel, norm), out_shape=(jax.Shap...  69.9 us
    pallas_call x1, Pallas kernels, finish(): pl.pallas_call(finish_kernel, out_shape=(jax.ShapeDtypeStruct((32, D), BF...  1.82 us

profile of v8, /device:TPU:1, one launch (start us, length us, event | category | flops | bytes accessed | tf_op | source)
XLA Modules:
  0.0 72.4 jit_solution(6339915255820501365)
XLA Ops:
  0.6 69.9 %whole.1 = (f32[8,16,128]{2,1,0:T(8,128)}, f32[2,40,128]{2,1,0:T(8,128)}, f32[2,40,256]{2,1,0:T(8,128)}, bf16[32,2560]{1,0:T(8,128)(2,1)}) custom-call(bf16[32,2560]{1,0:T(8,128)(2,1)} %bitcast.8, bf16[128,640]{1,0:T(8,128)(2,1)} %bitcast.9, bf16[2560,640]{1,0:T(8,128)(2,1)} %wi_h.1, bf16[2560,256]{1,0:T(8,128)(2,1)} %wm_h.1, bf16[10,2560]{1,0:T(8,128)(2,1)} %bitcast.10, ...), custom_call_target="tpu_custom_call" | custom-call | tf_op jit(solution)/shard_map/whole/pallas_call | solution.py:774
  70.5 1.8 %finish.1 = (bf16[32,2560]{1,0:T(8,128)(2,1)}, f32[40,640]{1,0:T(8,128)}, f32[10,256]{1,0:T(8,128)}, f32[10,40]{1,0:T(8,128)}) custom-call(f32[8,16,128]{2,1,0:T(8,128)} %get-tuple-element.12.mt, f32[2,40,128]{2,1,0:T(8,128)} %get-tuple-element.13.fat, f32[2,40,256]{2,1,0:T(8,128)} %get-tuple-element.14.fb, bf16[32,2560]{1,0:T(8,128)(2,1)} %get-tuple-element.15.ig), custom_call_target="tpu_custom_call" | custom-call | tf_op jit(solution)/shard_map/finish/pallas_call | solution.py:829
